TPU v7x, 16 devices: a whole 2x2x2 slice. The times are simulated.
16 devices in a mesh: model: 2 (over z), data: 2 (over y), stage: 4 (over x, core).
Axes of the slice: x: 2, y: 2, z: 2, core: 2. Of those that a mesh axis runs over, the one named last changes fastest.
Arguments:
- w_up: float32 [4, 768, 3072], P('stage', None, 'model')
- w_down: float32 [4, 3072, 768], P('stage', 'model')
- m_up: float32 [4, 768, 3072], P('stage', None, 'model')
- m_down: float32 [4, 3072, 768], P('stage', 'model')
- v_up: float32 [4, 768, 3072], P('stage', None, 'model')
- v_down: float32 [4, 3072, 768], P('stage', 'model')
- g_up: float32 [2, 4, 768, 3072], P('data', 'stage', None, 'model')
- g_down: float32 [2, 4, 3072, 768], P('data', 'stage', 'model')
- acts_last: bfloat16 [4, 1024, 768], P('stage', 'data')
- grad_out: bfloat16 [1024, 768], P('data')
- x_next: bfloat16 [3, 1024, 768], P(None, 'data')
- learn_rate: float32 [1], replicated
- max_norm: float32 [1], replicated
Outputs:
- output 1: float32 [4, 768, 3072], P('stage', None, 'model')
- output 2: float32 [4, 3072, 768], P('stage', 'model')
- output 3: float32 [4, 768, 3072], P('stage', None, 'model')
- output 4: float32 [4, 3072, 768], P('stage', 'model')
- output 5: float32 [4, 768, 3072], P('stage', None, 'model')
- output 6: float32 [4, 3072, 768], P('stage', 'model')
- output 7: bfloat16 [3, 1024, 768], P(None, 'data')
All inputs are finite; a program needn't handle non-finite values.
Results may differ from a plain program's by a relative error of at most 0.00893322.
Values are sent between devices in bfloat16 or wider.
A program may use at most 1 GiB of HBM per device.

v0:
```python
import jax
import jax.numpy as jnp
from jax import lax
from jax.sharding import PartitionSpec as P

ADAM_STEP = 10
BETA_ONE = 0.9
BETA_TWO = 0.95
ADAM_EPS = 1e-8
WEIGHT_DECAY = 0.1
NORM_EPS = 1e-6
CONTRACT_LAST = (((1,), (1,)), ((), ()))
CONTRACT_FIRST = (((0,), (0,)), ((), ()))


def gelu_vjp(pre_act, upstream):
    pull_back = jax.vjp(jax.nn.gelu, pre_act)[1]
    return pull_back(upstream)[0]


def adamw_update(weight, moment_one, moment_two, grad_step, step_rate):
    mom_new = BETA_ONE * moment_one + (1.0 - BETA_ONE) * grad_step
    sec_new = BETA_TWO * moment_two + (1.0 - BETA_TWO) * grad_step * grad_step
    one_corr = 1.0 - BETA_ONE ** ADAM_STEP
    two_corr = 1.0 - BETA_TWO ** ADAM_STEP
    direction = (mom_new / one_corr) / (jnp.sqrt(sec_new / two_corr) + ADAM_EPS)
    weight_new = weight - step_rate * (direction + WEIGHT_DECAY * weight)
    return weight_new, mom_new, sec_new


def solution(mesh):
    n_stage = mesh.shape['stage']
    n_data = mesh.shape['data']
    down_perm = [(sender, sender - 1) for sender in range(1, n_stage)]
    up_perm = [(sender, sender + 1) for sender in range(n_stage - 1)]
    up_spec = P('stage', None, 'model')
    down_spec = P('stage', 'model', None)
    row_spec = P(None, 'data', None)
    in_specs = (up_spec, down_spec, up_spec, down_spec, up_spec, down_spec, P('data', 'stage', None, 'model'), P('data', 'stage', 'model', None), P('stage', 'data', None), P('data', None), row_spec, P(None), P(None))
    out_specs = (up_spec, down_spec, up_spec, down_spec, up_spec, down_spec, row_spec)

    def device_step(w_up, w_down, m_up, m_down, v_up, v_down, g_up, g_down, acts_last, grad_out, x_next, learn_rate, max_norm):
        stage_id = lax.axis_index('stage')
        acts_in = acts_last[0]
        up_bf = w_up[0].astype(jnp.bfloat16)
        down_bf = w_down[0].astype(jnp.bfloat16)
        row_count, d_model = acts_in.shape
        ff_local = up_bf.shape[1]
        n_micro = x_next.shape[0]

        def back_core(upstream):
            pre_act = jnp.dot(acts_in, up_bf, preferred_element_type=jnp.float32)
            hidden = jax.nn.gelu(pre_act).astype(jnp.bfloat16)
            grad_hid = lax.dot_general(upstream, down_bf, CONTRACT_LAST, preferred_element_type=jnp.float32)
            grad_pre = gelu_vjp(pre_act, grad_hid).astype(jnp.bfloat16)
            return hidden, grad_pre

        def back_send(state_in):
            hidden, grad_pre = back_core(state_in[0])
            part_sum = lax.dot_general(grad_pre, up_bf, CONTRACT_LAST, preferred_element_type=jnp.float32)
            return hidden, grad_pre, state_in[0], part_sum

        def hold_send(state_in):
            return state_in[1], state_in[2], state_in[3], jnp.zeros((row_count, d_model), jnp.float32)

        def back_keep(state_in):
            hidden, grad_pre = back_core(state_in[0])
            return hidden, grad_pre, state_in[0]

        def hold_keep(state_in):
            return state_in[1], state_in[2], state_in[3]

        upstream = grad_out
        keep_hid = jnp.zeros((row_count, ff_local), jnp.bfloat16)
        keep_pre = jnp.zeros((row_count, ff_local), jnp.bfloat16)
        keep_up = grad_out
        for step_idx in range(n_stage - 1):
            active = stage_id == n_stage - 1 - step_idx
            keep_hid, keep_pre, keep_up, part_sum = lax.cond(active, back_send, hold_send, (upstream, keep_hid, keep_pre, keep_up))
            summed = lax.psum(part_sum, 'model')
            grad_in = (upstream.astype(jnp.float32) + summed).astype(jnp.bfloat16)
            upstream = lax.ppermute(grad_in, 'stage', down_perm)
        keep_hid, keep_pre, keep_up = lax.cond(stage_id == 0, back_keep, hold_keep, (upstream, keep_hid, keep_pre, keep_up))

        grad_down = lax.dot_general(keep_hid, keep_up, CONTRACT_FIRST, preferred_element_type=jnp.float32)
        grad_up = lax.dot_general(acts_in, keep_pre, CONTRACT_FIRST, preferred_element_type=jnp.float32)
        mean_up = lax.psum(g_up[0, 0] + grad_up, 'data') / n_data
        mean_down = lax.psum(g_down[0, 0] + grad_down, 'data') / n_data
        local_sq = lax.psum(jnp.sum(mean_up * mean_up) + jnp.sum(mean_down * mean_down), 'model')
        norm_acc = local_sq
        for step_idx in range(n_stage - 1):
            incoming = lax.ppermute(norm_acc, 'stage', down_perm)
            norm_acc = jnp.where(stage_id == n_stage - 2 - step_idx, local_sq + incoming, norm_acc)
        clip_cur = jnp.minimum(1.0, max_norm[0] / (jnp.sqrt(norm_acc) + NORM_EPS))
        step_rate = learn_rate[0]

        def apply_update(state_in):
            clip_now = state_in[1]
            up_w, up_m, up_v = adamw_update(w_up[0], m_up[0], v_up[0], clip_now * mean_up, step_rate)
            down_w, down_m, down_v = adamw_update(w_down[0], m_down[0], v_down[0], clip_now * mean_down, step_rate)
            return (up_w, down_w, up_m, down_m, up_v, down_v, up_w.astype(jnp.bfloat16), down_w.astype(jnp.bfloat16))

        def keep_state(state_in):
            return state_in[0]

        def fwd_local(state_in):
            acts_cur, up_new_bf, down_new_bf = state_in
            pre_act = jnp.dot(acts_cur, up_new_bf, preferred_element_type=jnp.float32)
            hidden = jax.nn.gelu(pre_act).astype(jnp.bfloat16)
            return jnp.dot(hidden, down_new_bf, preferred_element_type=jnp.float32)

        def fwd_idle(state_in):
            return jnp.zeros((row_count, d_model), jnp.float32)

        opt_state = (w_up[0], w_down[0], m_up[0], m_down[0], v_up[0], v_down[0], up_bf, down_bf)
        acts_cur = x_next[0]
        finished = []
        for step_idx in range(n_micro + n_stage - 1):
            if step_idx < n_stage:
                opt_state = lax.cond(stage_id == step_idx, apply_update, keep_state, (opt_state, clip_cur))
            if 0 < step_idx < n_micro:
                acts_cur = jnp.where(stage_id == 0, x_next[step_idx], acts_cur)
            micro_idx = step_idx - stage_id
            is_busy = (micro_idx >= 0) & (micro_idx < n_micro)
            branch = lax.cond(is_busy, fwd_local, fwd_idle, (acts_cur, opt_state[6], opt_state[7]))
            summed = lax.psum(branch, 'model')
            acts_out = (acts_cur.astype(jnp.float32) + summed).astype(jnp.bfloat16)
            if step_idx >= n_stage - 1:
                finished.append(acts_out)
            if step_idx < n_micro + n_stage - 2:
                acts_cur = lax.ppermute(acts_out, 'stage', up_perm)
            if step_idx < n_stage - 1:
                clip_cur = lax.ppermute(clip_cur, 'stage', up_perm)
        y_local = jnp.stack(finished)
        y_next = lax.psum(jnp.where(stage_id == n_stage - 1, y_local, jnp.zeros_like(y_local)), 'stage')
        return (opt_state[0][None], opt_state[1][None], opt_state[2][None], opt_state[3][None], opt_state[4][None], opt_state[5][None], y_next)

    return jax.shard_map(device_step, mesh=mesh, in_specs=in_specs, out_specs=out_specs, check_vma=False)
```

profile of v0, /device:TPU:1, one launch (start us, length us, event | category | flops | bytes accessed | tf_op | source)
XLA Modules:
  0.0 1090.0 jit_solution(3607466575625627497)
XLA Ops:
  15.8 59.9 %all-reduce.13.cloned.1.call-done = f32[512,768]{1,0:T(8,128)} async-done(((f32[512,768]{1,0:T(8,128)}), f32[512,768]{1,0:T(8,128)}) %all-reduce.13.cloned.1.call-update) | async-done | bytes 1572880 | tf_op jit(solution)/shard_map/psum | solution.py:80
  81.0 10.7 collective-permute-done
  93.0 58.1 %all-reduce.15.cloned.1.call-done = f32[512,768]{1,0:T(8,128)} async-done(((f32[512,768]{1,0:T(8,128)}), f32[512,768]{1,0:T(8,128)}) %all-reduce.15.cloned.1.call-update) | async-done | bytes 1572880 | tf_op jit(solution)/shard_map/psum | solution.py:80
  156.4 10.7 collective-permute-done.1
  167.1 13.9 %conditional.16 = (bf16[512,1536]{1,0:T(8,128)(2,1)S(1)}, bf16[512,1536]{1,0:T(8,128)(2,1)}, bf16[512,768]{1,0:T(8,128)(2,1)S(1)}, f32[512,768]{1,0:T(8,128)}) conditional(s32[]{:T(128)} %convert_element_type.162, (bf16[512,1536]{1,0:T(8,128)(2,1)S(1)}, bf16[512,1536]{1,0:T(8,128)(2,1)}, bf16[512,768]{1,0:T(8,128)(2,1)S(1)}) %tuple.120, ...), branch_computations={%region_6.0_spmd, %region_7.0_spmd} | conditional | flops 3641180160 | bytes 25952316 | solution.py:79
  181.1 45.9 %all-reduce.17.cloned.1.call-done = f32[512,768]{1,0:T(8,128)} async-done(((f32[512,768]{1,0:T(8,128)}), f32[512,768]{1,0:T(8,128)}) %all-reduce.17.cloned.1.call-update) | async-done | bytes 1572880 | tf_op jit(solution)/shard_map/psum | solution.py:80
  243.0 6.6 bitcast_add_fusion.9
  255.2 218.4 %all-reduce.33.cloned.1.call-done = (f32[768,1536]{0,1:T(8,128)}, f32[1536,768]{1,0:T(8,128)}) async-done(((f32[768,1536]{0,1:T(8,128)}, f32[1536,768]{1,0:T(8,128)}), (f32[768,1536]{0,1:T(8,128)}, f32[1536,768]{1,0:T(8,128)})) %all-reduce.33.cloned.1.call-update) | async-done | bytes 9437200 | tf_op jit(solution)/shard_map/psum | solution.py:87
  510.1 20.0 %conditional.18 = (f32[768,1536]{1,0:T(8,128)}, f32[1536,768]{1,0:T(8,128)}, f32[768,1536]{1,0:T(8,128)}, f32[1536,768]{1,0:T(8,128)}, f32[768,1536]{1,0:T(8,128...) conditional(s32[]{:T(128)} %convert_element_type.163, ...), branch_computations={%region_16.17_spmd, %region_17.18_spmd} | conditional | flops 40108032 | bytes 136839440 | solution.py:120
  531.4 60.6 %all-reduce.19.cloned.1.call-done = f32[512,768]{1,0:T(8,128)} async-done(((f32[512,768]{1,0:T(8,128)}), f32[512,768]{1,0:T(8,128)}) %all-reduce.19.cloned.1.call-update) | async-done | bytes 1572880 | tf_op jit(solution)/shard_map/psum | solution.py:126
  597.8 8.9 collective-permute-start.6
  606.7 32.4 %conditional.19 = ((f32[768,1536]{1,0:T(8,128)}, f32[1536,768]{1,0:T(8,128)}, f32[768,1536]{1,0:T(8,128)}, f32[1536,768]{1,0:T(8,128)}, f32[768,1536]{1,0:T(8,12...) conditional(s32[]{:T(128)} %convert_element_type.162, ...), branch_computations={%region_18.19_spmd, %region_19.20_spmd} | conditional | flops 40108032 | bytes 136839456 | solution.py:120
  613.0 16.0 %fusion.148 = (bf16[768,1536]{1,0:T(8,128)(2,1)}, f32[768,1536]{1,0:T(8,128)}, f32[768,1536]{1,0:T(8,128)}, f32[768,1536]{1,0:T(8,128)}) fusion(f32[]{:T(128)} %get-tuple-element.304, f32[1,768,1536]{2,1,0:T(8,128)} %get-tuple-element.303, f32[768,1536]{1,0:T(8,128)} %copy.22, f32[]{:T(128)} %get-tuple-element.306, f32[1,768,1536]{2,1,0:T(8,128)} %get-tuple-element.305, ...), kind=kLoop, calls=%fused_computation.210 | loop fusion | flops 20054016 | bytes 35389448 | tf_op jit(solution)/shard_map/cond/branch_1_fun/convert_element_type | solution.py:101
  630.7 8.4 fusion.146
  646.7 45.9 %all-reduce.21.cloned.1.call-done = f32[512,768]{1,0:T(8,128)} async-done(((f32[512,768]{1,0:T(8,128)}), f32[512,768]{1,0:T(8,128)}) %all-reduce.21.cloned.1.call-update) | async-done | bytes 1572880 | tf_op jit(solution)/shard_map/psum | solution.py:126
  700.9 7.0 collective-permute-done.7
  716.0 80.3 %all-reduce.23.cloned.1.call-done = f32[512,768]{1,0:T(8,128)} async-done(((f32[512,768]{1,0:T(8,128)}), f32[512,768]{1,0:T(8,128)}) %all-reduce.23.cloned.1.call-update) | async-done | bytes 1572880 | tf_op jit(solution)/shard_map/psum | solution.py:126
  804.6 7.0 collective-permute-done.8
  818.2 72.3 %all-reduce.25.cloned.1.call-done = f32[512,768]{1,0:T(8,128)} async-done(((f32[512,768]{1,0:T(8,128)}), f32[512,768]{1,0:T(8,128)}) %all-reduce.25.cloned.1.call-update) | async-done | bytes 1572880 | tf_op jit(solution)/shard_map/psum | solution.py:126
  895.9 8.9 collective-permute-done.12
  906.2 53.4 %all-reduce.27.cloned.1.call-done = f32[512,768]{1,0:T(8,128)} async-done(((f32[512,768]{1,0:T(8,128)}), f32[512,768]{1,0:T(8,128)}) %all-reduce.27.cloned.1.call-update) | async-done | bytes 1572880 | tf_op jit(solution)/shard_map/psum | solution.py:126
  965.3 8.9 collective-permute-done.13
  976.6 48.1 %all-reduce.29.cloned.1.call-done = f32[512,768]{1,0:T(8,128)} async-done(((f32[512,768]{1,0:T(8,128)}), f32[512,768]{1,0:T(8,128)}) %all-reduce.29.cloned.1.call-update) | async-done | bytes 1572880 | tf_op jit(solution)/shard_map/psum | solution.py:126
  1028.2 51.8 %all-reduce.31.cloned.1.call-done = bf16[3,512,768]{2,1,0:T(8,128)(2,1)} async-done(((bf16[3,512,768]{2,1,0:T(8,128)(2,1)}), bf16[3,512,768]{2,1,0:T(8,128)(2,1)}) %all-reduce.31.cloned.1.call-update) | async-done | bytes 2359312 | tf_op jit(solution)/shard_map/psum | solution.py:135
  (175 shorter events, 200.3 us)
Async XLA Ops:
  7.2 68.6 %all-reduce.13.cloned.1.call-start = ((), (), s32[]{:S(2)}) async-start(), calls=%async_computation | async-start | bytes 3145728 | tf_op jit(solution)/shard_map/psum | solution.py:80
  15.8 135.3 %all-reduce.15.cloned.1.call-start = ((), (), s32[]{:S(2)}) async-start(), calls=%async_computation.1 | async-start | bytes 3145728 | tf_op jit(solution)/shard_map/psum | solution.py:80
  78.2 13.6 %collective-permute-start = (bf16[512,768]{1,0:T(8,128)(2,1)}, bf16[512,768]{1,0:T(8,128)(2,1)S(1)}, u32[]{:S(2)}, u32[]{:S(2)}) collective-permute-start(bf16[512,768]{1,0:T(8,128)(2,1)} %add_convert_fusion.8), channel_id=1, source_target_pairs={{1,0},{2,1},{3,2},{5,4},{6,5},{7,6},{9,8},{10,9},{11,10},{13,12},{... | collective-permute-start | bytes 2359304 | tf_op jit(solution)/shard_map/ppermute | solution.py:82
  93.0 134.0 %all-reduce.17.cloned.1.call-start = ((), (), s32[]{:S(2)}) async-start(), calls=%async_computation.2 | async-start | bytes 3145728 | tf_op jit(solution)/shard_map/psum | solution.py:80
  153.5 13.6 %collective-permute-start.1 = (bf16[512,768]{1,0:T(8,128)(2,1)}, bf16[512,768]{1,0:T(8,128)(2,1)S(1)}, u32[]{:S(2)}, u32[]{:S(2)}) collective-permute-start(bf16[512,768]{1,0:T(8,128)(2,1)} %add_convert_fusion.7), channel_id=1, source_target_pairs={{1,0},{2,1},{3,2},{5,4},{6,5},{7,6},{9,8},{10,9},{11,10},{13,12},{... | collective-permute-start | bytes 2359304 | tf_op jit(solution)/shard_map/ppermute | solution.py:82
  181.0 292.6 %all-reduce.33.cloned.1.call-start = ((), (), s32[]{:S(2)}) async-start(), calls=%async_computation.10 | async-start | bytes 18874368 | tf_op jit(solution)/shard_map/psum | solution.py:87
  229.4 13.6 %collective-permute-start.2 = (bf16[512,768]{1,0:T(8,128)(2,1)}, bf16[512,768]{1,0:T(8,128)(2,1)}, u32[]{:S(2)}, u32[]{:S(2)}) collective-permute-start(bf16[512,768]{1,0:T(8,128)(2,1)} %add_convert_fusion.6), channel_id=1, source_target_pairs={{1,0},{2,1},{3,2},{5,4},{6,5},{7,6},{9,8},{10,9},{11,10},{13,12},{... | collective-permute-start | bytes 2359304 | tf_op jit(solution)/shard_map/ppermute | solution.py:82
  253.3 338.8 %all-reduce.19.cloned.1.call-start = ((), (), s32[]{:S(2)}) async-start(), calls=%async_computation.3 | async-start | bytes 3145728 | tf_op jit(solution)/shard_map/psum | solution.py:126
  489.6 6.3 collective-permute-start.3
  497.7 4.9 collective-permute-start.4
  531.4 161.2 %all-reduce.21.cloned.1.call-start = ((), (), s32[]{:S(2)}) async-start(), calls=%async_computation.4 | async-start | bytes 3145728 | tf_op jit(solution)/shard_map/psum | solution.py:126
  593.8 45.2 %collective-permute-start.9 = (bf16[512,768]{1,0:T(8,128)(2,1)S(1)}, bf16[512,768]{1,0:T(8,128)(2,1)S(1)}, u32[]{:S(2)}, u32[]{:S(2)}) collective-permute-start(bf16[512,768]{1,0:T(8,128)(2,1)S(1)} %add_convert_fusion.5), channel_id=1, source_target_pairs={{0,1},{1,2},{2,3},{4,5},{5,6},{6,7},{8,9},{9,10},{10,11},{12,13},{... | collective-permute-start | bytes 2359304 | tf_op jit(solution)/shard_map/ppermute | solution.py:131
  597.8 8.9 collective-permute-start.6
  646.6 149.7 %all-reduce.23.cloned.1.call-start = ((), (), s32[]{:S(2)}) async-start(), calls=%async_computation.5 | async-start | bytes 3145728 | tf_op jit(solution)/shard_map/psum | solution.py:126
  695.1 13.3 %collective-permute-start.10 = (bf16[512,768]{1,0:T(8,128)(2,1)}, bf16[512,768]{1,0:T(8,128)(2,1)S(1)}, u32[]{:S(2)}, u32[]{:S(2)}) collective-permute-start(bf16[512,768]{1,0:T(8,128)(2,1)} %add_convert_fusion.4), channel_id=1, source_target_pairs={{0,1},{1,2},{2,3},{4,5},{5,6},{6,7},{8,9},{9,10},{10,11},{12,13},{... | collective-permute-start | bytes 2359304 | tf_op jit(solution)/shard_map/ppermute | solution.py:131
  699.0 8.9 collective-permute-start.7
  715.9 174.5 %all-reduce.25.cloned.1.call-start = ((), (), s32[]{:S(2)}) async-start(), calls=%async_computation.6 | async-start | bytes 3145728 | tf_op jit(solution)/shard_map/psum | solution.py:126
  798.8 13.0 %collective-permute-start.11 = (bf16[512,768]{1,0:T(8,128)(2,1)}, bf16[512,768]{1,0:T(8,128)(2,1)S(1)}, u32[]{:S(2)}, u32[]{:S(2)}) collective-permute-start(bf16[512,768]{1,0:T(8,128)(2,1)} %add_convert_fusion.3), channel_id=1, source_target_pairs={{0,1},{1,2},{2,3},{4,5},{5,6},{6,7},{8,9},{9,10},{10,11},{12,13},{... | collective-permute-start | bytes 2359304 | tf_op jit(solution)/shard_map/ppermute | solution.py:131
  802.7 8.9 collective-permute-start.8
  818.1 141.5 %all-reduce.27.cloned.1.call-start = ((), (), s32[]{:S(2)}) async-start(), calls=%async_computation.7 | async-start | bytes 3145728 | tf_op jit(solution)/shard_map/psum | solution.py:126
  892.0 12.8 %collective-permute-start.12 = (bf16[512,768]{1,0:T(8,128)(2,1)S(1)}, bf16[512,768]{1,0:T(8,128)(2,1)}, u32[]{:S(2)}, u32[]{:S(2)}) collective-permute-start(bf16[512,768]{1,0:T(8,128)(2,1)S(1)} %add_convert_fusion.2), channel_id=1, source_target_pairs={{0,1},{1,2},{2,3},{4,5},{5,6},{6,7},{8,9},{9,10},{10,11},{12,13},{... | collective-permute-start | bytes 2359304 | tf_op jit(solution)/shard_map/ppermute | solution.py:131
  906.1 118.6 %all-reduce.29.cloned.1.call-start = ((), (), s32[]{:S(2)}) async-start(), calls=%async_computation.8 | async-start | bytes 3145728 | tf_op jit(solution)/shard_map/psum | solution.py:126
  961.3 12.8 %collective-permute-start.13 = (bf16[512,768]{1,0:T(8,128)(2,1)S(1)}, bf16[512,768]{1,0:T(8,128)(2,1)S(1)}, u32[]{:S(2)}, u32[]{:S(2)}) collective-permute-start(bf16[512,768]{1,0:T(8,128)(2,1)S(1)} %add_convert_fusion.1), channel_id=1, source_target_pairs={{0,1},{1,2},{2,3},{4,5},{5,6},{6,7},{8,9},{9,10},{10,11},{12,13},{... | collective-permute-start | bytes 2359304 | tf_op jit(solution)/shard_map/ppermute | solution.py:131
  976.5 103.5 %all-reduce.31.cloned.1.call-start = ((), (), s32[]{:S(2)}) async-start(), calls=%async_computation.9 | async-start | bytes 4718592 | tf_op jit(solution)/shard_map/psum | solution.py:135
  (35 other events, 233.0 us)
Sparse Core Ops, SparseCore 0:
  15.9 59.7 all-reduce.12
  93.1 57.9 all-reduce.14
  181.1 45.7 all-reduce.16
  253.4 220.1 all-reduce.32
  531.5 60.5 all-reduce.18
  646.8 45.8 all-reduce.20
  716.1 80.2 all-reduce.22
  818.2 72.1 all-reduce.24
  906.2 53.2 all-reduce.26
  976.6 48.0 all-reduce.28
  1028.3 51.6 all-reduce.30
where the time goes:
time: 1100 us; the launch traced here: 1090 us
  waiting for transfers between devices  859 us (78%)
  other arithmetic  63.9 us (6%)
  starting transfers between devices  50.8 us (5%)
  local copies, waits for them, and re-layouts  50.1 us (5%)
  matrix products  39.5 us (4%)
  between operations  20.8 us (2%)
    psum x6, waiting for transfers between devices, device_step(): summed = lax.psum(branch, 'model')  361 us
    psum x1, waiting for transfers between devices, device_step(): mean_up = lax.psum(g_up[0, 0] + grad_up, 'data') / n_data  218 us
    psum x3, waiting for transfers between devices, device_step(): summed = lax.psum(part_sum, 'model')  164 us
    psum x1, waiting for transfers between devices, device_step(): lax.psum(jnp.where(stage_id == n_stage - 1, y_local, jnp.zeros_like(y_loc...  51.8 us
    ppermute x3, waiting for transfers between devices, device_step(): upstream = lax.ppermute(grad_in, 'stage', down_perm)  25.9 us
  transfers between devices with their start and end apart: 25, of which 21 were waited for; matrix products, arithmetic and copies ran while one was open for 3% of the time, Pallas kernels for 0%

commit v1 on v0

v1 whole, which is shorter than its diff:
```python
import functools

import jax
import jax.numpy as jnp
from jax import lax
from jax.experimental import pallas as pl
from jax.experimental.pallas import tpu as pltpu
from jax.sharding import PartitionSpec as P

ADAM_STEP = 10
BETA_ONE = 0.9
BETA_TWO = 0.95
ADAM_EPS = 1e-8
WEIGHT_DECAY = 0.1
NORM_EPS = 1e-6
ONE_CORR = 1.0 - BETA_ONE ** ADAM_STEP
TWO_CORR = 1.0 - BETA_TWO ** ADAM_STEP
GELU_SCALE = (2.0 / 3.141592653589793) ** 0.5
GELU_CUBE = 0.044715
NN = (((1,), (0,)), ((), ()))
NT = (((1,), (1,)), ((), ()))
TN = (((0,), (0,)), ((), ()))
F32 = jnp.float32
BF16 = jnp.bfloat16
MESH = pl.DeviceIdType.MESH
BACK_ROWS = 128
FWD_ROWS = 128
VMEM_LIMIT = 66_000_000


def mm(lhs, rhs, dims):
    return lax.dot_general(lhs, rhs, dims, preferred_element_type=F32)


def gelu_val(pre):
    return pre * (0.5 * (1.0 + jnp.tanh(GELU_SCALE * (pre + GELU_CUBE * (pre * pre * pre)))))


def gelu_both(pre):
    sq = pre * pre
    tan = jnp.tanh(GELU_SCALE * (pre + GELU_CUBE * (sq * pre)))
    cdf = 0.5 * (1.0 + tan)
    slope = cdf + 0.5 * pre * (1.0 - tan * tan) * (GELU_SCALE * (1.0 + (3.0 * GELU_CUBE) * sq))
    return pre * cdf, slope


def adamw_update(weight, moment_one, moment_two, grad_step, step_rate):
    mom_new = BETA_ONE * moment_one + (1.0 - BETA_ONE) * grad_step
    sec_new = BETA_TWO * moment_two + (1.0 - BETA_TWO) * grad_step * grad_step
    direction = (mom_new / ONE_CORR) / (jnp.sqrt(sec_new / TWO_CORR) + ADAM_EPS)
    weight_new = weight - step_rate * (direction + WEIGHT_DECAY * weight)
    return weight_new, mom_new, sec_new


def clip_of(norm_tile, max_norm):
    total = jnp.sum(jnp.sum(norm_tile, axis=0, keepdims=True), axis=1, keepdims=True)
    return jnp.minimum(1.0, max_norm / (jnp.sqrt(total) + NORM_EPS))


def whole_barrier(n_model, n_data, n_stage):
    barrier = pltpu.get_barrier_semaphore()
    me = (lax.axis_index('model'), lax.axis_index('data'), lax.axis_index('stage'))
    for dm in range(n_model):
        for dd in range(n_data):
            for ds in range(n_stage):
                if dm or dd or ds:
                    peer = (lax.rem(me[0] + dm, n_model), lax.rem(me[1] + dd, n_data), lax.rem(me[2] + ds, n_stage))
                    pl.semaphore_signal(barrier, inc=1, device_id=peer, device_id_type=MESH)
    pl.semaphore_wait(barrier, n_model * n_data * n_stage - 1)


def remote(src, dst, send_sem, recv_sem, device):
    return pltpu.make_async_remote_copy(src_ref=src, dst_ref=dst, send_sem=send_sem, recv_sem=recv_sem, device_id=device, device_id_type=MESH)


def bwd_kernel(dims, wu_hbm, wd_hbm, acts_hbm, dy_hbm, gu_hbm, gd_hbm,
               gbu_hbm, gbd_hbm, norm_out,
               wu32, wd32, wu_bf, wd_bf, aa, gg, hh, dzz, slope, slope_o, dz_own, h_own,
               gu_own, gd_own, gu_rcv, gd_rcv, part, part_rcv, fin, norm_buf,
               ld_sem, ysend, yrecv, psend, precv, fsend, frecv, nsend, nrecv, st_sem):
    n_model, n_data, n_stage = dims
    z, d, p = lax.axis_index('model'), lax.axis_index('data'), lax.axis_index('stage')
    zo, do = 1 - z, 1 - d
    ypeer, zpeer = (z, do, p), (zo, d, p)
    last = n_stage - 1
    rows = aa.shape[0] // 2
    width = aa.shape[1]
    half = hh.shape[1]
    rb = BACK_ROWS
    hb = rb // 2
    nb = rows // rb
    own_ff = pl.ds(pl.multiple_of(d * half, 128), half)
    oth_ff = pl.ds(pl.multiple_of(do * half, 128), half)
    mine, theirs = pl.ds(0, rows), pl.ds(rows, rows)

    loads = [
        pltpu.make_async_copy(wu_hbm, wu32, ld_sem.at[0]),
        pltpu.make_async_copy(acts_hbm, aa.at[mine], ld_sem.at[2]),
        pltpu.make_async_copy(wd_hbm, wd32, ld_sem.at[1]),
        pltpu.make_async_copy(gu_hbm.at[:, own_ff], gu_own, ld_sem.at[4]),
        pltpu.make_async_copy(gd_hbm.at[own_ff, :], gd_own, ld_sem.at[5]),
    ]
    for copy in loads:
        copy.start()
    dy_load = pltpu.make_async_copy(dy_hbm, gg.at[mine], ld_sem.at[3])

    @pl.when(p == last)
    def _():
        dy_load.start()

    whole_barrier(n_model, n_data, n_stage)
    send_acts = remote(acts_hbm, aa.at[theirs], ysend.at[0], yrecv.at[0], ypeer)
    send_gu = remote(gu_hbm.at[:, oth_ff], gu_rcv, ysend.at[1], yrecv.at[1], ypeer)
    send_gd = remote(gd_hbm.at[oth_ff, :], gd_rcv, ysend.at[2], yrecv.at[2], ypeer)
    send_g = remote(gg.at[mine], gg.at[theirs], ysend.at[3], yrecv.at[3], ypeer)
    send_acts.start()
    send_gu.start()

    loads[0].wait()
    loads[1].wait()

    def cast_up(i, carry):
        at = pl.ds(pl.multiple_of(i * 128, 128), 128)
        wu_bf[at, :] = wu32[at, :].astype(BF16)
        return carry
    lax.fori_loop(0, width // 128, cast_up, 0)

    def own_pre(i, carry):
        at = pl.ds(pl.multiple_of(i * rb, rb), rb)
        val, slp = gelu_both(mm(aa[at, :], wu_bf[...], NN))
        h_own[at, :] = val.astype(BF16)
        slope[at, :] = slp
        return carry
    lax.fori_loop(0, nb, own_pre, 0)
    loads[2].wait()

    def cast_down(i, carry):
        at = pl.ds(pl.multiple_of(i * 128, 128), 128)
        wd_bf[at, :] = wd32[at, :].astype(BF16)
        return carry
    lax.fori_loop(0, 2 * half // 128, cast_down, 0)

    @pl.when(p == last)
    def _():
        dy_load.wait()

    def g_at(c, zi):
        return gg.at[pl.ds(pl.multiple_of(c * rb + zi * hb, hb), hb)]

    def part_copy(c):
        return remote(part.at[c, pl.ds(pl.multiple_of(zo * hb, hb), hb)], part_rcv.at[c], psend.at[c], precv.at[c], zpeer)

    def fin_copy(c, zi):
        return remote(fin.at[c], g_at(c, z), fsend.at[c, zi], frecv.at[c, z], (zi, d, lax.max(p - 1, 0)))

    def compute(c):
        @pl.when(p < last)
        def _():
            for zi in range(n_model):
                pltpu.make_async_copy(fin.at[c], g_at(c, zi), frecv.at[c, zi]).wait()
        at = pl.ds(pl.multiple_of(c * rb, rb), rb)
        grad_hid = mm(gg[at, :], wd_bf[...], NT)
        dz_own[at, :] = (slope[at, :] * grad_hid).astype(BF16)

        @pl.when(p > 0)
        def _():
            part[c] = mm(dz_own[at, :], wu_bf[...], NT)
            part_copy(c).start()

    def finalize(c):
        part_copy(c).wait_recv()
        at = pl.ds(pl.multiple_of(c * rb + z * hb, hb), hb)
        total = part[c, pl.ds(pl.multiple_of(z * hb, hb), hb), :] + part_rcv[c]
        fin[c] = (gg[at, :].astype(F32) + total).astype(BF16)
        for zi in range(n_model):
            fin_copy(c, zi).start()

    lag = jnp.where(p == last, 1, 0)

    def chain(i, carry):
        @pl.when(i < nb)
        def _():
            compute(i)
        f = i - lag

        @pl.when((f >= 0) & (f < nb) & (p > 0))
        def _():
            finalize(f)
        return carry
    lax.fori_loop(0, nb + 1, chain, 0)

    send_g.start()
    send_gd.start()

    hh[mine, :] = h_own[:, own_ff]
    dzz[mine, :] = dz_own[:, own_ff]
    send_acts.wait_recv()

    def oth_pre(i, carry):
        at = pl.ds(pl.multiple_of(rows + i * rb, rb), rb)
        val, slp = gelu_both(mm(aa[at, :], wu_bf[:, own_ff], NN))
        hh[at, :] = val.astype(BF16)
        slope_o[pl.ds(pl.multiple_of(i * rb, rb), rb), :] = slp
        return carry
    lax.fori_loop(0, nb, oth_pre, 0)
    send_g.wait_recv()

    def oth_dz(i, carry):
        at = pl.ds(pl.multiple_of(rows + i * rb, rb), rb)
        grad_hid = mm(gg[at, :], wd_bf[own_ff, :], NT)
        dzz[at, :] = (slope_o[pl.ds(pl.multiple_of(i * rb, rb), rb), :] * grad_hid).astype(BF16)
        return carry
    lax.fori_loop(0, nb, oth_dz, 0)
    loads[3].wait()
    loads[4].wait()

    def weight_grads(j, carry):
        at = pl.ds(pl.multiple_of(j * 128, 128), 128)
        gd_own[at, :] += mm(hh[:, at], gg[...], TN)
        gu_own[at, :] += mm(aa[:, at], dzz[...], TN)
        return carry
    lax.fori_loop(0, half // 128, weight_grads, 0)

    def combine(own, rcv):
        def body(i, acc):
            at = pl.ds(pl.multiple_of(i * 32, 32), 32)
            mean = (own[at, :] + rcv[at, :]) * 0.5
            own[at, :] = mean
            return acc + jnp.sum((mean * mean).reshape(4, 8, mean.shape[1]), axis=0)
        return body
    acc = jnp.zeros((8, half), F32)
    send_gu.wait_recv()
    acc = lax.fori_loop(0, gu_own.shape[0] // 32, combine(gu_own, gu_rcv), acc)
    store_u = pltpu.make_async_copy(gu_own, gbu_hbm, st_sem.at[0])
    store_u.start()
    send_gd.wait_recv()
    acc = lax.fori_loop(0, gd_own.shape[0] // 32, combine(gd_own, gd_rcv), acc)
    store_d = pltpu.make_async_copy(gd_own, gbd_hbm, st_sem.at[1])
    store_d.start()
    tile = acc[:, 0:128]
    for k in range(1, half // 128):
        tile = tile + acc[:, k * 128:(k + 1) * 128]
    n_all = n_model * n_data * n_stage
    my_id = (z * n_data + d) * n_stage + p
    norm_buf[my_id] = tile

    def norm_copy(k):
        peer = lax.rem(my_id + k, n_all)
        device = (peer // (n_data * n_stage), lax.rem(peer // n_stage, n_data), lax.rem(peer, n_stage))
        return remote(norm_buf.at[my_id], norm_buf.at[my_id], nsend.at[k], nrecv.at[my_id], device)
    for k in range(1, n_all):
        norm_copy(k).start()
    for k in range(1, n_all):
        peer = lax.rem(my_id + k, n_all)
        pltpu.make_async_copy(norm_buf.at[peer], norm_buf.at[peer], nrecv.at[peer]).wait()
    total = norm_buf[0]
    for k in range(1, n_all):
        total = total + norm_buf[k]
    norm_out[...] = total

    for k in range(1, n_all):
        norm_copy(k).wait_send()
    for copy in (send_acts, send_gu, send_gd, send_g):
        copy.wait_send()

    @pl.when(p > 0)
    def _():
        for c in range(nb):
            part_copy(c).wait_send()
            for zi in range(n_model):
                fin_copy(c, zi).wait_send()
    store_u.wait()
    store_d.wait()


def fwd_kernel(dims, norm_ref, lr_ref, mn_ref, wu_hbm, wd_hbm, mu_hbm, md_hbm, vu_hbm, vd_hbm, gbu_hbm, gbd_hbm, x_hbm,
               gu_full, gd_full, y_hbm,
               wu32, wd32, mu32, md32, vu32, vd32, gu32, gd32, wu_bf, wd_bf, a_buf, y_buf, part, part_rcv, fin,
               ld_sem, ysend, yrecv, psend, precv, fsend, frecv, agsend, agrecv, outsend, outrecv, st_sem):
    n_model, n_data, n_stage = dims
    z, d, p = lax.axis_index('model'), lax.axis_index('data'), lax.axis_index('stage')
    zo, do = 1 - z, 1 - d
    ypeer, zpeer = (z, do, p), (zo, d, p)
    last = n_stage - 1
    half = wu32.shape[1]
    nc, rb, width = a_buf.shape
    hb = rb // 2
    own_ff = pl.ds(pl.multiple_of(d * half, 128), half)

    loads = [
        pltpu.make_async_copy(gbu_hbm, gu32, ld_sem.at[0]),
        pltpu.make_async_copy(wu_hbm.at[:, own_ff], wu32, ld_sem.at[1]),
        pltpu.make_async_copy(mu_hbm.at[:, own_ff], mu32, ld_sem.at[2]),
        pltpu.make_async_copy(vu_hbm.at[:, own_ff], vu32, ld_sem.at[3]),
        pltpu.make_async_copy(gbd_hbm, gd32, ld_sem.at[4]),
        pltpu.make_async_copy(wd_hbm.at[own_ff, :], wd32, ld_sem.at[5]),
        pltpu.make_async_copy(md_hbm.at[own_ff, :], md32, ld_sem.at[6]),
        pltpu.make_async_copy(vd_hbm.at[own_ff, :], vd32, ld_sem.at[7]),
    ]
    for copy in loads:
        copy.start()
    x_load = pltpu.make_async_copy(x_hbm, a_buf, ld_sem.at[8])

    @pl.when(p == 0)
    def _():
        x_load.start()
    whole_barrier(n_model, n_data, n_stage)

    clip = clip_of(norm_ref[...], mn_ref[0])
    rate = lr_ref[0]
    for copy in loads[:4]:
        copy.wait()

    def update_up(i, carry):
        at = pl.ds(pl.multiple_of(i * 32, 32), 32)
        new = adamw_update(wu32[at, :], mu32[at, :], vu32[at, :], clip * gu32[at, :], rate)[0]
        wu_bf[at, own_ff] = new.astype(BF16)
        return carry
    lax.fori_loop(0, width // 32, update_up, 0)
    send_wu = remote(wu_bf.at[:, own_ff], wu_bf.at[:, own_ff], ysend.at[0], yrecv.at[0], ypeer)
    send_wd = remote(wd_bf.at[own_ff, :], wd_bf.at[own_ff, :], ysend.at[1], yrecv.at[1], ypeer)
    send_gu = remote(gu32, gu_full.at[:, own_ff], ysend.at[2], yrecv.at[2], ypeer)
    send_gd = remote(gd32, gd_full.at[own_ff, :], ysend.at[3], yrecv.at[3], ypeer)
    for copy in loads[4:]:
        copy.wait()
    send_wu.start()

    def update_down(i, carry):
        at = pl.ds(pl.multiple_of(i * 32, 32), 32)
        new = adamw_update(wd32[at, :], md32[at, :], vd32[at, :], clip * gd32[at, :], rate)[0]
        wd_bf[pl.ds(pl.multiple_of(d * half + i * 32, 32), 32), :] = new.astype(BF16)
        return carry
    lax.fori_loop(0, half // 32, update_down, 0)
    store_u = pltpu.make_async_copy(gu32, gu_full.at[:, own_ff], st_sem.at[0])
    store_d = pltpu.make_async_copy(gd32, gd_full.at[own_ff, :], st_sem.at[1])
    store_u.start()
    store_d.start()
    send_wd.start()
    send_gu.start()
    send_gd.start()

    @pl.when(p == 0)
    def _():
        x_load.wait()
    send_wu.wait_recv()
    send_wd.wait_recv()

    def half_rows(zi):
        return pl.ds(pl.multiple_of(zi * hb, hb), hb)

    def part_copy(c):
        return remote(part.at[c, half_rows(zo)], part_rcv.at[c], psend.at[c], precv.at[c], zpeer)

    def fin_copy(c, zi):
        return remote(fin.at[c], a_buf.at[c, half_rows(z)], fsend.at[c, zi], frecv.at[c, z], (zi, d, lax.min(p + 1, last)))

    def gather_copy(c):
        return remote(fin.at[c], y_buf.at[c, half_rows(z)], agsend.at[c], agrecv.at[c], zpeer)

    def out_copy(c, q):
        return remote(y_buf.at[c], y_hbm.at[c], outsend.at[c, q], outrecv.at[c], (z, d, q))

    def out_local(c):
        return pltpu.make_async_copy(y_buf.at[c], y_hbm.at[c], outsend.at[c, last])

    def compute(c):
        @pl.when(p > 0)
        def _():
            for zi in range(n_model):
                pltpu.make_async_copy(fin.at[c], a_buf.at[c, half_rows(zi)], frecv.at[c, zi]).wait()
        hid = gelu_val(mm(a_buf[c], wu_bf[...], NN)).astype(BF16)
        part[c] = mm(hid, wd_bf[...], NN)
        part_copy(c).start()

    def finalize(c):
        part_copy(c).wait_recv()
        total = part[c, half_rows(z), :] + part_rcv[c]
        new = (a_buf[c, half_rows(z), :].astype(F32) + total).astype(BF16)
        fin[c] = new

        @pl.when(p < last)
        def _():
            for zi in range(n_model):
                fin_copy(c, zi).start()

        @pl.when(p == last)
        def _():
            y_buf[c, half_rows(z), :] = new
            gather_copy(c).start()

    def publish(c):
        gather_copy(c).wait_recv()
        out_local(c).start()
        for q in range(last):
            out_copy(c, q).start()

    lag = jnp.where(p == 0, 1, 0)

    def chain(i, carry):
        @pl.when(i < nc)
        def _():
            compute(i)
        f = i - lag

        @pl.when((f >= 0) & (f < nc))
        def _():
            finalize(f)

        @pl.when((i >= 1) & (p == last))
        def _():
            publish(i - 1)
        return carry
    lax.fori_loop(0, nc + 1, chain, 0)

    def drain(c, carry):
        part_copy(c).wait_send()

        @pl.when(p < last)
        def _():
            for zi in range(n_model):
                fin_copy(c, zi).wait_send()
            pltpu.make_async_copy(y_buf.at[c], y_hbm.at[c], outrecv.at[c]).wait()

        @pl.when(p == last)
        def _():
            gather_copy(c).wait_send()
            out_local(c).wait()
            for q in range(last):
                out_copy(c, q).wait_send()
        return carry
    lax.fori_loop(0, nc, drain, 0)
    send_wu.wait_send()
    send_wd.wait_send()
    store_u.wait()
    store_d.wait()
    send_gu.wait()
    send_gd.wait()


def solution(mesh):
    n_model, n_data, n_stage = (mesh.shape[k] for k in ('model', 'data', 'stage'))
    dims = (n_model, n_data, n_stage)
    n_all = n_model * n_data * n_stage
    up_spec = P('stage', None, 'model')
    down_spec = P('stage', 'model', None)
    row_spec = P(None, 'data', None)
    in_specs = (up_spec, down_spec, up_spec, down_spec, up_spec, down_spec, P('data', 'stage', None, 'model'), P('data', 'stage', 'model', None), P('stage', 'data', None), P('data', None), row_spec, P(None), P(None))
    out_specs = (up_spec, down_spec, up_spec, down_spec, up_spec, down_spec, row_spec)
    any_spec = pl.BlockSpec(memory_space=pl.ANY)
    vmem_spec = pl.BlockSpec(memory_space=pltpu.VMEM)
    smem_spec = pl.BlockSpec(memory_space=pltpu.SMEM)
    dma = pltpu.SemaphoreType.DMA

    def device_step(w_up, w_down, m_up, m_down, v_up, v_down, g_up, g_down, acts_last, grad_out, x_next, learn_rate, max_norm):
        rows, width = grad_out.shape
        ff = w_up.shape[2]
        half = ff // 2
        nb = rows // BACK_ROWS
        hb = BACK_ROWS // 2
        sds = jax.ShapeDtypeStruct
        gbar_u, gbar_d, norm_tile = pl.pallas_call(
            functools.partial(bwd_kernel, dims),
            out_shape=(sds((width, half), F32), sds((half, width), F32), sds((8, 128), F32)),
            in_specs=[any_spec] * 6,
            out_specs=(any_spec, any_spec, vmem_spec),
            scratch_shapes=[
                pltpu.VMEM((width, ff), F32), pltpu.VMEM((ff, width), F32),
                pltpu.VMEM((width, ff), BF16), pltpu.VMEM((ff, width), BF16),
                pltpu.VMEM((2 * rows, width), BF16), pltpu.VMEM((2 * rows, width), BF16),
                pltpu.VMEM((2 * rows, half), BF16), pltpu.VMEM((2 * rows, half), BF16),
                pltpu.VMEM((rows, ff), F32), pltpu.VMEM((rows, half), F32),
                pltpu.VMEM((rows, ff), BF16), pltpu.VMEM((rows, ff), BF16),
                pltpu.VMEM((width, half), F32), pltpu.VMEM((half, width), F32),
                pltpu.VMEM((width, half), F32), pltpu.VMEM((half, width), F32),
                pltpu.VMEM((nb, BACK_ROWS, width), F32), pltpu.VMEM((nb, hb, width), F32),
                pltpu.VMEM((nb, hb, width), BF16), pltpu.VMEM((n_all, 8, 128), F32),
                dma((6,)), dma((4,)), dma((4,)), dma((nb,)), dma((nb,)), dma((nb, 2)), dma((nb, 2)),
                dma((n_all,)), dma((n_all,)), dma((2,)),
            ],
            compiler_params=pltpu.CompilerParams(collective_id=0, has_side_effects=True, vmem_limit_bytes=VMEM_LIMIT),
            name='backward',
        )(w_up[0], w_down[0], acts_last[0], grad_out, g_up[0, 0], g_down[0, 0])

        n_micro = x_next.shape[0]
        nc = n_micro * rows // FWD_ROWS
        fb = FWD_ROWS // 2
        gu_full, gd_full, y_next = pl.pallas_call(
            functools.partial(fwd_kernel, dims),
            out_shape=(sds((width, ff), F32), sds((ff, width), F32), sds((nc, FWD_ROWS, width), BF16)),
            in_specs=[vmem_spec, smem_spec, smem_spec] + [any_spec] * 9,
            out_specs=(any_spec, any_spec, any_spec),
            scratch_shapes=[pltpu.VMEM((width, half), F32), pltpu.VMEM((half, width), F32)] * 4 + [
                pltpu.VMEM((width, ff), BF16), pltpu.VMEM((ff, width), BF16),
                pltpu.VMEM((nc, FWD_ROWS, width), BF16), pltpu.VMEM((nc, FWD_ROWS, width), BF16),
                pltpu.VMEM((nc, FWD_ROWS, width), F32), pltpu.VMEM((nc, fb, width), F32),
                pltpu.VMEM((nc, fb, width), BF16),
                dma((9,)), dma((4,)), dma((4,)), dma((nc,)), dma((nc,)), dma((nc, 2)), dma((nc, 2)),
                dma((nc,)), dma((nc,)), dma((nc, n_stage)), dma((nc,)), dma((2,)),
            ],
            compiler_params=pltpu.CompilerParams(collective_id=1, has_side_effects=True, vmem_limit_bytes=VMEM_LIMIT),
            name='forward',
        )(norm_tile, learn_rate, max_norm, w_up[0], w_down[0], m_up[0], m_down[0], v_up[0], v_down[0], gbar_u, gbar_d, x_next.reshape(nc, FWD_ROWS, width))

        clip = clip_of(norm_tile, max_norm[0])
        rate = learn_rate[0]
        up_w, up_m, up_v = adamw_update(w_up[0], m_up[0], v_up[0], clip * gu_full, rate)
        down_w, down_m, down_v = adamw_update(w_down[0], m_down[0], v_down[0], clip * gd_full, rate)
        return (up_w[None], down_w[None], up_m[None], down_m[None], up_v[None], down_v[None], y_next.reshape(n_micro, rows, width))

    return jax.shard_map(device_step, mesh=mesh, in_specs=in_specs, out_specs=out_specs, check_vma=False)
```

time: 1100 us -> 384 us (0.35)
  waiting for transfers between devices: 859 us -> 0 us
  Pallas kernels: 0 us -> 353 us
  starting transfers between devices: 50.8 us -> 0 us
  local copies, waits for them, and re-layouts: 50.1 us -> 4.33 us
  other arithmetic: 63.9 us -> 23.8 us
  matrix products: 39.5 us -> 0 us
  between operations: 20.8 us -> 2.72 us
    psum x11 -> x0, waiting for transfers between devices: 795 us -> none  [the longest x6 361 us: device_step(): summed = lax.psum(branch, 'model')]
    pallas_call x0 -> x2, Pallas kernels: none -> 353 us  [the longest x1 206 us: device_step(): pl.pallas_call(functools.partial(fwd_kernel, dims), out_shape=(sds((width...]
    ppermute x14 -> x0, waiting for transfers between devices: 64.2 us -> none  [the longest x3 25.9 us: device_step(): upstream = lax.ppermute(grad_in, 'stage', down_perm)]
    ppermute x14 -> x0, starting transfers between devices: 50.3 us -> none  [the longest x5 19.5 us: device_step(): acts_cur = lax.ppermute(acts_out, 'stage', up_perm)]
    convert_element_type x12 -> x0, other arithmetic: 47.6 us -> none  [the longest x1 16 us: apply_update(): up_w.astype(jnp.bfloat16)]
    dot_general x8 -> x0, matrix products: 39.5 us -> none  [the longest x3 15.4 us: fwd_local(): return jnp.dot(hidden, down_new_bf, preferred_element_type=jnp.float32)]
    broadcast_in_dim x0 -> x2, other arithmetic: none -> 22.5 us  [the longest x1 13.8 us: device_step(): up_v[None]]
    cond x45 -> x0, local copies, waits for them, and re-layouts: 21.4 us -> none
  transfers between devices with their start and end apart: 25 -> 0, of which waited for: 21 -> 0; matrix products, arithmetic and copies ran while one was open for 3% -> 0% of each run, Pallas kernels for 0% -> 0%
where the time goes in v1:
time: 384 us; the launch traced here: 383 us
  Pallas kernels  353 us (92%)
  other arithmetic  23.8 us (6%)
  local copies, waits for them, and re-layouts  4.33 us (1%)
    pallas_call x1, Pallas kernels, device_step(): pl.pallas_call(functools.partial(fwd_kernel, dims), out_shape=(sds((width...  206 us
    pallas_call x1, Pallas kernels, device_step(): pl.pallas_call(functools.partial(bwd_kernel, dims), out_shape=(sds((width...  146 us
    broadcast_in_dim x1, other arithmetic, device_step(): up_v[None]  13.8 us
    broadcast_in_dim x1, other arithmetic, device_step(): down_v[None]  8.67 us

profile of v1, /device:TPU:1, one launch (start us, length us, event | category | flops | bytes accessed | tf_op | source)
XLA Modules:
  0.0 383.4 jit_solution(15790862699334229681)
XLA Ops:
  1.9 146.2 %backward.1 = (f32[768,768]{1,0:T(8,128)}, f32[768,768]{1,0:T(8,128)}, f32[8,128]{1,0:T(8,128)}) custom-call(f32[768,1536]{1,0:T(8,128)} %bitcast.40, f32[1536,768]{1,0:T(8,128)} %bitcast.42, bf16[512,768]{1,0:T(8,128)(2,1)} %bitcast.52, bf16[512,768]{1,0:T(8,128)(2,1)} %dy_hbm.1, f32[768,1536]{1,0:T(8,128)} %bitcast.48, f32[1536,768]{1,0:T(8,128)} %bitcast.49), custom_call_target="tpu_custom_call" | custom-call | tf_op jit(solution)/shard_map/backward/pallas_call | solution.py:461
  148.1 1.3 reduce_sum.8
  150.1 206.4 %forward.1 = (f32[768,1536]{1,0:T(8,128)}, f32[1536,768]{1,0:T(8,128)}, bf16[12,128,768]{2,1,0:T(8,128)(2,1)}) custom-call(f32[8,128]{1,0:T(8,128)} %get-tuple-element.13.norm_ref, f32[1]{0:T(128)} %copy.21.lr_ref, f32[1]{0:T(128)} %copy.22.mn_ref, f32[768,1536]{1,0:T(8,128)} %bitcast.41, f32[1536,768]{1,0:T(8,128)} %bitcast.43, f32[768,1536]{1,0:T(8,128)} %bitcast.44, ...), custom_call_target="tpu_custom_call" | custom-call | tf_op jit(solution)/shard_map/forward/pallas_call | solution.py:487
  356.5 0.0 copy-start
  356.5 0.0 copy-start.1
  356.6 0.0 copy-start.2
  356.6 0.0 copy-start.3
  356.6 13.8 %fusion.5 = (f32[1,768,1536]{2,1,0:T(8,128)}, f32[1,768,1536]{2,1,0:T(8,128)}, f32[1,768,1536]{2,1,0:T(8,128)}) fusion(f32[768,1536]{1,0:T(8,128)} %get-tuple-element.16, f32[]{:T(128)} %bitcast.9, f32[1,768,1536]{2,1,0:T(8,128)} %param.17, f32[1,768,1536]{2,1,0:T(8,128)} %param.15, f32[]{:T(128)} %bitcast.37, f32[1,768,1536]{2,1,0:T(8,128)} %param.13), kind=kLoop, calls=%fused_computation.11 | loop fusion | flops 18874368 | bytes 33030152 | tf_op jit(solution)/shard_map/broadcast_in_dim | solution.py:508
  370.4 0.0 copy-done
  370.4 0.0 copy-done.1
  370.4 1.6 copy-done.2
  371.9 1.3 copy-done.3
  373.3 0.0 copy-start.4
  373.3 8.7 %fusion.4 = (f32[1,1536,768]{2,1,0:T(8,128)}, f32[1,1536,768]{2,1,0:T(8,128)}, f32[1,1536,768]{2,1,0:T(8,128)}) fusion(f32[1536,768]{1,0:T(8,128)S(1)} %copy-done.3, f32[]{:T(128)} %bitcast.9, f32[1,1536,768]{2,1,0:T(8,128)S(1)} %copy-done.2, f32[1,1536,768]{2,1,0:T(8,128)S(1)} %copy-done.1, f32[]{:T(128)} %bitcast.38, f32[1,1536,768]{2,1,0:T(8,128)S(1)} %copy-done), kind=kLoop, calls=%fused_computation.10 | loop fusion | flops 18874368 | bytes 33030152 | tf_op jit(solution)/shard_map/broadcast_in_dim | solution.py:508
  382.0 0.0 copy-done.4
  382.0 1.4 copy.23
Async XLA Ops:
  356.5 13.8 %copy-start = (f32[1,1536,768]{2,1,0:T(8,128)S(1)}, f32[1,1536,768]{2,1,0:T(8,128)}, u32[]{:S(2)}) copy-start(f32[1,1536,768]{2,1,0:T(8,128)} %param.14) | copy-start | bytes 14155780
  356.5 13.8 %copy-start.1 = (f32[1,1536,768]{2,1,0:T(8,128)S(1)}, f32[1,1536,768]{2,1,0:T(8,128)}, u32[]{:S(2)}) copy-start(f32[1,1536,768]{2,1,0:T(8,128)} %param.16) | copy-start | bytes 14155780
  356.6 15.4 %copy-start.2 = (f32[1,1536,768]{2,1,0:T(8,128)S(1)}, f32[1,1536,768]{2,1,0:T(8,128)}, u32[]{:S(2)}) copy-start(f32[1,1536,768]{2,1,0:T(8,128)} %param.18) | copy-start | bytes 14155780
  356.6 16.7 %copy-start.3 = (f32[1536,768]{1,0:T(8,128)S(1)}, f32[1536,768]{1,0:T(8,128)}, u32[]{:S(2)}) copy-start(f32[1536,768]{1,0:T(8,128)} %get-tuple-element.17) | copy-start | bytes 14155780
  373.3 8.7 %copy-start.4 = (bf16[12,128,768]{2,1,0:T(8,128)(2,1)S(1)}, bf16[12,128,768]{2,1,0:T(8,128)(2,1)}, u32[]{:S(2)}) copy-start(bf16[12,128,768]{2,1,0:T(8,128)(2,1)} %get-tuple-element.18) | copy-start | bytes 7077892

commit v2 on v1

--- a/solution.py
+++ b/solution.py
@@ -24,7 +24,9 @@
 BF16 = jnp.bfloat16
 MESH = pl.DeviceIdType.MESH
 BACK_ROWS = 128
-FWD_ROWS = 128
+FWD_ROWS = 64
+UPD_ROWS = 128
+TURN_STEP = 8
 VMEM_LIMIT = 66_000_000
 
 
@@ -75,8 +77,8 @@
 
 def bwd_kernel(dims, wu_hbm, wd_hbm, acts_hbm, dy_hbm, gu_hbm, gd_hbm,
                gbu_hbm, gbd_hbm, norm_out,
-               wu32, wd32, wu_bf, wd_bf, aa, gg, hh, dzz, slope, slope_o, dz_own, h_own,
-               gu_own, gd_own, gu_rcv, gd_rcv, part, part_rcv, fin, norm_buf,
+               wu32, wd32, wu_bf, wd_bf, aa, gg, hid_o, dz_o, slope, slope_o, dz_own, h_own,
+               gu_own, gd_own, gu_oth, gd_oth, gu_rcv, gd_rcv, part, part_rcv, fin, norm_buf,
                ld_sem, ysend, yrecv, psend, precv, fsend, frecv, nsend, nrecv, st_sem):
     n_model, n_data, n_stage = dims
     z, d, p = lax.axis_index('model'), lax.axis_index('data'), lax.axis_index('stage')
@@ -85,7 +87,7 @@
     last = n_stage - 1
     rows = aa.shape[0] // 2
     width = aa.shape[1]
-    half = hh.shape[1]
+    half = hid_o.shape[1]
     rb = BACK_ROWS
     hb = rb // 2
     nb = rows // rb
@@ -100,21 +102,35 @@
         pltpu.make_async_copy(gu_hbm.at[:, own_ff], gu_own, ld_sem.at[4]),
         pltpu.make_async_copy(gd_hbm.at[own_ff, :], gd_own, ld_sem.at[5]),
     ]
-    for copy in loads:
+    dy_load = pltpu.make_async_copy(dy_hbm, gg.at[mine], ld_sem.at[3])
+    gu_load = pltpu.make_async_copy(gu_hbm.at[:, oth_ff], gu_oth, ld_sem.at[6])
+    gd_load = pltpu.make_async_copy(gd_hbm.at[oth_ff, :], gd_oth, ld_sem.at[7])
+    for copy in loads[:3]:
         copy.start()
-    dy_load = pltpu.make_async_copy(dy_hbm, gg.at[mine], ld_sem.at[3])
 
     @pl.when(p == last)
     def _():
         dy_load.start()
+    for copy in loads[3:]:
+        copy.start()
+
+    @pl.when(p > 0)
+    def _():
+        gd_load.start()
+        gu_load.start()
 
     whole_barrier(n_model, n_data, n_stage)
     send_acts = remote(acts_hbm, aa.at[theirs], ysend.at[0], yrecv.at[0], ypeer)
-    send_gu = remote(gu_hbm.at[:, oth_ff], gu_rcv, ysend.at[1], yrecv.at[1], ypeer)
-    send_gd = remote(gd_hbm.at[oth_ff, :], gd_rcv, ysend.at[2], yrecv.at[2], ypeer)
+    raw_gu = remote(gu_hbm.at[:, oth_ff], gu_rcv, ysend.at[1], yrecv.at[1], ypeer)
+    raw_gd = remote(gd_hbm.at[oth_ff, :], gd_rcv, ysend.at[2], yrecv.at[2], ypeer)
+    sum_gu = remote(gu_oth, gu_rcv, ysend.at[1], yrecv.at[1], ypeer)
+    sum_gd = remote(gd_oth, gd_rcv, ysend.at[2], yrecv.at[2], ypeer)
     send_g = remote(gg.at[mine], gg.at[theirs], ysend.at[3], yrecv.at[3], ypeer)
-    send_acts.start()
-    send_gu.start()
+
+    @pl.when(p == 0)
+    def _():
+        send_acts.start()
+        raw_gu.start()
 
     loads[0].wait()
     loads[1].wait()
@@ -175,51 +191,88 @@
         for zi in range(n_model):
             fin_copy(c, zi).start()
 
-    lag = jnp.where(p == last, 1, 0)
-
     def chain(i, carry):
         @pl.when(i < nb)
         def _():
             compute(i)
-        f = i - lag
-
-        @pl.when((f >= 0) & (f < nb) & (p > 0))
-        def _():
-            finalize(f)
+
+        @pl.when((i >= 1) & (p > 0))
+        def _():
+            finalize(i - 1)
         return carry
     lax.fori_loop(0, nb + 1, chain, 0)
 
-    send_g.start()
-    send_gd.start()
-
-    hh[mine, :] = h_own[:, own_ff]
-    dzz[mine, :] = dz_own[:, own_ff]
-    send_acts.wait_recv()
-
-    def oth_pre(i, carry):
-        at = pl.ds(pl.multiple_of(rows + i * rb, rb), rb)
-        val, slp = gelu_both(mm(aa[at, :], wu_bf[:, own_ff], NN))
-        hh[at, :] = val.astype(BF16)
-        slope_o[pl.ds(pl.multiple_of(i * rb, rb), rb), :] = slp
-        return carry
-    lax.fori_loop(0, nb, oth_pre, 0)
-    send_g.wait_recv()
-
-    def oth_dz(i, carry):
-        at = pl.ds(pl.multiple_of(rows + i * rb, rb), rb)
-        grad_hid = mm(gg[at, :], wd_bf[own_ff, :], NT)
-        dzz[at, :] = (slope_o[pl.ds(pl.multiple_of(i * rb, rb), rb), :] * grad_hid).astype(BF16)
-        return carry
-    lax.fori_loop(0, nb, oth_dz, 0)
+    def down_block(j, base):
+        at = pl.ds(pl.multiple_of(base * half + j * 128, 128), 128)
+        return mm(h_own[:, at], gg[mine, :], TN)
+
+    def up_block(j, ff_at):
+        at = pl.ds(pl.multiple_of(j * 128, 128), 128)
+        return mm(aa[mine, at], dz_own[:, ff_at], TN)
+
+    @pl.when(p > 0)
+    def _():
+        gd_load.wait()
+
+        def down_oth(j, carry):
+            gd_oth[pl.ds(pl.multiple_of(j * 128, 128), 128), :] += down_block(j, do)
+            return carry
+        lax.fori_loop(0, half // 128, down_oth, 0)
+        gu_load.wait()
+        sum_gd.start()
+
+        def up_oth(j, carry):
+            gu_oth[pl.ds(pl.multiple_of(j * 128, 128), 128), :] += up_block(j, oth_ff)
+            return carry
+        lax.fori_loop(0, width // 128, up_oth, 0)
+
+    @pl.when(p == 0)
+    def _():
+        send_g.start()
+        raw_gd.start()
     loads[3].wait()
     loads[4].wait()
 
-    def weight_grads(j, carry):
-        at = pl.ds(pl.multiple_of(j * 128, 128), 128)
-        gd_own[at, :] += mm(hh[:, at], gg[...], TN)
-        gu_own[at, :] += mm(aa[:, at], dzz[...], TN)
-        return carry
-    lax.fori_loop(0, half // 128, weight_grads, 0)
+    def down_own(j, carry):
+        gd_own[pl.ds(pl.multiple_of(j * 128, 128), 128), :] += down_block(j, d)
+        return carry
+    lax.fori_loop(0, half // 128, down_own, 0)
+
+    @pl.when(p > 0)
+    def _():
+        sum_gu.start()
+
+    def up_own(j, carry):
+        gu_own[pl.ds(pl.multiple_of(j * 128, 128), 128), :] += up_block(j, own_ff)
+        return carry
+    lax.fori_loop(0, width // 128, up_own, 0)
+
+    @pl.when(p == 0)
+    def _():
+        send_acts.wait_recv()
+
+        def oth_pre(i, carry):
+            at = pl.ds(pl.multiple_of(i * rb, rb), rb)
+            val, slp = gelu_both(mm(aa[pl.ds(pl.multiple_of(rows + i * rb, rb), rb), :], wu_bf[:, own_ff], NN))
+            hid_o[at, :] = val.astype(BF16)
+            slope_o[at, :] = slp
+            return carry
+        lax.fori_loop(0, nb, oth_pre, 0)
+        send_g.wait_recv()
+
+        def oth_dz(i, carry):
+            at = pl.ds(pl.multiple_of(i * rb, rb), rb)
+            grad_hid = mm(gg[pl.ds(pl.multiple_of(rows + i * rb, rb), rb), :], wd_bf[own_ff, :], NT)
+            dz_o[at, :] = (slope_o[at, :] * grad_hid).astype(BF16)
+            return carry
+        lax.fori_loop(0, nb, oth_dz, 0)
+
+        def oth_grads(j, carry):
+            at = pl.ds(pl.multiple_of(j * 128, 128), 128)
+            gd_own[at, :] += mm(hid_o[:, at], gg[theirs, :], TN)
+            gu_own[at, :] += mm(aa[theirs, at], dz_o[...], TN)
+            return carry
+        lax.fori_loop(0, half // 128, oth_grads, 0)
 
     def combine(own, rcv):
         def body(i, acc):
@@ -228,15 +281,21 @@
             own[at, :] = mean
             return acc + jnp.sum((mean * mean).reshape(4, 8, mean.shape[1]), axis=0)
         return body
+
+    def combine_up(acc):
+        raw_gu.wait_recv()
+        return lax.fori_loop(0, gu_own.shape[0] // 32, combine(gu_own, gu_rcv), acc)
+
+    def combine_down(acc):
+        raw_gd.wait_recv()
+        return lax.fori_loop(0, gd_own.shape[0] // 32, combine(gd_own, gd_rcv), acc)
     acc = jnp.zeros((8, half), F32)
-    send_gu.wait_recv()
-    acc = lax.fori_loop(0, gu_own.shape[0] // 32, combine(gu_own, gu_rcv), acc)
+    acc = combine_down(acc)
+    store_d = pltpu.make_async_copy(gd_own, gbd_hbm, st_sem.at[1])
+    store_d.start()
+    acc = combine_up(acc)
     store_u = pltpu.make_async_copy(gu_own, gbu_hbm, st_sem.at[0])
     store_u.start()
-    send_gd.wait_recv()
-    acc = lax.fori_loop(0, gd_own.shape[0] // 32, combine(gd_own, gd_rcv), acc)
-    store_d = pltpu.make_async_copy(gd_own, gbd_hbm, st_sem.at[1])
-    store_d.start()
     tile = acc[:, 0:128]
     for k in range(1, half // 128):
         tile = tile + acc[:, k * 128:(k + 1) * 128]
@@ -260,11 +319,16 @@
 
     for k in range(1, n_all):
         norm_copy(k).wait_send()
-    for copy in (send_acts, send_gu, send_gd, send_g):
-        copy.wait_send()
+
+    @pl.when(p == 0)
+    def _():
+        for copy in (send_acts, raw_gu, raw_gd, send_g):
+            copy.wait_send()
 
     @pl.when(p > 0)
     def _():
+        sum_gu.wait_send()
+        sum_gd.wait_send()
         for c in range(nb):
             part_copy(c).wait_send()
             for zi in range(n_model):
@@ -273,71 +337,69 @@
     store_d.wait()
 
 
-def fwd_kernel(dims, norm_ref, lr_ref, mn_ref, wu_hbm, wd_hbm, mu_hbm, md_hbm, vu_hbm, vd_hbm, gbu_hbm, gbd_hbm, x_hbm,
-               gu_full, gd_full, y_hbm,
-               wu32, wd32, mu32, md32, vu32, vd32, gu32, gd32, wu_bf, wd_bf, a_buf, y_buf, part, part_rcv, fin,
-               ld_sem, ysend, yrecv, psend, precv, fsend, frecv, agsend, agrecv, outsend, outrecv, st_sem):
+def update_kernel(d_ref, lr_ref, mn_ref, norm_ref, gu, gd, wu, wd, mu, md, vu, vd, *rest):
+    owu, owd, omu, omd, ovu, ovd = rest[:6]
+    clip = clip_of(norm_ref[...], mn_ref[0])
+    rate = lr_ref[0]
+    owu[...], omu[...], ovu[...] = adamw_update(wu[...], mu[...], vu[...], clip * gu[...], rate)
+    owd[...], omd[...], ovd[...] = adamw_update(wd[...], md[...], vd[...], clip * gd[...], rate)
+    if len(rest) == 8:
+        rest[6][...] = owu[...].astype(BF16)
+        rest[7][...] = owd[...].astype(BF16)
+
+
+def fill_kernel(d_ref, lr_ref, mn_ref, norm_ref, gu, gd, wu, wd, mu, md, vu, vd, *rest):
+    update_kernel(d_ref, lr_ref, mn_ref, norm_ref, gu, gd, wu, wd, mu, md, vu, vd, *rest[6:])
+
+
+def fwd_kernel(dims, bu_hbm, bd_hbm, gbu_hbm, gbd_hbm, x_hbm,
+               gu_oth, gd_oth, y_hbm,
+               wu_bf, wd_bf, a_buf, y_buf, part, part_rcv, fin,
+               ld_sem, ysend, yrecv, psend, precv, fsend, frecv, agsend, agrecv, outsend, outrecv, turn):
     n_model, n_data, n_stage = dims
     z, d, p = lax.axis_index('model'), lax.axis_index('data'), lax.axis_index('stage')
     zo, do = 1 - z, 1 - d
     ypeer, zpeer = (z, do, p), (zo, d, p)
     last = n_stage - 1
-    half = wu32.shape[1]
     nc, rb, width = a_buf.shape
+    half = wu_bf.shape[1] // 2
     hb = rb // 2
     own_ff = pl.ds(pl.multiple_of(d * half, 128), half)
-
-    loads = [
-        pltpu.make_async_copy(gbu_hbm, gu32, ld_sem.at[0]),
-        pltpu.make_async_copy(wu_hbm.at[:, own_ff], wu32, ld_sem.at[1]),
-        pltpu.make_async_copy(mu_hbm.at[:, own_ff], mu32, ld_sem.at[2]),
-        pltpu.make_async_copy(vu_hbm.at[:, own_ff], vu32, ld_sem.at[3]),
-        pltpu.make_async_copy(gbd_hbm, gd32, ld_sem.at[4]),
-        pltpu.make_async_copy(wd_hbm.at[own_ff, :], wd32, ld_sem.at[5]),
-        pltpu.make_async_copy(md_hbm.at[own_ff, :], md32, ld_sem.at[6]),
-        pltpu.make_async_copy(vd_hbm.at[own_ff, :], vd32, ld_sem.at[7]),
-    ]
-    for copy in loads:
-        copy.start()
-    x_load = pltpu.make_async_copy(x_hbm, a_buf, ld_sem.at[8])
+    even = lax.rem(p, 2) == 0
+
+    load_u = pltpu.make_async_copy(bu_hbm, wu_bf.at[:, own_ff], ld_sem.at[0])
+    load_d = pltpu.make_async_copy(bd_hbm, wd_bf.at[own_ff, :], ld_sem.at[1])
+    load_u.start()
+    load_d.start()
+    x_load = pltpu.make_async_copy(x_hbm, a_buf, ld_sem.at[2])
 
     @pl.when(p == 0)
     def _():
         x_load.start()
     whole_barrier(n_model, n_data, n_stage)
 
-    clip = clip_of(norm_ref[...], mn_ref[0])
-    rate = lr_ref[0]
-    for copy in loads[:4]:
-        copy.wait()
-
-    def update_up(i, carry):
-        at = pl.ds(pl.multiple_of(i * 32, 32), 32)
-        new = adamw_update(wu32[at, :], mu32[at, :], vu32[at, :], clip * gu32[at, :], rate)[0]
-        wu_bf[at, own_ff] = new.astype(BF16)
-        return carry
-    lax.fori_loop(0, width // 32, update_up, 0)
     send_wu = remote(wu_bf.at[:, own_ff], wu_bf.at[:, own_ff], ysend.at[0], yrecv.at[0], ypeer)
     send_wd = remote(wd_bf.at[own_ff, :], wd_bf.at[own_ff, :], ysend.at[1], yrecv.at[1], ypeer)
-    send_gu = remote(gu32, gu_full.at[:, own_ff], ysend.at[2], yrecv.at[2], ypeer)
-    send_gd = remote(gd32, gd_full.at[own_ff, :], ysend.at[3], yrecv.at[3], ypeer)
-    for copy in loads[4:]:
-        copy.wait()
-    send_wu.start()
-
-    def update_down(i, carry):
-        at = pl.ds(pl.multiple_of(i * 32, 32), 32)
-        new = adamw_update(wd32[at, :], md32[at, :], vd32[at, :], clip * gd32[at, :], rate)[0]
-        wd_bf[pl.ds(pl.multiple_of(d * half + i * 32, 32), 32), :] = new.astype(BF16)
-        return carry
-    lax.fori_loop(0, half // 32, update_down, 0)
-    store_u = pltpu.make_async_copy(gu32, gu_full.at[:, own_ff], st_sem.at[0])
-    store_d = pltpu.make_async_copy(gd32, gd_full.at[own_ff, :], st_sem.at[1])
-    store_u.start()
-    store_d.start()
-    send_wd.start()
-    send_gu.start()
-    send_gd.start()
+    send_gu = remote(gbu_hbm, gu_oth, ysend.at[2], yrecv.at[2], ypeer)
+    send_gd = remote(gbd_hbm, gd_oth, ysend.at[3], yrecv.at[3], ypeer)
+    load_u.wait()
+    load_d.wait()
+
+    @pl.when(even)
+    def _():
+        send_wu.start()
+        send_wd.start()
+        send_wu.wait_send()
+        send_wd.wait_send()
+        pl.semaphore_signal(turn, inc=1, device_id=(z, d, p + 1), device_id_type=MESH)
+
+    @pl.when(jnp.logical_not(even))
+    def _():
+        pl.semaphore_wait(turn, 1)
+        send_wu.start()
+        send_wd.start()
+        send_gu.start()
+        send_gd.start()
 
     @pl.when(p == 0)
     def _():
@@ -394,23 +456,32 @@
         for q in range(last):
             out_copy(c, q).start()
 
-    lag = jnp.where(p == 0, 1, 0)
-
     def chain(i, carry):
         @pl.when(i < nc)
         def _():
             compute(i)
-        f = i - lag
-
-        @pl.when((f >= 0) & (f < nc))
-        def _():
-            finalize(f)
-
-        @pl.when((i >= 1) & (p == last))
-        def _():
-            publish(i - 1)
-        return carry
-    lax.fori_loop(0, nc + 1, chain, 0)
+
+        @pl.when((i >= 1) & (i <= nc))
+        def _():
+            finalize(i - 1)
+
+        @pl.when((i >= 2) & (p == last))
+        def _():
+            publish(i - 2)
+
+        @pl.when((i == TURN_STEP) & even)
+        def _():
+            pl.semaphore_wait(turn, 1)
+            send_gu.start()
+            send_gd.start()
+
+        @pl.when((i == TURN_STEP - 1) & jnp.logical_not(even))
+        def _():
+            send_wu.wait_send()
+            send_wd.wait_send()
+            pl.semaphore_signal(turn, inc=1, device_id=(z, d, p - 1), device_id_type=MESH)
+        return carry
+    lax.fori_loop(0, nc + 2, chain, 0)
 
     def drain(c, carry):
         part_copy(c).wait_send()
@@ -429,10 +500,6 @@
                 out_copy(c, q).wait_send()
         return carry
     lax.fori_loop(0, nc, drain, 0)
-    send_wu.wait_send()
-    send_wd.wait_send()
-    store_u.wait()
-    store_d.wait()
     send_gu.wait()
     send_gd.wait()
 
@@ -467,44 +534,75 @@
                 pltpu.VMEM((width, ff), F32), pltpu.VMEM((ff, width), F32),
                 pltpu.VMEM((width, ff), BF16), pltpu.VMEM((ff, width), BF16),
                 pltpu.VMEM((2 * rows, width), BF16), pltpu.VMEM((2 * rows, width), BF16),
-                pltpu.VMEM((2 * rows, half), BF16), pltpu.VMEM((2 * rows, half), BF16),
+                pltpu.VMEM((rows, half), BF16), pltpu.VMEM((rows, half), BF16),
                 pltpu.VMEM((rows, ff), F32), pltpu.VMEM((rows, half), F32),
                 pltpu.VMEM((rows, ff), BF16), pltpu.VMEM((rows, ff), BF16),
-                pltpu.VMEM((width, half), F32), pltpu.VMEM((half, width), F32),
-                pltpu.VMEM((width, half), F32), pltpu.VMEM((half, width), F32),
+            ] + [pltpu.VMEM((width, half), F32), pltpu.VMEM((half, width), F32)] * 3 + [
                 pltpu.VMEM((nb, BACK_ROWS, width), F32), pltpu.VMEM((nb, hb, width), F32),
                 pltpu.VMEM((nb, hb, width), BF16), pltpu.VMEM((n_all, 8, 128), F32),
-                dma((6,)), dma((4,)), dma((4,)), dma((nb,)), dma((nb,)), dma((nb, 2)), dma((nb, 2)),
+                dma((8,)), dma((4,)), dma((4,)), dma((nb,)), dma((nb,)), dma((nb, 2)), dma((nb, 2)),
                 dma((n_all,)), dma((n_all,)), dma((2,)),
             ],
             compiler_params=pltpu.CompilerParams(collective_id=0, has_side_effects=True, vmem_limit_bytes=VMEM_LIMIT),
             name='backward',
         )(w_up[0], w_down[0], acts_last[0], grad_out, g_up[0, 0], g_down[0, 0])
 
+        blocks = half // UPD_ROWS
+        state = (w_up[0], w_down[0], m_up[0], m_down[0], v_up[0], v_down[0])
+        state_shapes = tuple(sds(s.shape, F32) for s in state)
+        which = lax.axis_index('data').astype(jnp.int32).reshape(1)
+
+        def update_specs(pick):
+            up = pl.BlockSpec((UPD_ROWS, half), lambda i, w: (i, pick(w[0])))
+            down = pl.BlockSpec((UPD_ROWS, width), lambda i, w: (pick(w[0]) * blocks + i, 0))
+            return [up, down]
+        plain_up = pl.BlockSpec((UPD_ROWS, half), lambda i, w: (i, 0))
+        plain_down = pl.BlockSpec((UPD_ROWS, width), lambda i, w: (i, 0))
+        small = [smem_spec, smem_spec, pl.BlockSpec((8, 128), lambda i, w: (0, 0))]
+        own = update_specs(lambda w: w)
+        *fresh, b_up, b_down = pl.pallas_call(
+            update_kernel,
+            out_shape=state_shapes + (sds((width, half), BF16), sds((half, width), BF16)),
+            grid_spec=pltpu.PrefetchScalarGridSpec(
+                num_scalar_prefetch=1, grid=(width // UPD_ROWS,),
+                in_specs=small + [plain_up, plain_down] + own * 3,
+                out_specs=own * 3 + [plain_up, plain_down]),
+            compiler_params=pltpu.CompilerParams(dimension_semantics=('arbitrary',), vmem_limit_bytes=VMEM_LIMIT),
+            name='update_own',
+        )(which, learn_rate, max_norm, norm_tile, gbar_u, gbar_d, *state)
+
         n_micro = x_next.shape[0]
         nc = n_micro * rows // FWD_ROWS
         fb = FWD_ROWS // 2
-        gu_full, gd_full, y_next = pl.pallas_call(
+        gu_oth, gd_oth, y_next = pl.pallas_call(
             functools.partial(fwd_kernel, dims),
-            out_shape=(sds((width, ff), F32), sds((ff, width), F32), sds((nc, FWD_ROWS, width), BF16)),
-            in_specs=[vmem_spec, smem_spec, smem_spec] + [any_spec] * 9,
+            out_shape=(sds((width, half), F32), sds((half, width), F32), sds((nc, FWD_ROWS, width), BF16)),
+            in_specs=[any_spec] * 5,
             out_specs=(any_spec, any_spec, any_spec),
-            scratch_shapes=[pltpu.VMEM((width, half), F32), pltpu.VMEM((half, width), F32)] * 4 + [
+            scratch_shapes=[
                 pltpu.VMEM((width, ff), BF16), pltpu.VMEM((ff, width), BF16),
                 pltpu.VMEM((nc, FWD_ROWS, width), BF16), pltpu.VMEM((nc, FWD_ROWS, width), BF16),
                 pltpu.VMEM((nc, FWD_ROWS, width), F32), pltpu.VMEM((nc, fb, width), F32),
                 pltpu.VMEM((nc, fb, width), BF16),
-                dma((9,)), dma((4,)), dma((4,)), dma((nc,)), dma((nc,)), dma((nc, 2)), dma((nc, 2)),
-                dma((nc,)), dma((nc,)), dma((nc, n_stage)), dma((nc,)), dma((2,)),
+                dma((3,)), dma((4,)), dma((4,)), dma((nc,)), dma((nc,)), dma((nc, 2)), dma((nc, 2)),
+                dma((nc,)), dma((nc,)), dma((nc, n_stage)), dma((nc,)), pltpu.SemaphoreType.REGULAR,
             ],
             compiler_params=pltpu.CompilerParams(collective_id=1, has_side_effects=True, vmem_limit_bytes=VMEM_LIMIT),
             name='forward',
-        )(norm_tile, learn_rate, max_norm, w_up[0], w_down[0], m_up[0], m_down[0], v_up[0], v_down[0], gbar_u, gbar_d, x_next.reshape(nc, FWD_ROWS, width))
-
-        clip = clip_of(norm_tile, max_norm[0])
-        rate = learn_rate[0]
-        up_w, up_m, up_v = adamw_update(w_up[0], m_up[0], v_up[0], clip * gu_full, rate)
-        down_w, down_m, down_v = adamw_update(w_down[0], m_down[0], v_down[0], clip * gd_full, rate)
-        return (up_w[None], down_w[None], up_m[None], down_m[None], up_v[None], down_v[None], y_next.reshape(n_micro, rows, width))
+        )(b_up, b_down, gbar_u, gbar_d, x_next.reshape(nc, FWD_ROWS, width))
+
+        other = update_specs(lambda w: 1 - w)
+        filled = pl.pallas_call(
+            fill_kernel,
+            out_shape=state_shapes,
+            grid_spec=pltpu.PrefetchScalarGridSpec(
+                num_scalar_prefetch=1, grid=(width // UPD_ROWS,),
+                in_specs=small + [plain_up, plain_down] + other * 3 + [any_spec] * 6,
+                out_specs=other * 3),
+            input_output_aliases={12 + k: k for k in range(6)},
+            compiler_params=pltpu.CompilerParams(dimension_semantics=('arbitrary',), vmem_limit_bytes=VMEM_LIMIT),
+            name='update_other',
+        )(which, learn_rate, max_norm, norm_tile, gu_oth, gd_oth, *state, *fresh)
+        return tuple(s[None] for s in filled) + (y_next.reshape(n_micro, rows, width),)
 
     return jax.shard_map(device_step, mesh=mesh, in_specs=in_specs, out_specs=out_specs, check_vma=False)

time: 384 us -> 341 us (0.89)
  other arithmetic: 23.8 us -> 0 us
  Pallas kernels: 353 us -> 336 us
    pallas_call x1, Pallas kernels: 206 us -> 167 us  [device_step(): pl.pallas_call(functools.partial(fwd_kernel, dims), out_shape=(sds((width...]
    pallas_call x0 -> x2, Pallas kernels: none -> 28.8 us  [the longest x1 14.7 us: device_step(): pl.pallas_call(update_kernel, out_shape=state_shapes + (sds((width, half)...]
    broadcast_in_dim x2 -> x0, other arithmetic: 22.5 us -> none  [the longest x1 13.8 us: device_step(): up_v[None]]
    pallas_call x1, Pallas kernels: 146 us -> 140 us  [device_step(): pl.pallas_call(functools.partial(bwd_kernel, dims), out_shape=(sds((width...]
where the time goes in v2:
time: 341 us
  Pallas kernels  336 us (99%)
    pallas_call x1, Pallas kernels, device_step(): pl.pallas_call(functools.partial(fwd_kernel, dims), out_shape=(sds((width...  167 us
    pallas_call x1, Pallas kernels, device_step(): pl.pallas_call(functools.partial(bwd_kernel, dims), out_shape=(sds((width...  140 us
    pallas_call x1, Pallas kernels, device_step(): pl.pallas_call(update_kernel, out_shape=state_shapes + (sds((width, half)...  14.7 us
    pallas_call x1, Pallas kernels, device_step(): pl.pallas_call(fill_kernel, out_shape=state_shapes, grid_spec=pltpu.Prefe...  14.1 us

profile of v2, /device:TPU:1, one launch (start us, length us, event | category | flops | bytes accessed | tf_op | source)
XLA Modules:
  0.0 341.0 jit_solution(3390741537756948162)
XLA Ops:
  1.9 139.6 %backward.1 = (f32[768,768]{1,0:T(8,128)}, f32[768,768]{1,0:T(8,128)}, f32[8,128]{1,0:T(8,128)}) custom-call(f32[768,1536]{1,0:T(8,128)} %bitcast.18, f32[1536,768]{1,0:T(8,128)} %bitcast.21, bf16[512,768]{1,0:T(8,128)(2,1)} %bitcast.42, bf16[512,768]{1,0:T(8,128)(2,1)} %dy_hbm.1, f32[768,1536]{1,0:T(8,128)} %bitcast.32, f32[1536,768]{1,0:T(8,128)} %bitcast.33), custom_call_target="tpu_custom_call" | custom-call | tf_op jit(solution)/shard_map/backward/pallas_call | solution.py:528
  141.5 14.7 %update_own.1 = (f32[768,1536]{1,0:T(8,128)}, f32[1536,768]{1,0:T(8,128)}, f32[768,1536]{1,0:T(8,128)}, f32[1536,768]{1,0:T(8,128)}, f32[768,1536]{1,0:T(8,128)}...) custom-call(s32[1]{0:T(128)} %bitcast.d_ref, f32[1]{0:T(128)S(6)} %copy.33.lr_ref, ...), custom_call_target="tpu_custom_call" | custom-call | tf_op jit(solution)/shard_map/update_own/pallas_call | solution.py:563
  156.2 167.4 %forward.1 = (f32[768,768]{1,0:T(8,128)}, f32[768,768]{1,0:T(8,128)}, bf16[24,64,768]{2,1,0:T(8,128)(2,1)}) custom-call(bf16[768,768]{1,0:T(8,128)(2,1)} %get-tuple-element.30.bu_hbm, bf16[768,768]{1,0:T(8,128)(2,1)} %get-tuple-element.31.bd_hbm, f32[768,768]{1,0:T(8,128)} %get-tuple-element.28.gu.gbu_hbm, f32[768,768]{1,0:T(8,128)} %get-tuple-element.29.gd.gbd_hbm, ...), custom_call_target="tpu_custom_call" | custom-call | tf_op jit(solution)/shard_map/forward/pallas_call | solution.py:577
  323.7 14.1 %update_other.1 = (f32[768,1536]{1,0:T(8,128)}, f32[1536,768]{1,0:T(8,128)}, f32[768,1536]{1,0:T(8,128)}, f32[1536,768]{1,0:T(8,128)}, f32[768,1536]{1,0:T(8,128)}, /*index=5*/f32[1536,768]{1,0:T(8,128)}) custom-call(s32[1]{0:T(128)} %bitcast.d_ref, ...), custom_call_target="tpu_custom_call", output_to_operand_aliasing={{0}: (12, {}), {1}: (13, {}), {2}: (14, {}), {3}: (15, {}),... | custom-call | tf_op jit(solution)/shard_map/update_other/pallas_call | solution.py:595
  337.8 3.2 copy.35

commit v3 on v2

--- a/solution.py
+++ b/solution.py
@@ -25,7 +25,8 @@
 MESH = pl.DeviceIdType.MESH
 BACK_ROWS = 128
 FWD_ROWS = 64
-UPD_ROWS = 128
+UPD_ROWS = 64
+EARLY_ROWS = 256
 TURN_STEP = 8
 VMEM_LIMIT = 66_000_000
 
@@ -76,7 +77,7 @@
 
 
 def bwd_kernel(dims, wu_hbm, wd_hbm, acts_hbm, dy_hbm, gu_hbm, gd_hbm,
-               gbu_hbm, gbd_hbm, norm_out,
+               gbu_hbm, gbd_hbm, early_hbm, norm_out,
                wu32, wd32, wu_bf, wd_bf, aa, gg, hid_o, dz_o, slope, slope_o, dz_own, h_own,
                gu_own, gd_own, gu_oth, gd_oth, gu_rcv, gd_rcv, part, part_rcv, fin, norm_buf,
                ld_sem, ysend, yrecv, psend, precv, fsend, frecv, nsend, nrecv, st_sem):
@@ -85,6 +86,8 @@
     zo, do = 1 - z, 1 - d
     ypeer, zpeer = (z, do, p), (zo, d, p)
     last = n_stage - 1
+    by_rows = lax.rem(p, 2) == 0
+    by_sums = lax.rem(p, 2) == 1
     rows = aa.shape[0] // 2
     width = aa.shape[1]
     half = hid_o.shape[1]
@@ -114,7 +117,7 @@
     for copy in loads[3:]:
         copy.start()
 
-    @pl.when(p > 0)
+    @pl.when(by_sums)
     def _():
         gd_load.start()
         gu_load.start()
@@ -127,9 +130,10 @@
     sum_gd = remote(gd_oth, gd_rcv, ysend.at[2], yrecv.at[2], ypeer)
     send_g = remote(gg.at[mine], gg.at[theirs], ysend.at[3], yrecv.at[3], ypeer)
 
-    @pl.when(p == 0)
+    @pl.when(by_rows)
     def _():
         send_acts.start()
+        raw_gd.start()
         raw_gu.start()
 
     loads[0].wait()
@@ -210,7 +214,7 @@
         at = pl.ds(pl.multiple_of(j * 128, 128), 128)
         return mm(aa[mine, at], dz_own[:, ff_at], TN)
 
-    @pl.when(p > 0)
+    @pl.when(by_sums)
     def _():
         gd_load.wait()
 
@@ -226,10 +230,9 @@
             return carry
         lax.fori_loop(0, width // 128, up_oth, 0)
 
-    @pl.when(p == 0)
+    @pl.when(by_rows)
     def _():
         send_g.start()
-        raw_gd.start()
     loads[3].wait()
     loads[4].wait()
 
@@ -238,7 +241,7 @@
         return carry
     lax.fori_loop(0, half // 128, down_own, 0)
 
-    @pl.when(p > 0)
+    @pl.when(by_sums)
     def _():
         sum_gu.start()
 
@@ -247,7 +250,7 @@
         return carry
     lax.fori_loop(0, width // 128, up_own, 0)
 
-    @pl.when(p == 0)
+    @pl.when(by_rows)
     def _():
         send_acts.wait_recv()
 
@@ -293,6 +296,8 @@
     acc = combine_down(acc)
     store_d = pltpu.make_async_copy(gd_own, gbd_hbm, st_sem.at[1])
     store_d.start()
+    store_early = pltpu.make_async_copy(gd_own.at[pl.ds(0, early_hbm.shape[0])], early_hbm, st_sem.at[2])
+    store_early.start()
     acc = combine_up(acc)
     store_u = pltpu.make_async_copy(gu_own, gbu_hbm, st_sem.at[0])
     store_u.start()
@@ -320,21 +325,25 @@
     for k in range(1, n_all):
         norm_copy(k).wait_send()
 
-    @pl.when(p == 0)
+    @pl.when(by_rows)
     def _():
         for copy in (send_acts, raw_gu, raw_gd, send_g):
             copy.wait_send()
 
-    @pl.when(p > 0)
+    @pl.when(by_sums)
     def _():
         sum_gu.wait_send()
         sum_gd.wait_send()
+
+    @pl.when(p > 0)
+    def _():
         for c in range(nb):
             part_copy(c).wait_send()
             for zi in range(n_model):
                 fin_copy(c, zi).wait_send()
     store_u.wait()
     store_d.wait()
+    store_early.wait()
 
 
 def update_kernel(d_ref, lr_ref, mn_ref, norm_ref, gu, gd, wu, wd, mu, md, vu, vd, *rest):
@@ -348,8 +357,14 @@
         rest[7][...] = owd[...].astype(BF16)
 
 
-def fill_kernel(d_ref, lr_ref, mn_ref, norm_ref, gu, gd, wu, wd, mu, md, vu, vd, *rest):
-    update_kernel(d_ref, lr_ref, mn_ref, norm_ref, gu, gd, wu, wd, mu, md, vu, vd, *rest[6:])
+def fill_kernel(d_ref, lr_ref, mn_ref, norm_ref, gu, gd_early, gd_late, y_in, wu, wd, mu, md, vu, vd, *rest):
+    owu, owd, omu, omd, ovu, ovd, y_out = rest[6:]
+    clip = clip_of(norm_ref[...], mn_ref[0])
+    rate = lr_ref[0]
+    gd = jnp.where(pl.program_id(0) < EARLY_ROWS // UPD_ROWS, gd_early[...], gd_late[...])
+    owu[...], omu[...], ovu[...] = adamw_update(wu[...], mu[...], vu[...], clip * gu[...], rate)
+    owd[...], omd[...], ovd[...] = adamw_update(wd[...], md[...], vd[...], clip * gd, rate)
+    y_out[...] = y_in[...]
 
 
 def fwd_kernel(dims, bu_hbm, bd_hbm, gbu_hbm, gbd_hbm, x_hbm,
@@ -381,7 +396,7 @@
     send_wu = remote(wu_bf.at[:, own_ff], wu_bf.at[:, own_ff], ysend.at[0], yrecv.at[0], ypeer)
     send_wd = remote(wd_bf.at[own_ff, :], wd_bf.at[own_ff, :], ysend.at[1], yrecv.at[1], ypeer)
     send_gu = remote(gbu_hbm, gu_oth, ysend.at[2], yrecv.at[2], ypeer)
-    send_gd = remote(gbd_hbm, gd_oth, ysend.at[3], yrecv.at[3], ypeer)
+    send_gd = remote(gbd_hbm.at[pl.ds(half - gd_oth.shape[0], gd_oth.shape[0])], gd_oth, ysend.at[3], yrecv.at[3], ypeer)
     load_u.wait()
     load_d.wait()
 
@@ -525,11 +540,11 @@
         nb = rows // BACK_ROWS
         hb = BACK_ROWS // 2
         sds = jax.ShapeDtypeStruct
-        gbar_u, gbar_d, norm_tile = pl.pallas_call(
+        gbar_u, gbar_d, early, norm_tile = pl.pallas_call(
             functools.partial(bwd_kernel, dims),
-            out_shape=(sds((width, half), F32), sds((half, width), F32), sds((8, 128), F32)),
+            out_shape=(sds((width, half), F32), sds((half, width), F32), sds((EARLY_ROWS, width), F32), sds((8, 128), F32)),
             in_specs=[any_spec] * 6,
-            out_specs=(any_spec, any_spec, vmem_spec),
+            out_specs=(any_spec, any_spec, any_spec, vmem_spec),
             scratch_shapes=[
                 pltpu.VMEM((width, ff), F32), pltpu.VMEM((ff, width), F32),
                 pltpu.VMEM((width, ff), BF16), pltpu.VMEM((ff, width), BF16),
@@ -541,12 +556,13 @@
                 pltpu.VMEM((nb, BACK_ROWS, width), F32), pltpu.VMEM((nb, hb, width), F32),
                 pltpu.VMEM((nb, hb, width), BF16), pltpu.VMEM((n_all, 8, 128), F32),
                 dma((8,)), dma((4,)), dma((4,)), dma((nb,)), dma((nb,)), dma((nb, 2)), dma((nb, 2)),
-                dma((n_all,)), dma((n_all,)), dma((2,)),
+                dma((n_all,)), dma((n_all,)), dma((3,)),
             ],
             compiler_params=pltpu.CompilerParams(collective_id=0, has_side_effects=True, vmem_limit_bytes=VMEM_LIMIT),
             name='backward',
         )(w_up[0], w_down[0], acts_last[0], grad_out, g_up[0, 0], g_down[0, 0])
 
+        early_oth = lax.ppermute(early, 'data', [(k, 1 - k) for k in range(n_data)])
         blocks = half // UPD_ROWS
         state = (w_up[0], w_down[0], m_up[0], m_down[0], v_up[0], v_down[0])
         state_shapes = tuple(sds(s.shape, F32) for s in state)
@@ -576,7 +592,7 @@
         fb = FWD_ROWS // 2
         gu_oth, gd_oth, y_next = pl.pallas_call(
             functools.partial(fwd_kernel, dims),
-            out_shape=(sds((width, half), F32), sds((half, width), F32), sds((nc, FWD_ROWS, width), BF16)),
+            out_shape=(sds((width, half), F32), sds((half - EARLY_ROWS, width), F32), sds((nc, FWD_ROWS, width), BF16)),
             in_specs=[any_spec] * 5,
             out_specs=(any_spec, any_spec, any_spec),
             scratch_shapes=[
@@ -592,17 +608,22 @@
         )(b_up, b_down, gbar_u, gbar_d, x_next.reshape(nc, FWD_ROWS, width))
 
         other = update_specs(lambda w: 1 - w)
-        filled = pl.pallas_call(
+        ne = EARLY_ROWS // UPD_ROWS
+        steps = width // UPD_ROWS
+        early_spec = pl.BlockSpec((UPD_ROWS, width), lambda i, w: (jnp.minimum(i, ne - 1), 0))
+        late_spec = pl.BlockSpec((UPD_ROWS, width), lambda i, w: (jnp.maximum(i - ne, 0), 0))
+        y_spec = pl.BlockSpec((nc // steps, FWD_ROWS, width), lambda i, w: (i, 0, 0))
+        *filled, y_next = pl.pallas_call(
             fill_kernel,
-            out_shape=state_shapes,
+            out_shape=state_shapes + (sds(y_next.shape, BF16),),
             grid_spec=pltpu.PrefetchScalarGridSpec(
-                num_scalar_prefetch=1, grid=(width // UPD_ROWS,),
-                in_specs=small + [plain_up, plain_down] + other * 3 + [any_spec] * 6,
-                out_specs=other * 3),
-            input_output_aliases={12 + k: k for k in range(6)},
+                num_scalar_prefetch=1, grid=(steps,),
+                in_specs=small + [plain_up, early_spec, late_spec, y_spec] + other * 3 + [any_spec] * 6,
+                out_specs=other * 3 + [y_spec]),
+            input_output_aliases={14 + k: k for k in range(6)},
             compiler_params=pltpu.CompilerParams(dimension_semantics=('arbitrary',), vmem_limit_bytes=VMEM_LIMIT),
             name='update_other',
-        )(which, learn_rate, max_norm, norm_tile, gu_oth, gd_oth, *state, *fresh)
+        )(which, learn_rate, max_norm, norm_tile, gu_oth, early_oth, gd_oth, y_next, *state, *fresh)
         return tuple(s[None] for s in filled) + (y_next.reshape(n_micro, rows, width),)
 
     return jax.shard_map(device_step, mesh=mesh, in_specs=in_specs, out_specs=out_specs, check_vma=False)

time: 341 us -> 336 us (0.985)
  Pallas kernels: 336 us -> 332 us
    pallas_call x1, Pallas kernels: 140 us -> 131 us  [device_step(): pl.pallas_call(functools.partial(bwd_kernel, dims), out_shape=(sds((width...]
    pallas_call x1, Pallas kernels: 14.1 us -> 17.6 us  [device_step(): pl.pallas_call(fill_kernel, out_shape=state_shapes + (sds(y_next.shape, B...]
  transfers between devices with their start and end apart: 0 -> 1, of which waited for: 0 -> 0; matrix products, arithmetic and copies ran while one was open for 0% -> 0% of each run, Pallas kernels for 0% -> 55%
where the time goes in v3:
time: 336 us; the launch traced here: 335 us
  Pallas kernels  332 us (99%)
    pallas_call x1, Pallas kernels, device_step(): pl.pallas_call(functools.partial(fwd_kernel, dims), out_shape=(sds((width...  166 us
    pallas_call x1, Pallas kernels, device_step(): pl.pallas_call(functools.partial(bwd_kernel, dims), out_shape=(sds((width...  131 us
    pallas_call x1, Pallas kernels, device_step(): pl.pallas_call(fill_kernel, out_shape=state_shapes + (sds(y_next.shape, B...  17.6 us
    pallas_call x1, Pallas kernels, device_step(): pl.pallas_call(update_kernel, out_shape=state_shapes + (sds((width, half)...  17.4 us
  transfers between devices with their start and end apart: 1, of which 0 were waited for; matrix products, arithmetic and copies ran while one was open for 0% of the time, Pallas kernels for 55%

profile of v3, /device:TPU:1, one launch (start us, length us, event | category | flops | bytes accessed | tf_op | source)
XLA Modules:
  0.0 335.4 jit_solution(15017044212083530407)
XLA Ops:
  0.6 130.7 %backward.1 = (f32[768,768]{1,0:T(8,128)}, f32[768,768]{1,0:T(8,128)}, f32[256,768]{1,0:T(8,128)}, f32[8,128]{1,0:T(8,128)}) custom-call(f32[768,1536]{1,0:T(8,128)} %bitcast.18, f32[1536,768]{1,0:T(8,128)} %bitcast.21, bf16[512,768]{1,0:T(8,128)(2,1)} %bitcast.41, bf16[512,768]{1,0:T(8,128)(2,1)} %dy_hbm.1, f32[768,1536]{1,0:T(8,128)} %bitcast.32, ...), custom_call_target="tpu_custom_call" | custom-call | tf_op jit(solution)/shard_map/backward/pallas_call | solution.py:543
  131.3 0.4 collective-permute-start
  133.0 17.4 %update_own.1 = (f32[768,1536]{1,0:T(8,128)}, f32[1536,768]{1,0:T(8,128)}, f32[768,1536]{1,0:T(8,128)}, f32[1536,768]{1,0:T(8,128)}, f32[768,1536]{1,0:T(8,128)}...) custom-call(s32[1]{0:T(128)} %bitcast.d_ref, f32[1]{0:T(128)S(6)} %copy.32.lr_ref, ...), custom_call_target="tpu_custom_call" | custom-call | tf_op jit(solution)/shard_map/update_own/pallas_call | solution.py:579
  150.4 166.4 %forward.1 = (f32[768,768]{1,0:T(8,128)}, f32[512,768]{1,0:T(8,128)}, bf16[24,64,768]{2,1,0:T(8,128)(2,1)}) custom-call(bf16[768,768]{1,0:T(8,128)(2,1)} %get-tuple-element.32.bu_hbm, bf16[768,768]{1,0:T(8,128)(2,1)} %get-tuple-element.33.bd_hbm, f32[768,768]{1,0:T(8,128)} %get-tuple-element.30.gu.gbu_hbm, f32[768,768]{1,0:T(8,128)} %get-tuple-element.31.gd.gbd_hbm, ...), custom_call_target="tpu_custom_call" | custom-call | tf_op jit(solution)/shard_map/forward/pallas_call | solution.py:593
  316.9 0.0 collective-permute-done.gd_early
  316.9 0.0 copy-start
  316.9 0.9 copy-done
  317.8 17.6 %update_other.1 = (f32[768,1536]{1,0:T(8,128)}, f32[1536,768]{1,0:T(8,128)}, f32[768,1536]{1,0:T(8,128)}, f32[1536,768]{1,0:T(8,128)}, f32[768,1536]{1,0:T(8,128...) custom-call(s32[1]{0:T(128)} %bitcast.d_ref, ...), custom_call_target="tpu_custom_call", output_to_operand_aliasing={{0}: (14, {}), {1}: (15, {}), {2}: (16, {}), {3}: (17, {}),... | custom-call | tf_op jit(solution)/shard_map/update_other/pallas_call | solution.py:616
Async XLA Ops:
  131.3 185.6 %collective-permute-start = (f32[256,768]{1,0:T(8,128)}, f32[256,768]{1,0:T(8,128)S(1)}, u32[]{:S(2)}, u32[]{:S(2)}) collective-permute-start(f32[256,768]{1,0:T(8,128)} %get-tuple-element.35), channel_id=1, source_target_pairs={{0,4},{4,0},{1,5},{5,1},{2,6},{6,2},{3,7},{7,3},{8,12},{12,8},{9,1... | collective-permute-start | bytes 2359304 | tf_op jit(solution)/shard_map/ppermute | solution.py:565
  316.9 0.9 copy-start

commit v4 on v3

--- a/solution.py
+++ b/solution.py
@@ -24,10 +24,10 @@
 BF16 = jnp.bfloat16
 MESH = pl.DeviceIdType.MESH
 BACK_ROWS = 128
-FWD_ROWS = 64
-UPD_ROWS = 64
+FWD_ROWS = 128
+UPD_ROWS = 128
 EARLY_ROWS = 256
-TURN_STEP = 8
+TURN_STEP = 4
 VMEM_LIMIT = 66_000_000
 
 

time: 336 us -> 333 us (level)
  no operation moved by 1% of the time
where the time goes in v4:
time: 333 us; the launch traced here: 332 us
  Pallas kernels  329 us (99%)
    pallas_call x1, Pallas kernels, device_step(): pl.pallas_call(functools.partial(fwd_kernel, dims), out_shape=(sds((width...  168 us
    pallas_call x1, Pallas kernels, device_step(): pl.pallas_call(functools.partial(bwd_kernel, dims), out_shape=(sds((width...  131 us
    pallas_call x1, Pallas kernels, device_step(): pl.pallas_call(fill_kernel, out_shape=state_shapes + (sds(y_next.shape, B...  16 us
    pallas_call x1, Pallas kernels, device_step(): pl.pallas_call(update_kernel, out_shape=state_shapes + (sds((width, half)...  14.8 us
  transfers between devices with their start and end apart: 1, of which 0 were waited for; matrix products, arithmetic and copies ran while one was open for 0% of the time, Pallas kernels for 55%

profile of v4, /device:TPU:1, one launch (start us, length us, event | category | flops | bytes accessed | tf_op | source)
XLA Modules:
  0.0 332.5 jit_solution(3930971704263807490)
XLA Ops:
  0.6 130.7 %backward.1 = (f32[768,768]{1,0:T(8,128)}, f32[768,768]{1,0:T(8,128)}, f32[256,768]{1,0:T(8,128)}, f32[8,128]{1,0:T(8,128)}) custom-call(f32[768,1536]{1,0:T(8,128)} %bitcast.18, f32[1536,768]{1,0:T(8,128)} %bitcast.21, bf16[512,768]{1,0:T(8,128)(2,1)} %bitcast.41, bf16[512,768]{1,0:T(8,128)(2,1)} %dy_hbm.1, f32[768,1536]{1,0:T(8,128)} %bitcast.32, ...), custom_call_target="tpu_custom_call" | custom-call | tf_op jit(solution)/shard_map/backward/pallas_call | solution.py:543
  131.3 0.4 collective-permute-start
  133.0 14.8 %update_own.1 = (f32[768,1536]{1,0:T(8,128)}, f32[1536,768]{1,0:T(8,128)}, f32[768,1536]{1,0:T(8,128)}, f32[1536,768]{1,0:T(8,128)}, f32[768,1536]{1,0:T(8,128)}...) custom-call(s32[1]{0:T(128)} %bitcast.d_ref, f32[1]{0:T(128)S(6)} %copy.32.lr_ref, ...), custom_call_target="tpu_custom_call" | custom-call | tf_op jit(solution)/shard_map/update_own/pallas_call | solution.py:579
  147.8 167.8 %forward.1 = (f32[768,768]{1,0:T(8,128)}, f32[512,768]{1,0:T(8,128)}, bf16[12,128,768]{2,1,0:T(8,128)(2,1)}) custom-call(bf16[768,768]{1,0:T(8,128)(2,1)} %get-tuple-element.32.bu_hbm, bf16[768,768]{1,0:T(8,128)(2,1)} %get-tuple-element.33.bd_hbm, f32[768,768]{1,0:T(8,128)} %get-tuple-element.30.gu.gbu_hbm, f32[768,768]{1,0:T(8,128)} %get-tuple-element.31.gd.gbd_hbm, ...), custom_call_target="tpu_custom_call" | custom-call | tf_op jit(solution)/shard_map/forward/pallas_call | solution.py:593
  315.6 0.0 collective-permute-done.gd_early
  315.6 0.0 copy-start
  315.6 0.9 copy-done
  316.5 16.0 %update_other.1 = (f32[768,1536]{1,0:T(8,128)}, f32[1536,768]{1,0:T(8,128)}, f32[768,1536]{1,0:T(8,128)}, f32[1536,768]{1,0:T(8,128)}, f32[768,1536]{1,0:T(8,128...) custom-call(s32[1]{0:T(128)} %bitcast.d_ref, ...), custom_call_target="tpu_custom_call", output_to_operand_aliasing={{0}: (14, {}), {1}: (15, {}), {2}: (16, {}), {3}: (17, {}),... | custom-call | tf_op jit(solution)/shard_map/update_other/pallas_call | solution.py:616
Async XLA Ops:
  131.3 184.3 %collective-permute-start = (f32[256,768]{1,0:T(8,128)}, f32[256,768]{1,0:T(8,128)S(1)}, u32[]{:S(2)}, u32[]{:S(2)}) collective-permute-start(f32[256,768]{1,0:T(8,128)} %get-tuple-element.35), channel_id=1, source_target_pairs={{0,4},{4,0},{1,5},{5,1},{2,6},{6,2},{3,7},{7,3},{8,12},{12,8},{9,1... | collective-permute-start | bytes 2359304 | tf_op jit(solution)/shard_map/ppermute | solution.py:565
  315.6 0.9 copy-start

commit v5 on v3

--- a/solution.py
+++ b/solution.py
@@ -25,7 +25,7 @@
 MESH = pl.DeviceIdType.MESH
 BACK_ROWS = 128
 FWD_ROWS = 64
-UPD_ROWS = 64
+UPD_ROWS = 128
 EARLY_ROWS = 256
 TURN_STEP = 8
 VMEM_LIMIT = 66_000_000
@@ -369,8 +369,8 @@
 
 def fwd_kernel(dims, bu_hbm, bd_hbm, gbu_hbm, gbd_hbm, x_hbm,
                gu_oth, gd_oth, y_hbm,
-               wu_bf, wd_bf, a_buf, y_buf, part, part_rcv, fin,
-               ld_sem, ysend, yrecv, psend, precv, fsend, frecv, agsend, agrecv, outsend, outrecv, turn):
+               wu_bf, wd_bf, wu_z, wd_z, a_buf, y_buf, part, part_rcv, fin,
+               ld_sem, ysend, yrecv, zsend, zrecv, psend, precv, fsend, frecv, agsend, agrecv, outsend, outrecv, turn):
     n_model, n_data, n_stage = dims
     z, d, p = lax.axis_index('model'), lax.axis_index('data'), lax.axis_index('stage')
     zo, do = 1 - z, 1 - d
@@ -380,7 +380,9 @@
     half = wu_bf.shape[1] // 2
     hb = rb // 2
     own_ff = pl.ds(pl.multiple_of(d * half, 128), half)
-    even = lax.rem(p, 2) == 0
+    oth_ff = pl.ds(pl.multiple_of(do * half, 128), half)
+    first = (p == 0) | (p == last)
+    partner = (z, d, p + 1 - 2 * lax.rem(p, 2))
 
     load_u = pltpu.make_async_copy(bu_hbm, wu_bf.at[:, own_ff], ld_sem.at[0])
     load_d = pltpu.make_async_copy(bd_hbm, wd_bf.at[own_ff, :], ld_sem.at[1])
@@ -400,27 +402,52 @@
     load_u.wait()
     load_d.wait()
 
-    @pl.when(even)
+    shard = [
+        remote(wu_bf.at[:, own_ff], wu_z.at[:, own_ff], zsend.at[0], zrecv.at[0], zpeer),
+        remote(wd_bf.at[own_ff, :], wd_z.at[own_ff, :], zsend.at[1], zrecv.at[1], zpeer),
+        remote(wu_bf.at[:, oth_ff], wu_z.at[:, oth_ff], zsend.at[2], zrecv.at[2], zpeer),
+        remote(wd_bf.at[oth_ff, :], wd_z.at[oth_ff, :], zsend.at[3], zrecv.at[3], zpeer),
+    ]
+
+    @pl.when(p == last)
+    def _():
+        shard[0].start()
+        shard[1].start()
+
+    @pl.when(first)
     def _():
         send_wu.start()
         send_wd.start()
         send_wu.wait_send()
         send_wd.wait_send()
-        pl.semaphore_signal(turn, inc=1, device_id=(z, d, p + 1), device_id_type=MESH)
-
-    @pl.when(jnp.logical_not(even))
+        pl.semaphore_signal(turn, inc=1, device_id=partner, device_id_type=MESH)
+
+    @pl.when(jnp.logical_not(first))
     def _():
         pl.semaphore_wait(turn, 1)
         send_wu.start()
         send_wd.start()
         send_gu.start()
         send_gd.start()
+        send_wu.wait_send()
+        send_wd.wait_send()
+        pl.semaphore_signal(turn, inc=1, device_id=partner, device_id_type=MESH)
 
     @pl.when(p == 0)
     def _():
         x_load.wait()
     send_wu.wait_recv()
+
+    @pl.when(p == last)
+    def _():
+        shard[2].start()
     send_wd.wait_recv()
+
+    @pl.when(p == last)
+    def _():
+        shard[3].start()
+        for copy in shard:
+            copy.wait_recv()
 
     def half_rows(zi):
         return pl.ds(pl.multiple_of(zi * hb, hb), hb)
@@ -440,30 +467,43 @@
     def out_local(c):
         return pltpu.make_async_copy(y_buf.at[c], y_hbm.at[c], outsend.at[c, last])
 
+    def arrived(c, zi):
+        pltpu.make_async_copy(fin.at[c], a_buf.at[c, half_rows(zi)], frecv.at[c, zi]).wait()
+
+    def branch(rows_in, w_up, w_down):
+        hid = gelu_val(mm(rows_in, w_up[...], NN)).astype(BF16)
+        return mm(hid, w_down[...], NN)
+
     def compute(c):
-        @pl.when(p > 0)
-        def _():
-            for zi in range(n_model):
-                pltpu.make_async_copy(fin.at[c], a_buf.at[c, half_rows(zi)], frecv.at[c, zi]).wait()
-        hid = gelu_val(mm(a_buf[c], wu_bf[...], NN)).astype(BF16)
-        part[c] = mm(hid, wd_bf[...], NN)
-        part_copy(c).start()
+        @pl.when(p < last)
+        def _():
+            @pl.when(p > 0)
+            def _():
+                for zi in range(n_model):
+                    arrived(c, zi)
+            part[c] = branch(a_buf[c], wu_bf, wd_bf)
+            part_copy(c).start()
+
+        @pl.when(p == last)
+        def _():
+            arrived(c, z)
+            at = half_rows(z)
+            rows_in = a_buf[c, at, :]
+            total = branch(rows_in, wu_bf, wd_bf) + branch(rows_in, wu_z, wd_z)
+            new = (rows_in.astype(F32) + total).astype(BF16)
+            fin[c] = new
+            y_buf[c, at, :] = new
+            gather_copy(c).start()
 
     def finalize(c):
         part_copy(c).wait_recv()
         total = part[c, half_rows(z), :] + part_rcv[c]
-        new = (a_buf[c, half_rows(z), :].astype(F32) + total).astype(BF16)
-        fin[c] = new
-
-        @pl.when(p < last)
-        def _():
-            for zi in range(n_model):
-                fin_copy(c, zi).start()
-
-        @pl.when(p == last)
-        def _():
-            y_buf[c, half_rows(z), :] = new
-            gather_copy(c).start()
+        fin[c] = (a_buf[c, half_rows(z), :].astype(F32) + total).astype(BF16)
+        fin_copy(c, z).start()
+
+        @pl.when(p < last - 1)
+        def _():
+            fin_copy(c, zo).start()
 
     def publish(c):
         gather_copy(c).wait_recv()
@@ -476,35 +516,31 @@
         def _():
             compute(i)
 
-        @pl.when((i >= 1) & (i <= nc))
+        @pl.when((i >= 1) & (i <= nc) & (p < last))
         def _():
             finalize(i - 1)
 
-        @pl.when((i >= 2) & (p == last))
-        def _():
-            publish(i - 2)
-
-        @pl.when((i == TURN_STEP) & even)
+        @pl.when((i >= 1) & (i <= nc) & (p == last))
+        def _():
+            publish(i - 1)
+
+        @pl.when((i == TURN_STEP) & first)
         def _():
             pl.semaphore_wait(turn, 1)
             send_gu.start()
             send_gd.start()
-
-        @pl.when((i == TURN_STEP - 1) & jnp.logical_not(even))
-        def _():
-            send_wu.wait_send()
-            send_wd.wait_send()
-            pl.semaphore_signal(turn, inc=1, device_id=(z, d, p - 1), device_id_type=MESH)
-        return carry
-    lax.fori_loop(0, nc + 2, chain, 0)
+        return carry
+    lax.fori_loop(0, nc + 1, chain, 0)
 
     def drain(c, carry):
-        part_copy(c).wait_send()
-
         @pl.when(p < last)
         def _():
-            for zi in range(n_model):
-                fin_copy(c, zi).wait_send()
+            part_copy(c).wait_send()
+            fin_copy(c, z).wait_send()
+
+            @pl.when(p < last - 1)
+            def _():
+                fin_copy(c, zo).wait_send()
             pltpu.make_async_copy(y_buf.at[c], y_hbm.at[c], outrecv.at[c]).wait()
 
         @pl.when(p == last)
@@ -515,6 +551,11 @@
                 out_copy(c, q).wait_send()
         return carry
     lax.fori_loop(0, nc, drain, 0)
+
+    @pl.when(p == last)
+    def _():
+        for copy in shard:
+            copy.wait_send()
     send_gu.wait()
     send_gd.wait()
 
@@ -595,12 +636,11 @@
             out_shape=(sds((width, half), F32), sds((half - EARLY_ROWS, width), F32), sds((nc, FWD_ROWS, width), BF16)),
             in_specs=[any_spec] * 5,
             out_specs=(any_spec, any_spec, any_spec),
-            scratch_shapes=[
-                pltpu.VMEM((width, ff), BF16), pltpu.VMEM((ff, width), BF16),
+            scratch_shapes=[pltpu.VMEM((width, ff), BF16), pltpu.VMEM((ff, width), BF16)] * 2 + [
                 pltpu.VMEM((nc, FWD_ROWS, width), BF16), pltpu.VMEM((nc, FWD_ROWS, width), BF16),
                 pltpu.VMEM((nc, FWD_ROWS, width), F32), pltpu.VMEM((nc, fb, width), F32),
                 pltpu.VMEM((nc, fb, width), BF16),
-                dma((3,)), dma((4,)), dma((4,)), dma((nc,)), dma((nc,)), dma((nc, 2)), dma((nc, 2)),
+                dma((3,)), dma((4,)), dma((4,)), dma((4,)), dma((4,)), dma((nc,)), dma((nc,)), dma((nc, 2)), dma((nc, 2)),
                 dma((nc,)), dma((nc,)), dma((nc, n_stage)), dma((nc,)), pltpu.SemaphoreType.REGULAR,
             ],
             compiler_params=pltpu.CompilerParams(collective_id=1, has_side_effects=True, vmem_limit_bytes=VMEM_LIMIT),

time: 336 us -> 309 us (0.920)
  Pallas kernels: 332 us -> 304 us
    pallas_call x1, Pallas kernels: 166 us -> 142 us  [device_step(): pl.pallas_call(functools.partial(fwd_kernel, dims), out_shape=(sds((width...]
  transfers between devices with their start and end apart: 1 -> 1, of which waited for: 0 -> 0; matrix products, arithmetic and copies ran while one was open for 0% -> 0% of each run, Pallas kernels for 55% -> 51%
where the time goes in v5:
time: 309 us; the launch traced here: 307 us
  Pallas kernels  304 us (98%)
    pallas_call x1, Pallas kernels, device_step(): pl.pallas_call(functools.partial(fwd_kernel, dims), out_shape=(sds((width...  142 us
    pallas_call x1, Pallas kernels, device_step(): pl.pallas_call(functools.partial(bwd_kernel, dims), out_shape=(sds((width...  131 us
    pallas_call x1, Pallas kernels, device_step(): pl.pallas_call(fill_kernel, out_shape=state_shapes + (sds(y_next.shape, B...  16 us
    pallas_call x1, Pallas kernels, device_step(): pl.pallas_call(update_kernel, out_shape=state_shapes + (sds((width, half)...  14.8 us
  transfers between devices with their start and end apart: 1, of which 0 were waited for; matrix products, arithmetic and copies ran while one was open for 0% of the time, Pallas kernels for 51%

profile of v5, /device:TPU:1, one launch (start us, length us, event | category | flops | bytes accessed | tf_op | source)
XLA Modules:
  0.0 307.1 jit_solution(5076093379071411984)
XLA Ops:
  0.6 130.7 %backward.1 = (f32[768,768]{1,0:T(8,128)}, f32[768,768]{1,0:T(8,128)}, f32[256,768]{1,0:T(8,128)}, f32[8,128]{1,0:T(8,128)}) custom-call(f32[768,1536]{1,0:T(8,128)} %bitcast.18, f32[1536,768]{1,0:T(8,128)} %bitcast.21, bf16[512,768]{1,0:T(8,128)(2,1)} %bitcast.41, bf16[512,768]{1,0:T(8,128)(2,1)} %dy_hbm.1, f32[768,1536]{1,0:T(8,128)} %bitcast.32, ...), custom_call_target="tpu_custom_call" | custom-call | tf_op jit(solution)/shard_map/backward/pallas_call | solution.py:584
  131.3 0.4 collective-permute-start
  133.0 14.8 %update_own.1 = (f32[768,1536]{1,0:T(8,128)}, f32[1536,768]{1,0:T(8,128)}, f32[768,1536]{1,0:T(8,128)}, f32[1536,768]{1,0:T(8,128)}, f32[768,1536]{1,0:T(8,128)}...) custom-call(s32[1]{0:T(128)} %bitcast.d_ref, f32[1]{0:T(128)S(6)} %copy.32.lr_ref, ...), custom_call_target="tpu_custom_call" | custom-call | tf_op jit(solution)/shard_map/update_own/pallas_call | solution.py:620
  147.8 142.4 %forward.1 = (f32[768,768]{1,0:T(8,128)}, f32[512,768]{1,0:T(8,128)}, bf16[24,64,768]{2,1,0:T(8,128)(2,1)}) custom-call(bf16[768,768]{1,0:T(8,128)(2,1)} %get-tuple-element.32.bu_hbm, bf16[768,768]{1,0:T(8,128)(2,1)} %get-tuple-element.33.bd_hbm, f32[768,768]{1,0:T(8,128)} %get-tuple-element.30.gu.gbu_hbm, f32[768,768]{1,0:T(8,128)} %get-tuple-element.31.gd.gbd_hbm, ...), custom_call_target="tpu_custom_call" | custom-call | tf_op jit(solution)/shard_map/forward/pallas_call | solution.py:634
  290.2 0.0 collective-permute-done.gd_early
  290.2 0.0 copy-start
  290.3 0.9 copy-done
  291.1 16.0 %update_other.1 = (f32[768,1536]{1,0:T(8,128)}, f32[1536,768]{1,0:T(8,128)}, f32[768,1536]{1,0:T(8,128)}, f32[1536,768]{1,0:T(8,128)}, f32[768,1536]{1,0:T(8,128...) custom-call(s32[1]{0:T(128)} %bitcast.d_ref, ...), custom_call_target="tpu_custom_call", output_to_operand_aliasing={{0}: (14, {}), {1}: (15, {}), {2}: (16, {}), {3}: (17, {}),... | custom-call | tf_op jit(solution)/shard_map/update_other/pallas_call | solution.py:656
Async XLA Ops:
  131.3 158.9 %collective-permute-start = (f32[256,768]{1,0:T(8,128)}, f32[256,768]{1,0:T(8,128)S(1)}, u32[]{:S(2)}, u32[]{:S(2)}) collective-permute-start(f32[256,768]{1,0:T(8,128)} %get-tuple-element.35), channel_id=1, source_target_pairs={{0,4},{4,0},{1,5},{5,1},{2,6},{6,2},{3,7},{7,3},{8,12},{12,8},{9,1... | collective-permute-start | bytes 2359304 | tf_op jit(solution)/shard_map/ppermute | solution.py:606
  290.2 0.9 copy-start

commit v6 on v5

--- a/solution.py
+++ b/solution.py
@@ -26,7 +26,9 @@
 BACK_ROWS = 128
 FWD_ROWS = 64
 UPD_ROWS = 128
+PRE_ROWS = 128
 EARLY_ROWS = 256
+LATE_ROWS = 128
 TURN_STEP = 8
 VMEM_LIMIT = 66_000_000
 
@@ -77,7 +79,7 @@
 
 
 def bwd_kernel(dims, wu_hbm, wd_hbm, acts_hbm, dy_hbm, gu_hbm, gd_hbm,
-               gbu_hbm, gbd_hbm, early_hbm, norm_out,
+               gbu_hbm, gbd_hbm, early_hbm, late_hbm, pre_oth, norm_out,
                wu32, wd32, wu_bf, wd_bf, aa, gg, hid_o, dz_o, slope, slope_o, dz_own, h_own,
                gu_own, gd_own, gu_oth, gd_oth, gu_rcv, gd_rcv, part, part_rcv, fin, norm_buf,
                ld_sem, ysend, yrecv, psend, precv, fsend, frecv, nsend, nrecv, st_sem):
@@ -296,11 +298,15 @@
     acc = combine_down(acc)
     store_d = pltpu.make_async_copy(gd_own, gbd_hbm, st_sem.at[1])
     store_d.start()
-    store_early = pltpu.make_async_copy(gd_own.at[pl.ds(0, early_hbm.shape[0])], early_hbm, st_sem.at[2])
+    store_early = pltpu.make_async_copy(gd_own.at[pl.ds(PRE_ROWS, EARLY_ROWS)], early_hbm, st_sem.at[2])
     store_early.start()
+    send_pre = remote(gd_own.at[pl.ds(0, PRE_ROWS)], pre_oth, ysend.at[4], yrecv.at[4], ypeer)
+    send_pre.start()
     acc = combine_up(acc)
     store_u = pltpu.make_async_copy(gu_own, gbu_hbm, st_sem.at[0])
     store_u.start()
+    store_late = pltpu.make_async_copy(gu_own.at[pl.ds(width - LATE_ROWS, LATE_ROWS)], late_hbm, st_sem.at[3])
+    store_late.start()
     tile = acc[:, 0:128]
     for k in range(1, half // 128):
         tile = tile + acc[:, k * 128:(k + 1) * 128]
@@ -344,6 +350,8 @@
     store_u.wait()
     store_d.wait()
     store_early.wait()
+    store_late.wait()
+    send_pre.wait()
 
 
 def update_kernel(d_ref, lr_ref, mn_ref, norm_ref, gu, gd, wu, wd, mu, md, vu, vd, *rest):
@@ -357,14 +365,21 @@
         rest[7][...] = owd[...].astype(BF16)
 
 
-def fill_kernel(d_ref, lr_ref, mn_ref, norm_ref, gu, gd_early, gd_late, y_in, wu, wd, mu, md, vu, vd, *rest):
+def fill_kernel(d_ref, lr_ref, mn_ref, norm_ref, gu, gd_pre, gd_early, gd_rest, y_in, wu, wd, mu, md, vu, vd, *rest):
     owu, owd, omu, omd, ovu, ovd, y_out = rest[6:]
     clip = clip_of(norm_ref[...], mn_ref[0])
     rate = lr_ref[0]
-    gd = jnp.where(pl.program_id(0) < EARLY_ROWS // UPD_ROWS, gd_early[...], gd_late[...])
+    step = pl.program_id(0)
+    gd = jnp.where(step < PRE_ROWS // UPD_ROWS, gd_pre[...], jnp.where(step < (PRE_ROWS + EARLY_ROWS) // UPD_ROWS, gd_early[...], gd_rest[...]))
     owu[...], omu[...], ovu[...] = adamw_update(wu[...], mu[...], vu[...], clip * gu[...], rate)
     owd[...], omd[...], ovd[...] = adamw_update(wd[...], md[...], vd[...], clip * gd, rate)
     y_out[...] = y_in[...]
+
+
+def late_kernel(d_ref, lr_ref, mn_ref, norm_ref, gu, wu, mu, vu, *rest):
+    owu, omu, ovu = rest[3:]
+    clip = clip_of(norm_ref[...], mn_ref[0])
+    owu[...], omu[...], ovu[...] = adamw_update(wu[...], mu[...], vu[...], clip * gu[...], lr_ref[0])
 
 
 def fwd_kernel(dims, bu_hbm, bd_hbm, gbu_hbm, gbd_hbm, x_hbm,
@@ -395,16 +410,14 @@
         x_load.start()
     whole_barrier(n_model, n_data, n_stage)
 
-    send_wu = remote(wu_bf.at[:, own_ff], wu_bf.at[:, own_ff], ysend.at[0], yrecv.at[0], ypeer)
-    send_wd = remote(wd_bf.at[own_ff, :], wd_bf.at[own_ff, :], ysend.at[1], yrecv.at[1], ypeer)
-    send_gu = remote(gbu_hbm, gu_oth, ysend.at[2], yrecv.at[2], ypeer)
+    send_wu = remote(bu_hbm, wu_bf.at[:, own_ff], ysend.at[0], yrecv.at[0], ypeer)
+    send_wd = remote(bd_hbm, wd_bf.at[own_ff, :], ysend.at[1], yrecv.at[1], ypeer)
+    send_gu = remote(gbu_hbm.at[pl.ds(0, gu_oth.shape[0])], gu_oth, ysend.at[2], yrecv.at[2], ypeer)
     send_gd = remote(gbd_hbm.at[pl.ds(half - gd_oth.shape[0], gd_oth.shape[0])], gd_oth, ysend.at[3], yrecv.at[3], ypeer)
-    load_u.wait()
-    load_d.wait()
 
     shard = [
-        remote(wu_bf.at[:, own_ff], wu_z.at[:, own_ff], zsend.at[0], zrecv.at[0], zpeer),
-        remote(wd_bf.at[own_ff, :], wd_z.at[own_ff, :], zsend.at[1], zrecv.at[1], zpeer),
+        remote(bu_hbm, wu_z.at[:, own_ff], zsend.at[0], zrecv.at[0], zpeer),
+        remote(bd_hbm, wd_z.at[own_ff, :], zsend.at[1], zrecv.at[1], zpeer),
         remote(wu_bf.at[:, oth_ff], wu_z.at[:, oth_ff], zsend.at[2], zrecv.at[2], zpeer),
         remote(wd_bf.at[oth_ff, :], wd_z.at[oth_ff, :], zsend.at[3], zrecv.at[3], zpeer),
     ]
@@ -436,6 +449,8 @@
     @pl.when(p == 0)
     def _():
         x_load.wait()
+    load_u.wait()
+    load_d.wait()
     send_wu.wait_recv()
 
     @pl.when(p == last)
@@ -581,11 +596,11 @@
         nb = rows // BACK_ROWS
         hb = BACK_ROWS // 2
         sds = jax.ShapeDtypeStruct
-        gbar_u, gbar_d, early, norm_tile = pl.pallas_call(
+        gbar_u, gbar_d, early, late, pre_oth, norm_tile = pl.pallas_call(
             functools.partial(bwd_kernel, dims),
-            out_shape=(sds((width, half), F32), sds((half, width), F32), sds((EARLY_ROWS, width), F32), sds((8, 128), F32)),
+            out_shape=(sds((width, half), F32), sds((half, width), F32), sds((EARLY_ROWS, width), F32), sds((LATE_ROWS, half), F32), sds((PRE_ROWS, width), F32), sds((8, 128), F32)),
             in_specs=[any_spec] * 6,
-            out_specs=(any_spec, any_spec, any_spec, vmem_spec),
+            out_specs=(any_spec,) * 5 + (vmem_spec,),
             scratch_shapes=[
                 pltpu.VMEM((width, ff), F32), pltpu.VMEM((ff, width), F32),
                 pltpu.VMEM((width, ff), BF16), pltpu.VMEM((ff, width), BF16),
@@ -596,8 +611,8 @@
             ] + [pltpu.VMEM((width, half), F32), pltpu.VMEM((half, width), F32)] * 3 + [
                 pltpu.VMEM((nb, BACK_ROWS, width), F32), pltpu.VMEM((nb, hb, width), F32),
                 pltpu.VMEM((nb, hb, width), BF16), pltpu.VMEM((n_all, 8, 128), F32),
-                dma((8,)), dma((4,)), dma((4,)), dma((nb,)), dma((nb,)), dma((nb, 2)), dma((nb, 2)),
-                dma((n_all,)), dma((n_all,)), dma((3,)),
+                dma((8,)), dma((5,)), dma((5,)), dma((nb,)), dma((nb,)), dma((nb, 2)), dma((nb, 2)),
+                dma((n_all,)), dma((n_all,)), dma((4,)),
             ],
             compiler_params=pltpu.CompilerParams(collective_id=0, has_side_effects=True, vmem_limit_bytes=VMEM_LIMIT),
             name='backward',
@@ -633,7 +648,7 @@
         fb = FWD_ROWS // 2
         gu_oth, gd_oth, y_next = pl.pallas_call(
             functools.partial(fwd_kernel, dims),
-            out_shape=(sds((width, half), F32), sds((half - EARLY_ROWS, width), F32), sds((nc, FWD_ROWS, width), BF16)),
+            out_shape=(sds((width - LATE_ROWS, half), F32), sds((half - PRE_ROWS - EARLY_ROWS, width), F32), sds((nc, FWD_ROWS, width), BF16)),
             in_specs=[any_spec] * 5,
             out_specs=(any_spec, any_spec, any_spec),
             scratch_shapes=[pltpu.VMEM((width, ff), BF16), pltpu.VMEM((ff, width), BF16)] * 2 + [
@@ -648,22 +663,42 @@
         )(b_up, b_down, gbar_u, gbar_d, x_next.reshape(nc, FWD_ROWS, width))
 
         other = update_specs(lambda w: 1 - w)
-        ne = EARLY_ROWS // UPD_ROWS
+        gu_oth, late = lax.optimization_barrier((gu_oth, late))
+        late_oth = lax.ppermute(late, 'data', [(k, 1 - k) for k in range(n_data)])
+        npre, nearly, nlate = PRE_ROWS // UPD_ROWS, EARLY_ROWS // UPD_ROWS, LATE_ROWS // UPD_ROWS
         steps = width // UPD_ROWS
-        early_spec = pl.BlockSpec((UPD_ROWS, width), lambda i, w: (jnp.minimum(i, ne - 1), 0))
-        late_spec = pl.BlockSpec((UPD_ROWS, width), lambda i, w: (jnp.maximum(i - ne, 0), 0))
+        lastup = steps - nlate - 1
+
+        def rows_spec(start, count):
+            return pl.BlockSpec((UPD_ROWS, width), lambda i, w: (jnp.clip(i - start, 0, count - 1), 0))
         y_spec = pl.BlockSpec((nc // steps, FWD_ROWS, width), lambda i, w: (i, 0, 0))
+        up_oth = pl.BlockSpec((UPD_ROWS, half), lambda i, w: (jnp.minimum(i, lastup), 1 - w[0]))
+        down_oth = pl.BlockSpec((UPD_ROWS, width), lambda i, w: ((1 - w[0]) * blocks + i, 0))
+        other = [up_oth, down_oth]
         *filled, y_next = pl.pallas_call(
             fill_kernel,
             out_shape=state_shapes + (sds(y_next.shape, BF16),),
             grid_spec=pltpu.PrefetchScalarGridSpec(
                 num_scalar_prefetch=1, grid=(steps,),
-                in_specs=small + [plain_up, early_spec, late_spec, y_spec] + other * 3 + [any_spec] * 6,
+                in_specs=small + [rows_spec(0, lastup + 1), rows_spec(0, npre), rows_spec(npre, nearly), rows_spec(npre + nearly, blocks - npre - nearly), y_spec] + other * 3 + [any_spec] * 6,
                 out_specs=other * 3 + [y_spec]),
-            input_output_aliases={14 + k: k for k in range(6)},
+            input_output_aliases={15 + k: k for k in range(6)},
             compiler_params=pltpu.CompilerParams(dimension_semantics=('arbitrary',), vmem_limit_bytes=VMEM_LIMIT),
+            cost_estimate=pl.CostEstimate(flops=10**10, bytes_accessed=40 * 10**6, transcendentals=0),
             name='update_other',
-        )(which, learn_rate, max_norm, norm_tile, gu_oth, early_oth, gd_oth, y_next, *state, *fresh)
+        )(which, learn_rate, max_norm, norm_tile, gu_oth, pre_oth, early_oth, gd_oth, y_next, *state, *fresh)
+        up_late = pl.BlockSpec((UPD_ROWS, half), lambda i, w: (steps - nlate + i, 1 - w[0]))
+        filled[0], filled[2], filled[4] = pl.pallas_call(
+            late_kernel,
+            out_shape=(state_shapes[0],) * 3,
+            grid_spec=pltpu.PrefetchScalarGridSpec(
+                num_scalar_prefetch=1, grid=(nlate,),
+                in_specs=small + [plain_up] + [up_late] * 3 + [any_spec] * 3,
+                out_specs=[up_late] * 3),
+            input_output_aliases={8 + k: k for k in range(3)},
+            compiler_params=pltpu.CompilerParams(dimension_semantics=('arbitrary',), vmem_limit_bytes=VMEM_LIMIT),
+            name='update_late',
+        )(which, learn_rate, max_norm, norm_tile, late_oth, state[0], state[2], state[4], filled[0], filled[2], filled[4])
         return tuple(s[None] for s in filled) + (y_next.reshape(n_micro, rows, width),)
 
     return jax.shard_map(device_step, mesh=mesh, in_specs=in_specs, out_specs=out_specs, check_vma=False)

time: 309 us -> 315 us (1.019)
  Pallas kernels: 304 us -> 310 us
    pallas_call x1, Pallas kernels: 131 us -> 135 us  [device_step(): pl.pallas_call(functools.partial(bwd_kernel, dims), out_shape=(sds((width...]
  transfers between devices with their start and end apart: 1 -> 2, of which waited for: 0 -> 0; matrix products, arithmetic and copies ran while one was open for 0% -> 0% of each run, Pallas kernels for 51% -> 55%
where the time goes in v6:
time: 315 us
  Pallas kernels  310 us (98%)
    pallas_call x1, Pallas kernels, device_step(): pl.pallas_call(functools.partial(fwd_kernel, dims), out_shape=(sds((width...  142 us
    pallas_call x1, Pallas kernels, device_step(): pl.pallas_call(functools.partial(bwd_kernel, dims), out_shape=(sds((width...  135 us
    pallas_call x1, Pallas kernels, device_step(): pl.pallas_call(fill_kernel, out_shape=state_shapes + (sds(y_next.shape, B...  15.5 us
    pallas_call x1, Pallas kernels, device_step(): pl.pallas_call(update_kernel, out_shape=state_shapes + (sds((width, half)...  14.7 us
  transfers between devices with their start and end apart: 2, of which 0 were waited for; matrix products, arithmetic and copies ran while one was open for 0% of the time, Pallas kernels for 55%

profile of v6, /device:TPU:1, one launch (start us, length us, event | category | flops | bytes accessed | tf_op | source)
XLA Modules:
  0.0 314.6 jit_solution(4012046323180122515)
XLA Ops:
  0.6 135.2 %backward.1 = (f32[768,768]{1,0:T(8,128)}, f32[768,768]{1,0:T(8,128)}, f32[256,768]{1,0:T(8,128)}, f32[128,768]{1,0:T(8,128)}, f32[128,768]{1,0:T(8,128)}, /*index=5*/f32[8,128]{1,0:T(8,128)}) custom-call(f32[768,1536]{1,0:T(8,128)} %bitcast.18, f32[1536,768]{1,0:T(8,128)} %bitcast.22, bf16[512,768]{1,0:T(8,128)(2,1)} %bitcast.44, bf16[512,768]{1,0:T(8,128)(2,1)} %dy_hbm.1, ...), custom_call_target="tpu_custom_call" | custom-call | tf_op jit(solution)/shard_map/backward/pallas_call | solution.py:599
  135.8 1.2 collective-permute-start.1
  138.3 14.7 %update_own.1 = (f32[768,1536]{1,0:T(8,128)}, f32[1536,768]{1,0:T(8,128)}, f32[768,1536]{1,0:T(8,128)}, f32[1536,768]{1,0:T(8,128)}, f32[768,1536]{1,0:T(8,128)}...) custom-call(s32[1]{0:T(128)} %bitcast.d_ref, f32[1]{0:T(128)S(6)} %copy.38.lr_ref, ...), custom_call_target="tpu_custom_call" | custom-call | tf_op jit(solution)/shard_map/update_own/pallas_call | solution.py:635
  153.0 141.5 %forward.1 = (f32[640,768]{1,0:T(8,128)}, f32[384,768]{1,0:T(8,128)}, bf16[24,64,768]{2,1,0:T(8,128)(2,1)}) custom-call(bf16[768,768]{1,0:T(8,128)(2,1)} %get-tuple-element.39.bu_hbm, bf16[768,768]{1,0:T(8,128)(2,1)} %get-tuple-element.40.bd_hbm, f32[768,768]{1,0:T(8,128)} %get-tuple-element.37.gu.gbu_hbm, f32[768,768]{1,0:T(8,128)} %get-tuple-element.38.gd.gbd_hbm, ...), custom_call_target="tpu_custom_call" | custom-call | tf_op jit(solution)/shard_map/forward/pallas_call | solution.py:649
  294.6 0.9 collective-permute-start
  295.4 0.0 collective-permute-done.1.gd_early
  295.4 0.0 copy-start
  295.4 0.9 copy-done
  296.3 15.5 %update_other.1 = (f32[768,1536]{1,0:T(8,128)}, f32[1536,768]{1,0:T(8,128)}, f32[768,1536]{1,0:T(8,128)}, f32[1536,768]{1,0:T(8,128)}, f32[768,1536]{1,0:T(8,128...) custom-call(s32[1]{0:T(128)} %bitcast.d_ref, ...), custom_call_target="tpu_custom_call", output_to_operand_aliasing={{0}: (15, {}), {1}: (16, {}), {2}: (17, {}), {3}: (18, {}),... | custom-call | flops 10000000000 | bytes 40000000 | tf_op jit(solution)/shard_map/update_other/pallas_call | solution.py:678
  311.8 0.0 collective-permute-done.gu
  311.8 2.8 update_late.1
Async XLA Ops:
  135.8 159.6 %collective-permute-start.1 = (f32[256,768]{1,0:T(8,128)}, f32[256,768]{1,0:T(8,128)S(1)}, u32[]{:S(2)}, u32[]{:S(2)}) collective-permute-start(f32[256,768]{1,0:T(8,128)} %get-tuple-element.46), channel_id=1, source_target_pairs={{0,4},{4,0},{1,5},{5,1},{2,6},{6,2},{3,7},{7,3},{8,12},{12,8},{9,1... | collective-permute-start | bytes 2359304 | tf_op jit(solution)/shard_map/ppermute | solution.py:621
  294.6 17.3 %collective-permute-start = (f32[128,768]{1,0:T(8,128)}, f32[128,768]{1,0:T(8,128)}, u32[]{:S(2)}, u32[]{:S(2)}) collective-permute-start(f32[128,768]{1,0:T(8,128)} %get-tuple-element.43), channel_id=1, source_target_pairs={{0,4},{4,0},{1,5},{5,1},{2,6},{6,2},{3,7},{7,3},{8,12},{12,8},{9,1... | collective-permute-start | bytes 1179656 | tf_op jit(solution)/shard_map/ppermute | solution.py:667
  295.4 0.9 copy-start

commit v7 on v6

--- a/solution.py
+++ b/solution.py
@@ -24,12 +24,12 @@
 BF16 = jnp.bfloat16
 MESH = pl.DeviceIdType.MESH
 BACK_ROWS = 128
-FWD_ROWS = 64
+FWD_ROWS = 96
 UPD_ROWS = 128
-PRE_ROWS = 128
-EARLY_ROWS = 256
+PRE_ROWS = 64
+EARLY_ROWS = 192
 LATE_ROWS = 128
-TURN_STEP = 8
+TURN_STEP = 5
 VMEM_LIMIT = 66_000_000
 
 
@@ -365,12 +365,12 @@
         rest[7][...] = owd[...].astype(BF16)
 
 
-def fill_kernel(d_ref, lr_ref, mn_ref, norm_ref, gu, gd_pre, gd_early, gd_rest, y_in, wu, wd, mu, md, vu, vd, *rest):
+def fill_kernel(d_ref, lr_ref, mn_ref, norm_ref, gu, gd_early, gd_rest, y_in, wu, wd, mu, md, vu, vd, *rest):
     owu, owd, omu, omd, ovu, ovd, y_out = rest[6:]
     clip = clip_of(norm_ref[...], mn_ref[0])
     rate = lr_ref[0]
     step = pl.program_id(0)
-    gd = jnp.where(step < PRE_ROWS // UPD_ROWS, gd_pre[...], jnp.where(step < (PRE_ROWS + EARLY_ROWS) // UPD_ROWS, gd_early[...], gd_rest[...]))
+    gd = jnp.where(step < (PRE_ROWS + EARLY_ROWS) // UPD_ROWS, gd_early[...], gd_rest[...])
     owu[...], omu[...], ovu[...] = adamw_update(wu[...], mu[...], vu[...], clip * gu[...], rate)
     owd[...], omd[...], ovd[...] = adamw_update(wd[...], md[...], vd[...], clip * gd, rate)
     y_out[...] = y_in[...]
@@ -665,13 +665,15 @@
         other = update_specs(lambda w: 1 - w)
         gu_oth, late = lax.optimization_barrier((gu_oth, late))
         late_oth = lax.ppermute(late, 'data', [(k, 1 - k) for k in range(n_data)])
-        npre, nearly, nlate = PRE_ROWS // UPD_ROWS, EARLY_ROWS // UPD_ROWS, LATE_ROWS // UPD_ROWS
+        early_oth = jnp.concatenate([pre_oth, early_oth])
+        y_next = y_next.reshape(n_micro * rows, width)
+        nearly, nlate = (PRE_ROWS + EARLY_ROWS) // UPD_ROWS, LATE_ROWS // UPD_ROWS
         steps = width // UPD_ROWS
         lastup = steps - nlate - 1
 
         def rows_spec(start, count):
             return pl.BlockSpec((UPD_ROWS, width), lambda i, w: (jnp.clip(i - start, 0, count - 1), 0))
-        y_spec = pl.BlockSpec((nc // steps, FWD_ROWS, width), lambda i, w: (i, 0, 0))
+        y_spec = pl.BlockSpec((n_micro * rows // steps, width), lambda i, w: (i, 0))
         up_oth = pl.BlockSpec((UPD_ROWS, half), lambda i, w: (jnp.minimum(i, lastup), 1 - w[0]))
         down_oth = pl.BlockSpec((UPD_ROWS, width), lambda i, w: ((1 - w[0]) * blocks + i, 0))
         other = [up_oth, down_oth]
@@ -680,13 +682,13 @@
             out_shape=state_shapes + (sds(y_next.shape, BF16),),
             grid_spec=pltpu.PrefetchScalarGridSpec(
                 num_scalar_prefetch=1, grid=(steps,),
-                in_specs=small + [rows_spec(0, lastup + 1), rows_spec(0, npre), rows_spec(npre, nearly), rows_spec(npre + nearly, blocks - npre - nearly), y_spec] + other * 3 + [any_spec] * 6,
+                in_specs=small + [rows_spec(0, lastup + 1), rows_spec(0, nearly), rows_spec(nearly, blocks - nearly), y_spec] + other * 3 + [any_spec] * 6,
                 out_specs=other * 3 + [y_spec]),
-            input_output_aliases={15 + k: k for k in range(6)},
+            input_output_aliases={14 + k: k for k in range(6)},
             compiler_params=pltpu.CompilerParams(dimension_semantics=('arbitrary',), vmem_limit_bytes=VMEM_LIMIT),
             cost_estimate=pl.CostEstimate(flops=10**10, bytes_accessed=40 * 10**6, transcendentals=0),
             name='update_other',
-        )(which, learn_rate, max_norm, norm_tile, gu_oth, pre_oth, early_oth, gd_oth, y_next, *state, *fresh)
+        )(which, learn_rate, max_norm, norm_tile, gu_oth, early_oth, gd_oth, y_next, *state, *fresh)
         up_late = pl.BlockSpec((UPD_ROWS, half), lambda i, w: (steps - nlate + i, 1 - w[0]))
         filled[0], filled[2], filled[4] = pl.pallas_call(
             late_kernel,

time: 315 us -> 307 us (0.975)
  Pallas kernels: 310 us -> 302 us
    pallas_call x1, Pallas kernels: 142 us -> 137 us  [device_step(): pl.pallas_call(functools.partial(fwd_kernel, dims), out_shape=(sds((width...]
    pallas_call x1, Pallas kernels: 135 us -> 132 us  [device_step(): pl.pallas_call(functools.partial(bwd_kernel, dims), out_shape=(sds((width...]
  transfers between devices with their start and end apart: 2 -> 2, of which waited for: 0 -> 0; matrix products, arithmetic and copies ran while one was open for 0% -> 1% of each run, Pallas kernels for 55% -> 55%
where the time goes in v7:
time: 307 us
  Pallas kernels  302 us (98%)
    pallas_call x1, Pallas kernels, device_step(): pl.pallas_call(functools.partial(fwd_kernel, dims), out_shape=(sds((width...  137 us
    pallas_call x1, Pallas kernels, device_step(): pl.pallas_call(functools.partial(bwd_kernel, dims), out_shape=(sds((width...  132 us
    pallas_call x1, Pallas kernels, device_step(): pl.pallas_call(fill_kernel, out_shape=state_shapes + (sds(y_next.shape, B...  15.7 us
    pallas_call x1, Pallas kernels, device_step(): pl.pallas_call(update_kernel, out_shape=state_shapes + (sds((width, half)...  14.7 us
  transfers between devices with their start and end apart: 2, of which 0 were waited for; matrix products, arithmetic and copies ran while one was open for 1% of the time, Pallas kernels for 55%

profile of v7, /device:TPU:1, one launch (start us, length us, event | category | flops | bytes accessed | tf_op | source)
XLA Modules:
  0.0 306.7 jit_solution(8892170495514037704)
XLA Ops:
  0.6 131.7 %backward.1 = (f32[768,768]{1,0:T(8,128)}, f32[768,768]{1,0:T(8,128)}, f32[192,768]{1,0:T(8,128)}, f32[128,768]{1,0:T(8,128)}, f32[64,768]{1,0:T(8,128)}, /*index=5*/f32[8,128]{1,0:T(8,128)}) custom-call(f32[768,1536]{1,0:T(8,128)} %bitcast.19, f32[1536,768]{1,0:T(8,128)} %bitcast.23, bf16[512,768]{1,0:T(8,128)(2,1)} %bitcast.46, bf16[512,768]{1,0:T(8,128)(2,1)} %dy_hbm.1, ...), custom_call_target="tpu_custom_call" | custom-call | tf_op jit(solution)/shard_map/backward/pallas_call | solution.py:599
  132.4 0.4 collective-permute-start.1
  134.1 14.7 %update_own.1 = (f32[768,1536]{1,0:T(8,128)}, f32[1536,768]{1,0:T(8,128)}, f32[768,1536]{1,0:T(8,128)}, f32[1536,768]{1,0:T(8,128)}, f32[768,1536]{1,0:T(8,128)}...) custom-call(s32[1]{0:T(128)} %bitcast.d_ref, f32[1]{0:T(128)S(6)} %copy.38.lr_ref, ...), custom_call_target="tpu_custom_call" | custom-call | tf_op jit(solution)/shard_map/update_own/pallas_call | solution.py:635
  148.8 136.8 %forward.1 = (f32[640,768]{1,0:T(8,128)}, f32[512,768]{1,0:T(8,128)}, bf16[16,96,768]{2,1,0:T(8,128)(2,1)}) custom-call(bf16[768,768]{1,0:T(8,128)(2,1)} %get-tuple-element.39.bu_hbm, bf16[768,768]{1,0:T(8,128)(2,1)} %get-tuple-element.40.bd_hbm, f32[768,768]{1,0:T(8,128)} %get-tuple-element.37.gu.gbu_hbm, f32[768,768]{1,0:T(8,128)} %get-tuple-element.38.gd.gbd_hbm, ...), custom_call_target="tpu_custom_call" | custom-call | tf_op jit(solution)/shard_map/forward/pallas_call | solution.py:649
  285.6 0.0 collective-permute-start
  285.6 0.0 collective-permute-done.1
  285.6 1.9 pad_maximum_fusion.gd_early
  287.5 15.7 %update_other.1 = (f32[768,1536]{1,0:T(8,128)}, f32[1536,768]{1,0:T(8,128)}, f32[768,1536]{1,0:T(8,128)}, f32[1536,768]{1,0:T(8,128)}, f32[768,1536]{1,0:T(8,128...) custom-call(s32[1]{0:T(128)} %bitcast.d_ref, ...), custom_call_target="tpu_custom_call", output_to_operand_aliasing={{0}: (14, {}), {1}: (15, {}), {2}: (16, {}), {3}: (17, {}),... | custom-call | flops 10000000000 | bytes 40000000 | tf_op jit(solution)/shard_map/update_other/pallas_call | solution.py:680
  303.2 0.0 collective-permute-done.gu
  303.2 0.0 copy-start
  303.2 0.7 copy-done
  304.0 2.8 update_late.1
Async XLA Ops:
  132.4 153.3 %collective-permute-start.1 = (f32[192,768]{1,0:T(8,128)}, f32[192,768]{1,0:T(8,128)S(1)}, u32[]{:S(2)}, u32[]{:S(2)}) collective-permute-start(f32[192,768]{1,0:T(8,128)} %get-tuple-element.46), channel_id=1, source_target_pairs={{0,4},{4,0},{1,5},{5,1},{2,6},{6,2},{3,7},{7,3},{8,12},{12,8},{9,1... | collective-permute-start | bytes 1769480 | tf_op jit(solution)/shard_map/ppermute | solution.py:621
  285.6 17.6 %collective-permute-start = (f32[128,768]{1,0:T(8,128)}, f32[128,768]{1,0:T(8,128)S(1)}, u32[]{:S(2)}, u32[]{:S(2)}) collective-permute-start(f32[128,768]{1,0:T(8,128)} %get-tuple-element.43), channel_id=1, source_target_pairs={{0,4},{4,0},{1,5},{5,1},{2,6},{6,2},{3,7},{7,3},{8,12},{12,8},{9,1... | collective-permute-start | bytes 1179656 | tf_op jit(solution)/shard_map/ppermute | solution.py:667
  303.2 0.7 copy-start

commit v8 on v7

--- a/solution.py
+++ b/solution.py
@@ -26,10 +26,9 @@
 BACK_ROWS = 128
 FWD_ROWS = 96
 UPD_ROWS = 128
-PRE_ROWS = 64
-EARLY_ROWS = 192
-LATE_ROWS = 128
-TURN_STEP = 5
+PRE_ROWS = 128
+LATE_ROWS = 256
+TURN_STEP = 8
 VMEM_LIMIT = 66_000_000
 
 
@@ -78,10 +77,10 @@
     return pltpu.make_async_remote_copy(src_ref=src, dst_ref=dst, send_sem=send_sem, recv_sem=recv_sem, device_id=device, device_id_type=MESH)
 
 
-def bwd_kernel(dims, wu_hbm, wd_hbm, acts_hbm, dy_hbm, gu_hbm, gd_hbm,
-               gbu_hbm, gbd_hbm, early_hbm, late_hbm, pre_oth, norm_out,
+def bwd_kernel(dims, lr_ref, mn_ref, wu_hbm, wd_hbm, mu_hbm, md_hbm, vu_hbm, vd_hbm, acts_hbm, dy_hbm, gu_hbm, gd_hbm,
+               gbu_hbm, gbd_hbm, late_hbm, pre_oth, own_hbm, norm_out,
                wu32, wd32, wu_bf, wd_bf, aa, gg, hid_o, dz_o, slope, slope_o, dz_own, h_own,
-               gu_own, gd_own, gu_oth, gd_oth, gu_rcv, gd_rcv, part, part_rcv, fin, norm_buf,
+               gu_own, gd_own, gu_oth, gd_oth, gu_rcv, gd_rcv, mu32, md32, vu32, vd32, new_bf, part, part_rcv, fin, norm_buf,
                ld_sem, ysend, yrecv, psend, precv, fsend, frecv, nsend, nrecv, st_sem):
     n_model, n_data, n_stage = dims
     z, d, p = lax.axis_index('model'), lax.axis_index('data'), lax.axis_index('stage')
@@ -124,6 +123,14 @@
         gd_load.start()
         gu_load.start()
 
+    moments = [
+        pltpu.make_async_copy(mu_hbm.at[:, own_ff], mu32, ld_sem.at[8]),
+        pltpu.make_async_copy(md_hbm.at[own_ff, :], md32, ld_sem.at[9]),
+        pltpu.make_async_copy(vu_hbm.at[:, own_ff], vu32, ld_sem.at[10]),
+        pltpu.make_async_copy(vd_hbm.at[own_ff, :], vd32, ld_sem.at[11]),
+    ]
+    for copy in moments:
+        copy.start()
     whole_barrier(n_model, n_data, n_stage)
     send_acts = remote(acts_hbm, aa.at[theirs], ysend.at[0], yrecv.at[0], ypeer)
     raw_gu = remote(gu_hbm.at[:, oth_ff], gu_rcv, ysend.at[1], yrecv.at[1], ypeer)
@@ -298,8 +305,6 @@
     acc = combine_down(acc)
     store_d = pltpu.make_async_copy(gd_own, gbd_hbm, st_sem.at[1])
     store_d.start()
-    store_early = pltpu.make_async_copy(gd_own.at[pl.ds(PRE_ROWS, EARLY_ROWS)], early_hbm, st_sem.at[2])
-    store_early.start()
     send_pre = remote(gd_own.at[pl.ds(0, PRE_ROWS)], pre_oth, ysend.at[4], yrecv.at[4], ypeer)
     send_pre.start()
     acc = combine_up(acc)
@@ -328,6 +333,28 @@
         total = total + norm_buf[k]
     norm_out[...] = total
 
+    for copy in moments:
+        copy.wait()
+    clip = clip_of(total, mn_ref[0])
+    rate = lr_ref[0]
+
+    def new_up(i, carry):
+        at = pl.ds(pl.multiple_of(i * 32, 32), 32)
+        new_bf[at, :] = adamw_update(wu32[at, own_ff], mu32[at, :], vu32[at, :], clip * gu_own[at, :], rate)[0].astype(BF16)
+        return carry
+    lax.fori_loop(0, width // 32, new_up, 0)
+    store_bu = pltpu.make_async_copy(new_bf.at[pl.ds(0, width)], own_hbm.at[pl.ds(0, width)], st_sem.at[2])
+    store_bu.start()
+
+    def new_down(i, carry):
+        at = pl.ds(pl.multiple_of(i * 32, 32), 32)
+        weight = wd32[pl.ds(pl.multiple_of(d * half + i * 32, 32), 32), :]
+        new_bf[pl.ds(pl.multiple_of(width + i * 32, 32), 32), :] = adamw_update(weight, md32[at, :], vd32[at, :], clip * gd_own[at, :], rate)[0].astype(BF16)
+        return carry
+    lax.fori_loop(0, half // 32, new_down, 0)
+    store_bd = pltpu.make_async_copy(new_bf.at[pl.ds(width, half)], own_hbm.at[pl.ds(width, half)], st_sem.at[4])
+    store_bd.start()
+
     for k in range(1, n_all):
         norm_copy(k).wait_send()
 
@@ -349,9 +376,10 @@
                 fin_copy(c, zi).wait_send()
     store_u.wait()
     store_d.wait()
-    store_early.wait()
     store_late.wait()
     send_pre.wait()
+    store_bu.wait()
+    store_bd.wait()
 
 
 def update_kernel(d_ref, lr_ref, mn_ref, norm_ref, gu, gd, wu, wd, mu, md, vu, vd, *rest):
@@ -360,17 +388,14 @@
     rate = lr_ref[0]
     owu[...], omu[...], ovu[...] = adamw_update(wu[...], mu[...], vu[...], clip * gu[...], rate)
     owd[...], omd[...], ovd[...] = adamw_update(wd[...], md[...], vd[...], clip * gd[...], rate)
-    if len(rest) == 8:
-        rest[6][...] = owu[...].astype(BF16)
-        rest[7][...] = owd[...].astype(BF16)
-
-
-def fill_kernel(d_ref, lr_ref, mn_ref, norm_ref, gu, gd_early, gd_rest, y_in, wu, wd, mu, md, vu, vd, *rest):
+
+
+def fill_kernel(d_ref, lr_ref, mn_ref, norm_ref, gu, gd_pre, gd_rest, y_in, wu, wd, mu, md, vu, vd, *rest):
     owu, owd, omu, omd, ovu, ovd, y_out = rest[6:]
     clip = clip_of(norm_ref[...], mn_ref[0])
     rate = lr_ref[0]
     step = pl.program_id(0)
-    gd = jnp.where(step < (PRE_ROWS + EARLY_ROWS) // UPD_ROWS, gd_early[...], gd_rest[...])
+    gd = jnp.where(step < PRE_ROWS // UPD_ROWS, gd_pre[...], gd_rest[...])
     owu[...], omu[...], ovu[...] = adamw_update(wu[...], mu[...], vu[...], clip * gu[...], rate)
     owd[...], omd[...], ovd[...] = adamw_update(wd[...], md[...], vd[...], clip * gd, rate)
     y_out[...] = y_in[...]
@@ -382,7 +407,7 @@
     owu[...], omu[...], ovu[...] = adamw_update(wu[...], mu[...], vu[...], clip * gu[...], lr_ref[0])
 
 
-def fwd_kernel(dims, bu_hbm, bd_hbm, gbu_hbm, gbd_hbm, x_hbm,
+def fwd_kernel(dims, own_hbm, first_hbm, shard_hbm, gbu_hbm, gbd_hbm, x_hbm, after_hbm,
                gu_oth, gd_oth, y_hbm,
                wu_bf, wd_bf, wu_z, wd_z, a_buf, y_buf, part, part_rcv, fin,
                ld_sem, ysend, yrecv, zsend, zrecv, psend, precv, fsend, frecv, agsend, agrecv, outsend, outrecv, turn):
@@ -399,10 +424,31 @@
     first = (p == 0) | (p == last)
     partner = (z, d, p + 1 - 2 * lax.rem(p, 2))
 
-    load_u = pltpu.make_async_copy(bu_hbm, wu_bf.at[:, own_ff], ld_sem.at[0])
-    load_d = pltpu.make_async_copy(bd_hbm, wd_bf.at[own_ff, :], ld_sem.at[1])
-    load_u.start()
-    load_d.start()
+    up_rows, down_rows = pl.ds(0, width), pl.ds(width, half)
+    loads = [
+        pltpu.make_async_copy(own_hbm.at[up_rows], wu_bf.at[:, own_ff], ld_sem.at[0]),
+        pltpu.make_async_copy(own_hbm.at[down_rows], wd_bf.at[own_ff, :], ld_sem.at[1]),
+    ]
+    first_loads = [
+        pltpu.make_async_copy(first_hbm.at[up_rows], wu_bf.at[:, oth_ff], ld_sem.at[3]),
+        pltpu.make_async_copy(first_hbm.at[down_rows], wd_bf.at[oth_ff, :], ld_sem.at[4]),
+    ]
+    shard_loads = [
+        pltpu.make_async_copy(shard_hbm.at[up_rows], wu_z.at[:, own_ff], ld_sem.at[5]),
+        pltpu.make_async_copy(shard_hbm.at[down_rows], wd_z.at[own_ff, :], ld_sem.at[6]),
+    ]
+    for copy in loads:
+        copy.start()
+
+    @pl.when(first)
+    def _():
+        for copy in first_loads:
+            copy.start()
+
+    @pl.when(p == last)
+    def _():
+        for copy in shard_loads:
+            copy.start()
     x_load = pltpu.make_async_copy(x_hbm, a_buf, ld_sem.at[2])
 
     @pl.when(p == 0)
@@ -410,57 +456,46 @@
         x_load.start()
     whole_barrier(n_model, n_data, n_stage)
 
-    send_wu = remote(bu_hbm, wu_bf.at[:, own_ff], ysend.at[0], yrecv.at[0], ypeer)
-    send_wd = remote(bd_hbm, wd_bf.at[own_ff, :], ysend.at[1], yrecv.at[1], ypeer)
+    send_wu = remote(own_hbm.at[up_rows], wu_bf.at[:, own_ff], ysend.at[0], yrecv.at[0], ypeer)
+    send_wd = remote(own_hbm.at[down_rows], wd_bf.at[own_ff, :], ysend.at[1], yrecv.at[1], ypeer)
     send_gu = remote(gbu_hbm.at[pl.ds(0, gu_oth.shape[0])], gu_oth, ysend.at[2], yrecv.at[2], ypeer)
     send_gd = remote(gbd_hbm.at[pl.ds(half - gd_oth.shape[0], gd_oth.shape[0])], gd_oth, ysend.at[3], yrecv.at[3], ypeer)
 
     shard = [
-        remote(bu_hbm, wu_z.at[:, own_ff], zsend.at[0], zrecv.at[0], zpeer),
-        remote(bd_hbm, wd_z.at[own_ff, :], zsend.at[1], zrecv.at[1], zpeer),
-        remote(wu_bf.at[:, oth_ff], wu_z.at[:, oth_ff], zsend.at[2], zrecv.at[2], zpeer),
-        remote(wd_bf.at[oth_ff, :], wd_z.at[oth_ff, :], zsend.at[3], zrecv.at[3], zpeer),
+        remote(first_hbm.at[up_rows], wu_z.at[:, oth_ff], zsend.at[0], zrecv.at[0], zpeer),
+        remote(first_hbm.at[down_rows], wd_z.at[oth_ff, :], zsend.at[1], zrecv.at[1], zpeer),
     ]
 
     @pl.when(p == last)
     def _():
-        shard[0].start()
-        shard[1].start()
-
-    @pl.when(first)
-    def _():
-        send_wu.start()
-        send_wd.start()
-        send_wu.wait_send()
-        send_wd.wait_send()
-        pl.semaphore_signal(turn, inc=1, device_id=partner, device_id_type=MESH)
+        for copy in shard:
+            copy.start()
 
     @pl.when(jnp.logical_not(first))
     def _():
-        pl.semaphore_wait(turn, 1)
         send_wu.start()
         send_wd.start()
         send_gu.start()
         send_gd.start()
-        send_wu.wait_send()
-        send_wd.wait_send()
+        send_wu.wait()
+        send_wd.wait()
         pl.semaphore_signal(turn, inc=1, device_id=partner, device_id_type=MESH)
+    for copy in loads:
+        copy.wait()
+
+    @pl.when(first)
+    def _():
+        for copy in first_loads:
+            copy.wait()
 
     @pl.when(p == 0)
     def _():
         x_load.wait()
-    load_u.wait()
-    load_d.wait()
-    send_wu.wait_recv()
 
     @pl.when(p == last)
     def _():
-        shard[2].start()
-    send_wd.wait_recv()
-
-    @pl.when(p == last)
-    def _():
-        shard[3].start()
+        for copy in shard_loads:
+            copy.wait()
         for copy in shard:
             copy.wait_recv()
 
@@ -596,10 +631,10 @@
         nb = rows // BACK_ROWS
         hb = BACK_ROWS // 2
         sds = jax.ShapeDtypeStruct
-        gbar_u, gbar_d, early, late, pre_oth, norm_tile = pl.pallas_call(
+        gbar_u, gbar_d, late, pre_oth, b_own, norm_tile = pl.pallas_call(
             functools.partial(bwd_kernel, dims),
-            out_shape=(sds((width, half), F32), sds((half, width), F32), sds((EARLY_ROWS, width), F32), sds((LATE_ROWS, half), F32), sds((PRE_ROWS, width), F32), sds((8, 128), F32)),
-            in_specs=[any_spec] * 6,
+            out_shape=(sds((width, half), F32), sds((half, width), F32), sds((LATE_ROWS, half), F32), sds((PRE_ROWS, width), F32), sds((width + half, width), BF16), sds((8, 128), F32)),
+            in_specs=[smem_spec] * 2 + [any_spec] * 10,
             out_specs=(any_spec,) * 5 + (vmem_spec,),
             scratch_shapes=[
                 pltpu.VMEM((width, ff), F32), pltpu.VMEM((ff, width), F32),
@@ -608,17 +643,20 @@
                 pltpu.VMEM((rows, half), BF16), pltpu.VMEM((rows, half), BF16),
                 pltpu.VMEM((rows, ff), F32), pltpu.VMEM((rows, half), F32),
                 pltpu.VMEM((rows, ff), BF16), pltpu.VMEM((rows, ff), BF16),
-            ] + [pltpu.VMEM((width, half), F32), pltpu.VMEM((half, width), F32)] * 3 + [
+            ] + [pltpu.VMEM((width, half), F32), pltpu.VMEM((half, width), F32)] * 5 + [
+                pltpu.VMEM((width + half, width), BF16),
                 pltpu.VMEM((nb, BACK_ROWS, width), F32), pltpu.VMEM((nb, hb, width), F32),
                 pltpu.VMEM((nb, hb, width), BF16), pltpu.VMEM((n_all, 8, 128), F32),
-                dma((8,)), dma((5,)), dma((5,)), dma((nb,)), dma((nb,)), dma((nb, 2)), dma((nb, 2)),
-                dma((n_all,)), dma((n_all,)), dma((4,)),
+                dma((12,)), dma((5,)), dma((5,)), dma((nb,)), dma((nb,)), dma((nb, 2)), dma((nb, 2)),
+                dma((n_all,)), dma((n_all,)), dma((5,)),
             ],
             compiler_params=pltpu.CompilerParams(collective_id=0, has_side_effects=True, vmem_limit_bytes=VMEM_LIMIT),
             name='backward',
-        )(w_up[0], w_down[0], acts_last[0], grad_out, g_up[0, 0], g_down[0, 0])
-
-        early_oth = lax.ppermute(early, 'data', [(k, 1 - k) for k in range(n_data)])
+        )(learn_rate, max_norm, w_up[0], w_down[0], m_up[0], m_down[0], v_up[0], v_down[0], acts_last[0], grad_out, g_up[0, 0], g_down[0, 0])
+
+        ends = (0, n_stage - 1)
+        b_first = lax.ppermute(b_own, ('data', 'stage'), [(k * n_stage + q, (1 - k) * n_stage + q) for k in range(n_data) for q in ends])
+        b_shard = lax.ppermute(b_own, ('model', 'stage'), [(k * n_stage + ends[1], (1 - k) * n_stage + ends[1]) for k in range(n_model)])
         blocks = half // UPD_ROWS
         state = (w_up[0], w_down[0], m_up[0], m_down[0], v_up[0], v_down[0])
         state_shapes = tuple(sds(s.shape, F32) for s in state)
@@ -632,14 +670,15 @@
         plain_down = pl.BlockSpec((UPD_ROWS, width), lambda i, w: (i, 0))
         small = [smem_spec, smem_spec, pl.BlockSpec((8, 128), lambda i, w: (0, 0))]
         own = update_specs(lambda w: w)
-        *fresh, b_up, b_down = pl.pallas_call(
+        fresh = pl.pallas_call(
             update_kernel,
-            out_shape=state_shapes + (sds((width, half), BF16), sds((half, width), BF16)),
+            out_shape=state_shapes,
             grid_spec=pltpu.PrefetchScalarGridSpec(
                 num_scalar_prefetch=1, grid=(width // UPD_ROWS,),
                 in_specs=small + [plain_up, plain_down] + own * 3,
-                out_specs=own * 3 + [plain_up, plain_down]),
+                out_specs=own * 3),
             compiler_params=pltpu.CompilerParams(dimension_semantics=('arbitrary',), vmem_limit_bytes=VMEM_LIMIT),
+            cost_estimate=pl.CostEstimate(flops=10**10, bytes_accessed=34 * 10**6, transcendentals=0),
             name='update_own',
         )(which, learn_rate, max_norm, norm_tile, gbar_u, gbar_d, *state)
 
@@ -648,26 +687,25 @@
         fb = FWD_ROWS // 2
         gu_oth, gd_oth, y_next = pl.pallas_call(
             functools.partial(fwd_kernel, dims),
-            out_shape=(sds((width - LATE_ROWS, half), F32), sds((half - PRE_ROWS - EARLY_ROWS, width), F32), sds((nc, FWD_ROWS, width), BF16)),
-            in_specs=[any_spec] * 5,
+            out_shape=(sds((width - LATE_ROWS, half), F32), sds((half - PRE_ROWS, width), F32), sds((nc, FWD_ROWS, width), BF16)),
+            in_specs=[any_spec] * 7,
             out_specs=(any_spec, any_spec, any_spec),
             scratch_shapes=[pltpu.VMEM((width, ff), BF16), pltpu.VMEM((ff, width), BF16)] * 2 + [
                 pltpu.VMEM((nc, FWD_ROWS, width), BF16), pltpu.VMEM((nc, FWD_ROWS, width), BF16),
                 pltpu.VMEM((nc, FWD_ROWS, width), F32), pltpu.VMEM((nc, fb, width), F32),
                 pltpu.VMEM((nc, fb, width), BF16),
-                dma((3,)), dma((4,)), dma((4,)), dma((4,)), dma((4,)), dma((nc,)), dma((nc,)), dma((nc, 2)), dma((nc, 2)),
+                dma((7,)), dma((4,)), dma((4,)), dma((2,)), dma((2,)), dma((nc,)), dma((nc,)), dma((nc, 2)), dma((nc, 2)),
                 dma((nc,)), dma((nc,)), dma((nc, n_stage)), dma((nc,)), pltpu.SemaphoreType.REGULAR,
             ],
             compiler_params=pltpu.CompilerParams(collective_id=1, has_side_effects=True, vmem_limit_bytes=VMEM_LIMIT),
             name='forward',
-        )(b_up, b_down, gbar_u, gbar_d, x_next.reshape(nc, FWD_ROWS, width))
+        )(b_own, b_first, b_shard, gbar_u, gbar_d, x_next.reshape(nc, FWD_ROWS, width), fresh[0])
 
         other = update_specs(lambda w: 1 - w)
         gu_oth, late = lax.optimization_barrier((gu_oth, late))
         late_oth = lax.ppermute(late, 'data', [(k, 1 - k) for k in range(n_data)])
-        early_oth = jnp.concatenate([pre_oth, early_oth])
         y_next = y_next.reshape(n_micro * rows, width)
-        nearly, nlate = (PRE_ROWS + EARLY_ROWS) // UPD_ROWS, LATE_ROWS // UPD_ROWS
+        npre, nlate = PRE_ROWS // UPD_ROWS, LATE_ROWS // UPD_ROWS
         steps = width // UPD_ROWS
         lastup = steps - nlate - 1
 
@@ -682,13 +720,13 @@
             out_shape=state_shapes + (sds(y_next.shape, BF16),),
             grid_spec=pltpu.PrefetchScalarGridSpec(
                 num_scalar_prefetch=1, grid=(steps,),
-                in_specs=small + [rows_spec(0, lastup + 1), rows_spec(0, nearly), rows_spec(nearly, blocks - nearly), y_spec] + other * 3 + [any_spec] * 6,
+                in_specs=small + [rows_spec(0, lastup + 1), rows_spec(0, npre), rows_spec(npre, blocks - npre), y_spec] + other * 3 + [any_spec] * 6,
                 out_specs=other * 3 + [y_spec]),
             input_output_aliases={14 + k: k for k in range(6)},
             compiler_params=pltpu.CompilerParams(dimension_semantics=('arbitrary',), vmem_limit_bytes=VMEM_LIMIT),
             cost_estimate=pl.CostEstimate(flops=10**10, bytes_accessed=40 * 10**6, transcendentals=0),
             name='update_other',
-        )(which, learn_rate, max_norm, norm_tile, gu_oth, early_oth, gd_oth, y_next, *state, *fresh)
+        )(which, learn_rate, max_norm, norm_tile, gu_oth, pre_oth, gd_oth, y_next, *state, *fresh)
         up_late = pl.BlockSpec((UPD_ROWS, half), lambda i, w: (steps - nlate + i, 1 - w[0]))
         filled[0], filled[2], filled[4] = pl.pallas_call(
             late_kernel,

time: 307 us -> 319 us (1.039)
  the two profiles are of different devices: /device:TPU:1 before, /device:TPU:3 now
where the time goes in v8:
time: 319 us; the launch traced here: 318 us
  Pallas kernels  296 us (93%)
  waiting for transfers between devices  12.3 us (4%)
  starting transfers between devices  7.42 us (2%)
    pallas_call x1, Pallas kernels, device_step(): pl.pallas_call(functools.partial(bwd_kernel, dims), out_shape=(sds((width...  139 us
    pallas_call x1, Pallas kernels, device_step(): pl.pallas_call(functools.partial(fwd_kernel, dims), out_shape=(sds((width...  125 us
    pallas_call x1, Pallas kernels, device_step(): pl.pallas_call(fill_kernel, out_shape=state_shapes + (sds(y_next.shape, B...  14.4 us
    pallas_call x1, Pallas kernels, device_step(): pl.pallas_call(update_kernel, out_shape=state_shapes, grid_spec=pltpu.Pre...  14.1 us
    ppermute x1, waiting for transfers between devices, device_step(): lax.ppermute(b_own, ('data', 'stage'), [(k * n_stage + q, (1 - k) * n_sta...  9.26 us
  transfers between devices with their start and end apart: 3, of which 2 were waited for; matrix products, arithmetic and copies ran while one was open for 0% of the time, Pallas kernels for 9%

profile of v8, /device:TPU:3, one launch (start us, length us, event | category | flops | bytes accessed | tf_op | source)
XLA Modules:
  0.0 318.4 jit_solution(14652667811846565058)
XLA Ops:
  1.9 139.1 %backward.1 = (f32[768,768]{1,0:T(8,128)}, f32[768,768]{1,0:T(8,128)}, f32[256,768]{1,0:T(8,128)}, f32[128,768]{1,0:T(8,128)}, bf16[1536,768]{1,0:T(8,128)(2,1)}, /*index=5*/f32[8,128]{1,0:T(8,128)}) custom-call(f32[1]{0:T(128)S(6)} %copy.38.lr_ref, f32[1]{0:T(128)S(6)} %copy.39.mn_ref, f32[768,1536]{1,0:T(8,128)} %bitcast.19, f32[1536,768]{1,0:T(8,128)} %bitcast.34, ...), custom_call_target="tpu_custom_call" | custom-call | tf_op jit(solution)/shard_map/backward/pallas_call | solution.py:634
  141.0 3.1 collective-permute-start
  144.1 3.1 collective-permute-start.1
  147.2 14.1 %update_own.1 = (f32[768,1536]{1,0:T(8,128)}, f32[1536,768]{1,0:T(8,128)}, f32[768,1536]{1,0:T(8,128)}, f32[1536,768]{1,0:T(8,128)}, f32[768,1536]{1,0:T(8,128)}, /*index=5*/f32[1536,768]{1,0:T(8,128)}) custom-call(s32[1]{0:T(128)} %bitcast.d_ref, f32[1]{0:T(128)S(6)} %copy.38.lr_ref, f32[1]{0:T(128)S(6)} %copy.39.mn_ref, ...), custom_call_target="tpu_custom_call" | custom-call | flops 10000000000 | bytes 34000000 | tf_op jit(solution)/shard_map/update_own/pallas_call | solution.py:673
  161.4 9.3 %collective-permute-done.first_hbm = bf16[1536,768]{1,0:T(8,128)(2,1)} collective-permute-done((bf16[1536,768]{1,0:T(8,128)(2,1)}, bf16[1536,768]{1,0:T(8,128)(2,1)}, u32[]{:S(2)}, u32[]{:S(2)}) %collective-permute-start) | collective-permute-done | bytes 2359328 | tf_op jit(solution)/shard_map/ppermute | solution.py:658
  170.6 3.1 collective-permute-done.1.shard_hbm
  173.7 124.5 %forward.1 = (f32[512,768]{1,0:T(8,128)}, f32[640,768]{1,0:T(8,128)}, bf16[16,96,768]{2,1,0:T(8,128)(2,1)}) custom-call(bf16[1536,768]{1,0:T(8,128)(2,1)} %get-tuple-element.35.own_hbm, bf16[1536,768]{1,0:T(8,128)(2,1)} %collective-permute-done.first_hbm, bf16[1536,768]{1,0:T(8,128)(2,1)} %collective-permute-done.1.shard_hbm, ...), custom_call_target="tpu_custom_call" | custom-call | tf_op jit(solution)/shard_map/forward/pallas_call | solution.py:688
  298.2 1.2 collective-permute-start.2
  299.5 14.4 %update_other.1 = (f32[768,1536]{1,0:T(8,128)}, f32[1536,768]{1,0:T(8,128)}, f32[768,1536]{1,0:T(8,128)}, f32[1536,768]{1,0:T(8,128)}, f32[768,1536]{1,0:T(8,128...) custom-call(s32[1]{0:T(128)} %bitcast.d_ref, ...), custom_call_target="tpu_custom_call", output_to_operand_aliasing={{0}: (14, {}), {1}: (15, {}), {2}: (16, {}), {3}: (17, {}),... | custom-call | flops 10000000000 | bytes 40000000 | tf_op jit(solution)/shard_map/update_other/pallas_call | solution.py:718
  313.9 0.0 collective-permute-done.2.gu
  313.9 0.0 copy-start
  313.9 0.9 copy-done
  314.8 3.6 %update_late.1 = (f32[768,1536]{1,0:T(8,128)}, f32[768,1536]{1,0:T(8,128)}, f32[768,1536]{1,0:T(8,128)}) custom-call(s32[1]{0:T(128)} %bitcast.d_ref, f32[1]{0:T(128)S(6)} %copy.38.lr_ref, f32[1]{0:T(128)S(6)} %copy.39.mn_ref, f32[8,128]{1,0:T(8,128)} %get-tuple-element.34.norm_ref, ...), custom_call_target="tpu_custom_call", output_to_operand_aliasing={{0}: (8, {}), {1}: (9, {}), {2}: (10, {})} | custom-call | tf_op jit(solution)/shard_map/update_late/pallas_call | solution.py:731
Async XLA Ops:
  141.0 29.6 %collective-permute-start = (bf16[1536,768]{1,0:T(8,128)(2,1)}, bf16[1536,768]{1,0:T(8,128)(2,1)}, u32[]{:S(2)}, u32[]{:S(2)}) collective-permute-start(bf16[1536,768]{1,0:T(8,128)(2,1)} %get-tuple-element.35.own_hbm), channel_id=1, source_target_pairs={{0,4},{3,7},{4,0},{7,3},{8,12},{11,15},{12,8},{15,11}} | collective-permute-start | bytes 7077896 | tf_op jit(solution)/shard_map/ppermute | solution.py:658
  144.1 29.6 %collective-permute-start.1 = (bf16[1536,768]{1,0:T(8,128)(2,1)}, bf16[1536,768]{1,0:T(8,128)(2,1)}, u32[]{:S(2)}, u32[]{:S(2)}) collective-permute-start(bf16[1536,768]{1,0:T(8,128)(2,1)} %get-tuple-element.35.own_hbm), channel_id=1, source_target_pairs={{3,11},{11,3},{7,15},{15,7}} | collective-permute-start | bytes 7077896 | tf_op jit(solution)/shard_map/ppermute | solution.py:659
  298.2 15.6 %collective-permute-start.2 = (f32[256,768]{1,0:T(8,128)}, f32[256,768]{1,0:T(8,128)S(1)}, u32[]{:S(2)}, u32[]{:S(2)}) collective-permute-start(f32[256,768]{1,0:T(8,128)} %get-tuple-element.41), channel_id=1, source_target_pairs={{0,4},{4,0},{1,5},{5,1},{2,6},{6,2},{3,7},{7,3},{8,12},{12,8},{9,1... | collective-permute-start | bytes 2359304 | tf_op jit(solution)/shard_map/ppermute | solution.py:706
  313.9 0.9 copy-start

commit v9 on v8

--- a/solution.py
+++ b/solution.py
@@ -27,7 +27,6 @@
 FWD_ROWS = 96
 UPD_ROWS = 128
 PRE_ROWS = 128
-LATE_ROWS = 256
 TURN_STEP = 8
 VMEM_LIMIT = 66_000_000
 
@@ -51,7 +50,7 @@
 def adamw_update(weight, moment_one, moment_two, grad_step, step_rate):
     mom_new = BETA_ONE * moment_one + (1.0 - BETA_ONE) * grad_step
     sec_new = BETA_TWO * moment_two + (1.0 - BETA_TWO) * grad_step * grad_step
-    direction = (mom_new / ONE_CORR) / (jnp.sqrt(sec_new / TWO_CORR) + ADAM_EPS)
+    direction = (mom_new * (1.0 / ONE_CORR)) / (jnp.sqrt(sec_new * (1.0 / TWO_CORR)) + ADAM_EPS)
     weight_new = weight - step_rate * (direction + WEIGHT_DECAY * weight)
     return weight_new, mom_new, sec_new
 
@@ -78,7 +77,7 @@
 
 
 def bwd_kernel(dims, lr_ref, mn_ref, wu_hbm, wd_hbm, mu_hbm, md_hbm, vu_hbm, vd_hbm, acts_hbm, dy_hbm, gu_hbm, gd_hbm,
-               gbu_hbm, gbd_hbm, late_hbm, pre_oth, own_hbm, norm_out,
+               gbu_hbm, gbd_hbm, pre_oth, own_hbm, norm_out,
                wu32, wd32, wu_bf, wd_bf, aa, gg, hid_o, dz_o, slope, slope_o, dz_own, h_own,
                gu_own, gd_own, gu_oth, gd_oth, gu_rcv, gd_rcv, mu32, md32, vu32, vd32, new_bf, part, part_rcv, fin, norm_buf,
                ld_sem, ysend, yrecv, psend, precv, fsend, frecv, nsend, nrecv, st_sem):
@@ -310,8 +309,6 @@
     acc = combine_up(acc)
     store_u = pltpu.make_async_copy(gu_own, gbu_hbm, st_sem.at[0])
     store_u.start()
-    store_late = pltpu.make_async_copy(gu_own.at[pl.ds(width - LATE_ROWS, LATE_ROWS)], late_hbm, st_sem.at[3])
-    store_late.start()
     tile = acc[:, 0:128]
     for k in range(1, half // 128):
         tile = tile + acc[:, k * 128:(k + 1) * 128]
@@ -352,7 +349,7 @@
         new_bf[pl.ds(pl.multiple_of(width + i * 32, 32), 32), :] = adamw_update(weight, md32[at, :], vd32[at, :], clip * gd_own[at, :], rate)[0].astype(BF16)
         return carry
     lax.fori_loop(0, half // 32, new_down, 0)
-    store_bd = pltpu.make_async_copy(new_bf.at[pl.ds(width, half)], own_hbm.at[pl.ds(width, half)], st_sem.at[4])
+    store_bd = pltpu.make_async_copy(new_bf.at[pl.ds(width, half)], own_hbm.at[pl.ds(width, half)], st_sem.at[3])
     store_bd.start()
 
     for k in range(1, n_all):
@@ -376,7 +373,6 @@
                 fin_copy(c, zi).wait_send()
     store_u.wait()
     store_d.wait()
-    store_late.wait()
     send_pre.wait()
     store_bu.wait()
     store_bd.wait()
@@ -401,13 +397,7 @@
     y_out[...] = y_in[...]
 
 
-def late_kernel(d_ref, lr_ref, mn_ref, norm_ref, gu, wu, mu, vu, *rest):
-    owu, omu, ovu = rest[3:]
-    clip = clip_of(norm_ref[...], mn_ref[0])
-    owu[...], omu[...], ovu[...] = adamw_update(wu[...], mu[...], vu[...], clip * gu[...], lr_ref[0])
-
-
-def fwd_kernel(dims, own_hbm, first_hbm, shard_hbm, gbu_hbm, gbd_hbm, x_hbm, after_hbm,
+def fwd_kernel(dims, own_hbm, first_hbm, gbu_hbm, gbd_hbm, x_hbm, after_hbm,
                gu_oth, gd_oth, y_hbm,
                wu_bf, wd_bf, wu_z, wd_z, a_buf, y_buf, part, part_rcv, fin,
                ld_sem, ysend, yrecv, zsend, zrecv, psend, precv, fsend, frecv, agsend, agrecv, outsend, outrecv, turn):
@@ -433,10 +423,6 @@
         pltpu.make_async_copy(first_hbm.at[up_rows], wu_bf.at[:, oth_ff], ld_sem.at[3]),
         pltpu.make_async_copy(first_hbm.at[down_rows], wd_bf.at[oth_ff, :], ld_sem.at[4]),
     ]
-    shard_loads = [
-        pltpu.make_async_copy(shard_hbm.at[up_rows], wu_z.at[:, own_ff], ld_sem.at[5]),
-        pltpu.make_async_copy(shard_hbm.at[down_rows], wd_z.at[own_ff, :], ld_sem.at[6]),
-    ]
     for copy in loads:
         copy.start()
 
@@ -445,10 +431,6 @@
         for copy in first_loads:
             copy.start()
 
-    @pl.when(p == last)
-    def _():
-        for copy in shard_loads:
-            copy.start()
     x_load = pltpu.make_async_copy(x_hbm, a_buf, ld_sem.at[2])
 
     @pl.when(p == 0)
@@ -458,12 +440,14 @@
 
     send_wu = remote(own_hbm.at[up_rows], wu_bf.at[:, own_ff], ysend.at[0], yrecv.at[0], ypeer)
     send_wd = remote(own_hbm.at[down_rows], wd_bf.at[own_ff, :], ysend.at[1], yrecv.at[1], ypeer)
-    send_gu = remote(gbu_hbm.at[pl.ds(0, gu_oth.shape[0])], gu_oth, ysend.at[2], yrecv.at[2], ypeer)
+    send_gu = remote(gbu_hbm, gu_oth, ysend.at[2], yrecv.at[2], ypeer)
     send_gd = remote(gbd_hbm.at[pl.ds(half - gd_oth.shape[0], gd_oth.shape[0])], gd_oth, ysend.at[3], yrecv.at[3], ypeer)
 
     shard = [
-        remote(first_hbm.at[up_rows], wu_z.at[:, oth_ff], zsend.at[0], zrecv.at[0], zpeer),
-        remote(first_hbm.at[down_rows], wd_z.at[oth_ff, :], zsend.at[1], zrecv.at[1], zpeer),
+        remote(own_hbm.at[up_rows], wu_z.at[:, own_ff], zsend.at[0], zrecv.at[0], zpeer),
+        remote(own_hbm.at[down_rows], wd_z.at[own_ff, :], zsend.at[1], zrecv.at[1], zpeer),
+        remote(first_hbm.at[up_rows], wu_z.at[:, oth_ff], zsend.at[2], zrecv.at[2], zpeer),
+        remote(first_hbm.at[down_rows], wd_z.at[oth_ff, :], zsend.at[3], zrecv.at[3], zpeer),
     ]
 
     @pl.when(p == last)
@@ -494,8 +478,9 @@
 
     @pl.when(p == last)
     def _():
-        for copy in shard_loads:
-            copy.wait()
+        pl.semaphore_wait(turn, 1)
+        send_gu.start()
+        send_gd.start()
         for copy in shard:
             copy.wait_recv()
 
@@ -574,7 +559,7 @@
         def _():
             publish(i - 1)
 
-        @pl.when((i == TURN_STEP) & first)
+        @pl.when((i == TURN_STEP) & (p == 0))
         def _():
             pl.semaphore_wait(turn, 1)
             send_gu.start()
@@ -631,11 +616,11 @@
         nb = rows // BACK_ROWS
         hb = BACK_ROWS // 2
         sds = jax.ShapeDtypeStruct
-        gbar_u, gbar_d, late, pre_oth, b_own, norm_tile = pl.pallas_call(
+        gbar_u, gbar_d, pre_oth, b_own, norm_tile = pl.pallas_call(
             functools.partial(bwd_kernel, dims),
-            out_shape=(sds((width, half), F32), sds((half, width), F32), sds((LATE_ROWS, half), F32), sds((PRE_ROWS, width), F32), sds((width + half, width), BF16), sds((8, 128), F32)),
+            out_shape=(sds((width, half), F32), sds((half, width), F32), sds((PRE_ROWS, width), F32), sds((width + half, width), BF16), sds((8, 128), F32)),
             in_specs=[smem_spec] * 2 + [any_spec] * 10,
-            out_specs=(any_spec,) * 5 + (vmem_spec,),
+            out_specs=(any_spec,) * 4 + (vmem_spec,),
             scratch_shapes=[
                 pltpu.VMEM((width, ff), F32), pltpu.VMEM((ff, width), F32),
                 pltpu.VMEM((width, ff), BF16), pltpu.VMEM((ff, width), BF16),
@@ -648,7 +633,7 @@
                 pltpu.VMEM((nb, BACK_ROWS, width), F32), pltpu.VMEM((nb, hb, width), F32),
                 pltpu.VMEM((nb, hb, width), BF16), pltpu.VMEM((n_all, 8, 128), F32),
                 dma((12,)), dma((5,)), dma((5,)), dma((nb,)), dma((nb,)), dma((nb, 2)), dma((nb, 2)),
-                dma((n_all,)), dma((n_all,)), dma((5,)),
+                dma((n_all,)), dma((n_all,)), dma((4,)),
             ],
             compiler_params=pltpu.CompilerParams(collective_id=0, has_side_effects=True, vmem_limit_bytes=VMEM_LIMIT),
             name='backward',
@@ -656,7 +641,6 @@
 
         ends = (0, n_stage - 1)
         b_first = lax.ppermute(b_own, ('data', 'stage'), [(k * n_stage + q, (1 - k) * n_stage + q) for k in range(n_data) for q in ends])
-        b_shard = lax.ppermute(b_own, ('model', 'stage'), [(k * n_stage + ends[1], (1 - k) * n_stage + ends[1]) for k in range(n_model)])
         blocks = half // UPD_ROWS
         state = (w_up[0], w_down[0], m_up[0], m_down[0], v_up[0], v_down[0])
         state_shapes = tuple(sds(s.shape, F32) for s in state)
@@ -687,58 +671,41 @@
         fb = FWD_ROWS // 2
         gu_oth, gd_oth, y_next = pl.pallas_call(
             functools.partial(fwd_kernel, dims),
-            out_shape=(sds((width - LATE_ROWS, half), F32), sds((half - PRE_ROWS, width), F32), sds((nc, FWD_ROWS, width), BF16)),
-            in_specs=[any_spec] * 7,
+            out_shape=(sds((width, half), F32), sds((half - PRE_ROWS, width), F32), sds((nc, FWD_ROWS, width), BF16)),
+            in_specs=[any_spec] * 6,
             out_specs=(any_spec, any_spec, any_spec),
             scratch_shapes=[pltpu.VMEM((width, ff), BF16), pltpu.VMEM((ff, width), BF16)] * 2 + [
                 pltpu.VMEM((nc, FWD_ROWS, width), BF16), pltpu.VMEM((nc, FWD_ROWS, width), BF16),
                 pltpu.VMEM((nc, FWD_ROWS, width), F32), pltpu.VMEM((nc, fb, width), F32),
                 pltpu.VMEM((nc, fb, width), BF16),
-                dma((7,)), dma((4,)), dma((4,)), dma((2,)), dma((2,)), dma((nc,)), dma((nc,)), dma((nc, 2)), dma((nc, 2)),
+                dma((5,)), dma((4,)), dma((4,)), dma((4,)), dma((4,)), dma((nc,)), dma((nc,)), dma((nc, 2)), dma((nc, 2)),
                 dma((nc,)), dma((nc,)), dma((nc, n_stage)), dma((nc,)), pltpu.SemaphoreType.REGULAR,
             ],
             compiler_params=pltpu.CompilerParams(collective_id=1, has_side_effects=True, vmem_limit_bytes=VMEM_LIMIT),
             name='forward',
-        )(b_own, b_first, b_shard, gbar_u, gbar_d, x_next.reshape(nc, FWD_ROWS, width), fresh[0])
+        )(b_own, b_first, gbar_u, gbar_d, x_next.reshape(nc, FWD_ROWS, width), fresh[0])
 
         other = update_specs(lambda w: 1 - w)
-        gu_oth, late = lax.optimization_barrier((gu_oth, late))
-        late_oth = lax.ppermute(late, 'data', [(k, 1 - k) for k in range(n_data)])
         y_next = y_next.reshape(n_micro * rows, width)
-        npre, nlate = PRE_ROWS // UPD_ROWS, LATE_ROWS // UPD_ROWS
+        npre = PRE_ROWS // UPD_ROWS
         steps = width // UPD_ROWS
-        lastup = steps - nlate - 1
 
         def rows_spec(start, count):
             return pl.BlockSpec((UPD_ROWS, width), lambda i, w: (jnp.clip(i - start, 0, count - 1), 0))
         y_spec = pl.BlockSpec((n_micro * rows // steps, width), lambda i, w: (i, 0))
-        up_oth = pl.BlockSpec((UPD_ROWS, half), lambda i, w: (jnp.minimum(i, lastup), 1 - w[0]))
-        down_oth = pl.BlockSpec((UPD_ROWS, width), lambda i, w: ((1 - w[0]) * blocks + i, 0))
-        other = [up_oth, down_oth]
+        other = update_specs(lambda w: 1 - w)
         *filled, y_next = pl.pallas_call(
             fill_kernel,
             out_shape=state_shapes + (sds(y_next.shape, BF16),),
             grid_spec=pltpu.PrefetchScalarGridSpec(
                 num_scalar_prefetch=1, grid=(steps,),
-                in_specs=small + [rows_spec(0, lastup + 1), rows_spec(0, npre), rows_spec(npre, blocks - npre), y_spec] + other * 3 + [any_spec] * 6,
+                in_specs=small + [plain_up, rows_spec(0, npre), rows_spec(npre, blocks - npre), y_spec] + other * 3 + [any_spec] * 6,
                 out_specs=other * 3 + [y_spec]),
             input_output_aliases={14 + k: k for k in range(6)},
             compiler_params=pltpu.CompilerParams(dimension_semantics=('arbitrary',), vmem_limit_bytes=VMEM_LIMIT),
             cost_estimate=pl.CostEstimate(flops=10**10, bytes_accessed=40 * 10**6, transcendentals=0),
             name='update_other',
         )(which, learn_rate, max_norm, norm_tile, gu_oth, pre_oth, gd_oth, y_next, *state, *fresh)
-        up_late = pl.BlockSpec((UPD_ROWS, half), lambda i, w: (steps - nlate + i, 1 - w[0]))
-        filled[0], filled[2], filled[4] = pl.pallas_call(
-            late_kernel,
-            out_shape=(state_shapes[0],) * 3,
-            grid_spec=pltpu.PrefetchScalarGridSpec(
-                num_scalar_prefetch=1, grid=(nlate,),
-                in_specs=small + [plain_up] + [up_late] * 3 + [any_spec] * 3,
-                out_specs=[up_late] * 3),
-            input_output_aliases={8 + k: k for k in range(3)},
-            compiler_params=pltpu.CompilerParams(dimension_semantics=('arbitrary',), vmem_limit_bytes=VMEM_LIMIT),
-            name='update_late',
-        )(which, learn_rate, max_norm, norm_tile, late_oth, state[0], state[2], state[4], filled[0], filled[2], filled[4])
         return tuple(s[None] for s in filled) + (y_next.reshape(n_micro, rows, width),)
 
     return jax.shard_map(device_step, mesh=mesh, in_specs=in_specs, out_specs=out_specs, check_vma=False)

time: 319 us -> 331 us (1.038)
  the two profiles are of different devices: /device:TPU:3 before, /device:TPU:1 now
where the time goes in v9:
time: 331 us
  Pallas kernels  327 us (99%)
    pallas_call x1, Pallas kernels, device_step(): pl.pallas_call(functools.partial(fwd_kernel, dims), out_shape=(sds((width...  156 us
    pallas_call x1, Pallas kernels, device_step(): pl.pallas_call(functools.partial(bwd_kernel, dims), out_shape=(sds((width...  141 us
    pallas_call x1, Pallas kernels, device_step(): pl.pallas_call(fill_kernel, out_shape=state_shapes + (sds(y_next.shape, B...  15.8 us
    pallas_call x1, Pallas kernels, device_step(): pl.pallas_call(update_kernel, out_shape=state_shapes, grid_spec=pltpu.Pre...  14 us
  transfers between devices with their start and end apart: 1, of which 0 were waited for; matrix products, arithmetic and copies ran while one was open for 0% of the time, Pallas kernels for 4%

profile of v9, /device:TPU:1, one launch (start us, length us, event | category | flops | bytes accessed | tf_op | source)
XLA Modules:
  0.0 331.2 jit_solution(18413959451212033919)
XLA Ops:
  1.9 140.8 %backward.1 = (f32[768,768]{1,0:T(8,128)}, f32[768,768]{1,0:T(8,128)}, f32[128,768]{1,0:T(8,128)}, bf16[1536,768]{1,0:T(8,128)(2,1)}, f32[8,128]{1,0:T(8,128)}) custom-call(f32[1]{0:T(128)S(6)} %copy.32.lr_ref, f32[1]{0:T(128)S(6)} %copy.33.mn_ref, f32[768,1536]{1,0:T(8,128)} %bitcast.19, f32[1536,768]{1,0:T(8,128)} %bitcast.22, f32[768,1536]{1,0:T(8,128)} %bitcast.25, ...), custom_call_target="tpu_custom_call" | custom-call | tf_op jit(solution)/shard_map/backward/pallas_call | solution.py:619
  142.7 2.2 collective-permute-start
  144.9 14.0 %update_own.1 = (f32[768,1536]{1,0:T(8,128)}, f32[1536,768]{1,0:T(8,128)}, f32[768,1536]{1,0:T(8,128)}, f32[1536,768]{1,0:T(8,128)}, f32[768,1536]{1,0:T(8,128)}, /*index=5*/f32[1536,768]{1,0:T(8,128)}) custom-call(s32[1]{0:T(128)} %bitcast.d_ref, f32[1]{0:T(128)S(6)} %copy.32.lr_ref, f32[1]{0:T(128)S(6)} %copy.33.mn_ref, ...), custom_call_target="tpu_custom_call" | custom-call | flops 10000000000 | bytes 34000000 | tf_op jit(solution)/shard_map/update_own/pallas_call | solution.py:657
  158.9 0.0 collective-permute-done.first_hbm
  158.9 156.4 %forward.1 = (f32[768,768]{1,0:T(8,128)}, f32[640,768]{1,0:T(8,128)}, bf16[16,96,768]{2,1,0:T(8,128)(2,1)}) custom-call(bf16[1536,768]{1,0:T(8,128)(2,1)} %get-tuple-element.29.own_hbm, bf16[1536,768]{1,0:T(8,128)(2,1)} %collective-permute-done.first_hbm, f32[768,768]{1,0:T(8,128)} %get-tuple-element.30.gu.gbu_hbm, f32[768,768]{1,0:T(8,128)} %get-tuple-element.31.gd.gbd_hbm, ...), custom_call_target="tpu_custom_call" | custom-call | tf_op jit(solution)/shard_map/forward/pallas_call | solution.py:672
  315.4 15.8 %update_other.1 = (f32[768,1536]{1,0:T(8,128)}, f32[1536,768]{1,0:T(8,128)}, f32[768,1536]{1,0:T(8,128)}, f32[1536,768]{1,0:T(8,128)}, f32[768,1536]{1,0:T(8,128...) custom-call(s32[1]{0:T(128)} %bitcast.d_ref, ...), custom_call_target="tpu_custom_call", output_to_operand_aliasing={{0}: (14, {}), {1}: (15, {}), {2}: (16, {}), {3}: (17, {}),... | custom-call | flops 10000000000 | bytes 40000000 | tf_op jit(solution)/shard_map/update_other/pallas_call | solution.py:697
Async XLA Ops:
  142.7 16.2 %collective-permute-start = (bf16[1536,768]{1,0:T(8,128)(2,1)}, bf16[1536,768]{1,0:T(8,128)(2,1)}, u32[]{:S(2)}, u32[]{:S(2)}) collective-permute-start(bf16[1536,768]{1,0:T(8,128)(2,1)} %get-tuple-element.29.own_hbm), channel_id=1, source_target_pairs={{0,4},{3,7},{4,0},{7,3},{8,12},{11,15},{12,8},{15,11}} | collective-permute-start | bytes 7077896 | tf_op jit(solution)/shard_map/ppermute | solution.py:643

commit v10 on v7

--- a/solution.py
+++ b/solution.py
@@ -26,8 +26,7 @@
 BACK_ROWS = 128
 FWD_ROWS = 96
 UPD_ROWS = 128
-PRE_ROWS = 64
-EARLY_ROWS = 192
+EARLY_ROWS = 256
 LATE_ROWS = 128
 TURN_STEP = 5
 VMEM_LIMIT = 66_000_000
@@ -52,7 +51,7 @@
 def adamw_update(weight, moment_one, moment_two, grad_step, step_rate):
     mom_new = BETA_ONE * moment_one + (1.0 - BETA_ONE) * grad_step
     sec_new = BETA_TWO * moment_two + (1.0 - BETA_TWO) * grad_step * grad_step
-    direction = (mom_new / ONE_CORR) / (jnp.sqrt(sec_new / TWO_CORR) + ADAM_EPS)
+    direction = (mom_new * (1.0 / ONE_CORR)) / (jnp.sqrt(sec_new * (1.0 / TWO_CORR)) + ADAM_EPS)
     weight_new = weight - step_rate * (direction + WEIGHT_DECAY * weight)
     return weight_new, mom_new, sec_new
 
@@ -79,17 +78,18 @@
 
 
 def bwd_kernel(dims, wu_hbm, wd_hbm, acts_hbm, dy_hbm, gu_hbm, gd_hbm,
-               gbu_hbm, gbd_hbm, early_hbm, late_hbm, pre_oth, norm_out,
+               gbu_hbm, gbd_hbm, early_hbm, late_hbm, norm_out,
                wu32, wd32, wu_bf, wd_bf, aa, gg, hid_o, dz_o, slope, slope_o, dz_own, h_own,
                gu_own, gd_own, gu_oth, gd_oth, gu_rcv, gd_rcv, part, part_rcv, fin, norm_buf,
-               ld_sem, ysend, yrecv, psend, precv, fsend, frecv, nsend, nrecv, st_sem):
+               ld_sem, ysend, yrecv, rsend, rrecv, psend, precv, fsend, frecv, nsend, nrecv, st_sem):
     n_model, n_data, n_stage = dims
     z, d, p = lax.axis_index('model'), lax.axis_index('data'), lax.axis_index('stage')
     zo, do = 1 - z, 1 - d
     ypeer, zpeer = (z, do, p), (zo, d, p)
     last = n_stage - 1
-    by_rows = lax.rem(p, 2) == 0
-    by_sums = lax.rem(p, 2) == 1
+    by_rows = p == 0
+    by_sums = p > 0
+    hub = n_stage // 2
     rows = aa.shape[0] // 2
     width = aa.shape[1]
     half = hid_o.shape[1]
@@ -125,7 +125,9 @@
         gu_load.start()
 
     whole_barrier(n_model, n_data, n_stage)
-    send_acts = remote(acts_hbm, aa.at[theirs], ysend.at[0], yrecv.at[0], ypeer)
+    send_acts = remote(acts_hbm, hid_o, ysend.at[0], rrecv.at[0], (z, d, hub))
+    relay_over = remote(hid_o, dz_o, rsend.at[0], rrecv.at[1], ypeer)
+    relay_back = remote(dz_o, aa.at[theirs], rsend.at[1], yrecv.at[0], (z, d, 0))
     raw_gu = remote(gu_hbm.at[:, oth_ff], gu_rcv, ysend.at[1], yrecv.at[1], ypeer)
     raw_gd = remote(gd_hbm.at[oth_ff, :], gd_rcv, ysend.at[2], yrecv.at[2], ypeer)
     sum_gu = remote(gu_oth, gu_rcv, ysend.at[1], yrecv.at[1], ypeer)
@@ -166,6 +168,35 @@
     def _():
         dy_load.wait()
 
+    @pl.when(p == hub)
+    def _():
+        pltpu.make_async_copy(hid_o, hid_o, rrecv.at[0]).wait()
+        relay_over.start()
+        pltpu.make_async_copy(dz_o, dz_o, rrecv.at[1]).wait()
+        relay_back.start()
+
+    def down_block(j, base):
+        at = pl.ds(pl.multiple_of(base * half + j * 128, 128), 128)
+        return mm(h_own[:, at], gg[mine, :], TN)
+
+    def up_block(j, ff_at):
+        at = pl.ds(pl.multiple_of(j * 128, 128), 128)
+        return mm(aa[mine, at], dz_own[:, ff_at], TN)
+
+    def send_down():
+        gd_load.wait()
+
+        def down_oth(j, carry):
+            gd_oth[pl.ds(pl.multiple_of(j * 128, 128), 128), :] += down_block(j, do)
+            return carry
+        lax.fori_loop(0, half // 128, down_oth, 0)
+        gu_load.wait()
+        sum_gd.start()
+
+    @pl.when(p == last)
+    def _():
+        send_down()
+
     def g_at(c, zi):
         return gg.at[pl.ds(pl.multiple_of(c * rb + zi * hb, hb), hb)]
 
@@ -208,25 +239,12 @@
         return carry
     lax.fori_loop(0, nb + 1, chain, 0)
 
-    def down_block(j, base):
-        at = pl.ds(pl.multiple_of(base * half + j * 128, 128), 128)
-        return mm(h_own[:, at], gg[mine, :], TN)
-
-    def up_block(j, ff_at):
-        at = pl.ds(pl.multiple_of(j * 128, 128), 128)
-        return mm(aa[mine, at], dz_own[:, ff_at], TN)
+    @pl.when(by_sums & (p < last))
+    def _():
+        send_down()
 
     @pl.when(by_sums)
     def _():
-        gd_load.wait()
-
-        def down_oth(j, carry):
-            gd_oth[pl.ds(pl.multiple_of(j * 128, 128), 128), :] += down_block(j, do)
-            return carry
-        lax.fori_loop(0, half // 128, down_oth, 0)
-        gu_load.wait()
-        sum_gd.start()
-
         def up_oth(j, carry):
             gu_oth[pl.ds(pl.multiple_of(j * 128, 128), 128), :] += up_block(j, oth_ff)
             return carry
@@ -254,7 +272,7 @@
 
     @pl.when(by_rows)
     def _():
-        send_acts.wait_recv()
+        pltpu.make_async_copy(aa.at[theirs], aa.at[theirs], yrecv.at[0]).wait()
 
         def oth_pre(i, carry):
             at = pl.ds(pl.multiple_of(i * rb, rb), rb)
@@ -298,10 +316,8 @@
     acc = combine_down(acc)
     store_d = pltpu.make_async_copy(gd_own, gbd_hbm, st_sem.at[1])
     store_d.start()
-    store_early = pltpu.make_async_copy(gd_own.at[pl.ds(PRE_ROWS, EARLY_ROWS)], early_hbm, st_sem.at[2])
+    store_early = pltpu.make_async_copy(gd_own.at[pl.ds(0, EARLY_ROWS)], early_hbm, st_sem.at[2])
     store_early.start()
-    send_pre = remote(gd_own.at[pl.ds(0, PRE_ROWS)], pre_oth, ysend.at[4], yrecv.at[4], ypeer)
-    send_pre.start()
     acc = combine_up(acc)
     store_u = pltpu.make_async_copy(gu_own, gbu_hbm, st_sem.at[0])
     store_u.start()
@@ -336,6 +352,11 @@
         for copy in (send_acts, raw_gu, raw_gd, send_g):
             copy.wait_send()
 
+    @pl.when(p == hub)
+    def _():
+        relay_over.wait_send()
+        relay_back.wait_send()
+
     @pl.when(by_sums)
     def _():
         sum_gu.wait_send()
@@ -351,7 +372,6 @@
     store_d.wait()
     store_early.wait()
     store_late.wait()
-    send_pre.wait()
 
 
 def update_kernel(d_ref, lr_ref, mn_ref, norm_ref, gu, gd, wu, wd, mu, md, vu, vd, *rest):
@@ -370,7 +390,7 @@
     clip = clip_of(norm_ref[...], mn_ref[0])
     rate = lr_ref[0]
     step = pl.program_id(0)
-    gd = jnp.where(step < (PRE_ROWS + EARLY_ROWS) // UPD_ROWS, gd_early[...], gd_rest[...])
+    gd = jnp.where(step < EARLY_ROWS // UPD_ROWS, gd_early[...], gd_rest[...])
     owu[...], omu[...], ovu[...] = adamw_update(wu[...], mu[...], vu[...], clip * gu[...], rate)
     owd[...], omd[...], ovd[...] = adamw_update(wd[...], md[...], vd[...], clip * gd, rate)
     y_out[...] = y_in[...]
@@ -596,11 +616,11 @@
         nb = rows // BACK_ROWS
         hb = BACK_ROWS // 2
         sds = jax.ShapeDtypeStruct
-        gbar_u, gbar_d, early, late, pre_oth, norm_tile = pl.pallas_call(
+        gbar_u, gbar_d, early, late, norm_tile = pl.pallas_call(
             functools.partial(bwd_kernel, dims),
-            out_shape=(sds((width, half), F32), sds((half, width), F32), sds((EARLY_ROWS, width), F32), sds((LATE_ROWS, half), F32), sds((PRE_ROWS, width), F32), sds((8, 128), F32)),
+            out_shape=(sds((width, half), F32), sds((half, width), F32), sds((EARLY_ROWS, width), F32), sds((LATE_ROWS, half), F32), sds((8, 128), F32)),
             in_specs=[any_spec] * 6,
-            out_specs=(any_spec,) * 5 + (vmem_spec,),
+            out_specs=(any_spec,) * 4 + (vmem_spec,),
             scratch_shapes=[
                 pltpu.VMEM((width, ff), F32), pltpu.VMEM((ff, width), F32),
                 pltpu.VMEM((width, ff), BF16), pltpu.VMEM((ff, width), BF16),
@@ -611,7 +631,7 @@
             ] + [pltpu.VMEM((width, half), F32), pltpu.VMEM((half, width), F32)] * 3 + [
                 pltpu.VMEM((nb, BACK_ROWS, width), F32), pltpu.VMEM((nb, hb, width), F32),
                 pltpu.VMEM((nb, hb, width), BF16), pltpu.VMEM((n_all, 8, 128), F32),
-                dma((8,)), dma((5,)), dma((5,)), dma((nb,)), dma((nb,)), dma((nb, 2)), dma((nb, 2)),
+                dma((8,)), dma((4,)), dma((4,)), dma((2,)), dma((2,)), dma((nb,)), dma((nb,)), dma((nb, 2)), dma((nb, 2)),
                 dma((n_all,)), dma((n_all,)), dma((4,)),
             ],
             compiler_params=pltpu.CompilerParams(collective_id=0, has_side_effects=True, vmem_limit_bytes=VMEM_LIMIT),
@@ -648,7 +668,7 @@
         fb = FWD_ROWS // 2
         gu_oth, gd_oth, y_next = pl.pallas_call(
             functools.partial(fwd_kernel, dims),
-            out_shape=(sds((width - LATE_ROWS, half), F32), sds((half - PRE_ROWS - EARLY_ROWS, width), F32), sds((nc, FWD_ROWS, width), BF16)),
+            out_shape=(sds((width - LATE_ROWS, half), F32), sds((half - EARLY_ROWS, width), F32), sds((nc, FWD_ROWS, width), BF16)),
             in_specs=[any_spec] * 5,
             out_specs=(any_spec, any_spec, any_spec),
             scratch_shapes=[pltpu.VMEM((width, ff), BF16), pltpu.VMEM((ff, width), BF16)] * 2 + [
@@ -665,9 +685,8 @@
         other = update_specs(lambda w: 1 - w)
         gu_oth, late = lax.optimization_barrier((gu_oth, late))
         late_oth = lax.ppermute(late, 'data', [(k, 1 - k) for k in range(n_data)])
-        early_oth = jnp.concatenate([pre_oth, early_oth])
         y_next = y_next.reshape(n_micro * rows, width)
-        nearly, nlate = (PRE_ROWS + EARLY_ROWS) // UPD_ROWS, LATE_ROWS // UPD_ROWS
+        nearly, nlate = EARLY_ROWS // UPD_ROWS, LATE_ROWS // UPD_ROWS
         steps = width // UPD_ROWS
         lastup = steps - nlate - 1
 

time: 307 us -> 305 us (level)
  transfers between devices with their start and end apart: 2 -> 2, of which waited for: 0 -> 0; matrix products, arithmetic and copies ran while one was open for 1% -> 0% of each run, Pallas kernels for 55% -> 54%
where the time goes in v10:
time: 305 us
  Pallas kernels  300 us (98%)
    pallas_call x1, Pallas kernels, device_step(): pl.pallas_call(functools.partial(fwd_kernel, dims), out_shape=(sds((width...  136 us
    pallas_call x1, Pallas kernels, device_step(): pl.pallas_call(functools.partial(bwd_kernel, dims), out_shape=(sds((width...  131 us
    pallas_call x1, Pallas kernels, device_step(): pl.pallas_call(fill_kernel, out_shape=state_shapes + (sds(y_next.shape, B...  15.7 us
    pallas_call x1, Pallas kernels, device_step(): pl.pallas_call(update_kernel, out_shape=state_shapes + (sds((width, half)...  14.7 us
  transfers between devices with their start and end apart: 2, of which 0 were waited for; matrix products, arithmetic and copies ran while one was open for 0% of the time, Pallas kernels for 54%

profile of v10, /device:TPU:1, one launch (start us, length us, event | category | flops | bytes accessed | tf_op | source)
XLA Modules:
  0.0 305.2 jit_solution(748332989500788607)
XLA Ops:
  0.6 131.1 %backward.1 = (f32[768,768]{1,0:T(8,128)}, f32[768,768]{1,0:T(8,128)}, f32[256,768]{1,0:T(8,128)}, f32[128,768]{1,0:T(8,128)}, f32[8,128]{1,0:T(8,128)}) custom-call(f32[768,1536]{1,0:T(8,128)} %bitcast.19, f32[1536,768]{1,0:T(8,128)} %bitcast.23, bf16[512,768]{1,0:T(8,128)(2,1)} %bitcast.46, bf16[512,768]{1,0:T(8,128)(2,1)} %dy_hbm.1, ...), custom_call_target="tpu_custom_call" | custom-call | tf_op jit(solution)/shard_map/backward/pallas_call | solution.py:619
  131.8 1.3 collective-permute-start.1
  134.3 14.7 %update_own.1 = (f32[768,1536]{1,0:T(8,128)}, f32[1536,768]{1,0:T(8,128)}, f32[768,1536]{1,0:T(8,128)}, f32[1536,768]{1,0:T(8,128)}, f32[768,1536]{1,0:T(8,128)}...) custom-call(s32[1]{0:T(128)} %bitcast.d_ref, f32[1]{0:T(128)S(6)} %copy.38.lr_ref, ...), custom_call_target="tpu_custom_call" | custom-call | tf_op jit(solution)/shard_map/update_own/pallas_call | solution.py:655
  149.0 135.6 %forward.1 = (f32[640,768]{1,0:T(8,128)}, f32[512,768]{1,0:T(8,128)}, bf16[16,96,768]{2,1,0:T(8,128)(2,1)}) custom-call(bf16[768,768]{1,0:T(8,128)(2,1)} %get-tuple-element.38.bu_hbm, bf16[768,768]{1,0:T(8,128)(2,1)} %get-tuple-element.39.bd_hbm, f32[768,768]{1,0:T(8,128)} %get-tuple-element.36.gu.gbu_hbm, f32[768,768]{1,0:T(8,128)} %get-tuple-element.37.gd.gbd_hbm, ...), custom_call_target="tpu_custom_call" | custom-call | tf_op jit(solution)/shard_map/forward/pallas_call | solution.py:669
  284.6 1.2 collective-permute-start
  285.8 0.0 collective-permute-done.1.gd_early
  285.8 0.0 copy-start
  285.8 0.9 copy-done
  286.7 15.7 %update_other.1 = (f32[768,1536]{1,0:T(8,128)}, f32[1536,768]{1,0:T(8,128)}, f32[768,1536]{1,0:T(8,128)}, f32[1536,768]{1,0:T(8,128)}, f32[768,1536]{1,0:T(8,128...) custom-call(s32[1]{0:T(128)} %bitcast.d_ref, ...), custom_call_target="tpu_custom_call", output_to_operand_aliasing={{0}: (14, {}), {1}: (15, {}), {2}: (16, {}), {3}: (17, {}),... | custom-call | flops 10000000000 | bytes 40000000 | tf_op jit(solution)/shard_map/update_other/pallas_call | solution.py:699
  302.4 0.0 collective-permute-done.gu
  302.4 2.8 update_late.1
Async XLA Ops:
  131.8 154.1 %collective-permute-start.1 = (f32[256,768]{1,0:T(8,128)}, f32[256,768]{1,0:T(8,128)S(1)}, u32[]{:S(2)}, u32[]{:S(2)}) collective-permute-start(f32[256,768]{1,0:T(8,128)} %get-tuple-element.44), channel_id=1, source_target_pairs={{0,4},{4,0},{1,5},{5,1},{2,6},{6,2},{3,7},{7,3},{8,12},{12,8},{9,1... | collective-permute-start | bytes 2359304 | tf_op jit(solution)/shard_map/ppermute | solution.py:641
  284.6 17.8 %collective-permute-start = (f32[128,768]{1,0:T(8,128)}, f32[128,768]{1,0:T(8,128)}, u32[]{:S(2)}, u32[]{:S(2)}) collective-permute-start(f32[128,768]{1,0:T(8,128)} %get-tuple-element.42), channel_id=1, source_target_pairs={{0,4},{4,0},{1,5},{5,1},{2,6},{6,2},{3,7},{7,3},{8,12},{12,8},{9,1... | collective-permute-start | bytes 1179656 | tf_op jit(solution)/shard_map/ppermute | solution.py:687
  285.8 0.9 copy-start

commit v11 on v10

--- a/solution.py
+++ b/solution.py
@@ -23,7 +23,8 @@
 F32 = jnp.float32
 BF16 = jnp.bfloat16
 MESH = pl.DeviceIdType.MESH
-BACK_ROWS = 128
+BACK_ROWS = 64
+PRE_BLOCK = 128
 FWD_ROWS = 96
 UPD_ROWS = 128
 EARLY_ROWS = 256
@@ -96,6 +97,7 @@
     rb = BACK_ROWS
     hb = rb // 2
     nb = rows // rb
+    pb = PRE_BLOCK
     own_ff = pl.ds(pl.multiple_of(d * half, 128), half)
     oth_ff = pl.ds(pl.multiple_of(do * half, 128), half)
     mine, theirs = pl.ds(0, rows), pl.ds(rows, rows)
@@ -150,12 +152,12 @@
     lax.fori_loop(0, width // 128, cast_up, 0)
 
     def own_pre(i, carry):
-        at = pl.ds(pl.multiple_of(i * rb, rb), rb)
+        at = pl.ds(pl.multiple_of(i * pb, pb), pb)
         val, slp = gelu_both(mm(aa[at, :], wu_bf[...], NN))
         h_own[at, :] = val.astype(BF16)
         slope[at, :] = slp
         return carry
-    lax.fori_loop(0, nb, own_pre, 0)
+    lax.fori_loop(0, rows // pb, own_pre, 0)
     loads[2].wait()
 
     def cast_down(i, carry):
@@ -275,20 +277,20 @@
         pltpu.make_async_copy(aa.at[theirs], aa.at[theirs], yrecv.at[0]).wait()
 
         def oth_pre(i, carry):
-            at = pl.ds(pl.multiple_of(i * rb, rb), rb)
-            val, slp = gelu_both(mm(aa[pl.ds(pl.multiple_of(rows + i * rb, rb), rb), :], wu_bf[:, own_ff], NN))
+            at = pl.ds(pl.multiple_of(i * pb, pb), pb)
+            val, slp = gelu_both(mm(aa[pl.ds(pl.multiple_of(rows + i * pb, pb), pb), :], wu_bf[:, own_ff], NN))
             hid_o[at, :] = val.astype(BF16)
             slope_o[at, :] = slp
             return carry
-        lax.fori_loop(0, nb, oth_pre, 0)
+        lax.fori_loop(0, rows // pb, oth_pre, 0)
         send_g.wait_recv()
 
         def oth_dz(i, carry):
-            at = pl.ds(pl.multiple_of(i * rb, rb), rb)
-            grad_hid = mm(gg[pl.ds(pl.multiple_of(rows + i * rb, rb), rb), :], wd_bf[own_ff, :], NT)
+            at = pl.ds(pl.multiple_of(i * pb, pb), pb)
+            grad_hid = mm(gg[pl.ds(pl.multiple_of(rows + i * pb, pb), pb), :], wd_bf[own_ff, :], NT)
             dz_o[at, :] = (slope_o[at, :] * grad_hid).astype(BF16)
             return carry
-        lax.fori_loop(0, nb, oth_dz, 0)
+        lax.fori_loop(0, rows // pb, oth_dz, 0)
 
         def oth_grads(j, carry):
             at = pl.ds(pl.multiple_of(j * 128, 128), 128)

time: 305 us -> 309 us (1.013)
  Pallas kernels: 300 us -> 304 us
    pallas_call x1, Pallas kernels: 131 us -> 135 us  [device_step(): pl.pallas_call(functools.partial(bwd_kernel, dims), out_shape=(sds((width...]
where the time goes in v11:
time: 309 us
  Pallas kernels  304 us (98%)
    pallas_call x1, Pallas kernels, device_step(): pl.pallas_call(functools.partial(fwd_kernel, dims), out_shape=(sds((width...  136 us
    pallas_call x1, Pallas kernels, device_step(): pl.pallas_call(functools.partial(bwd_kernel, dims), out_shape=(sds((width...  135 us
    pallas_call x1, Pallas kernels, device_step(): pl.pallas_call(fill_kernel, out_shape=state_shapes + (sds(y_next.shape, B...  15.7 us
    pallas_call x1, Pallas kernels, device_step(): pl.pallas_call(update_kernel, out_shape=state_shapes + (sds((width, half)...  14.7 us
  transfers between devices with their start and end apart: 2, of which 0 were waited for; matrix products, arithmetic and copies ran while one was open for 0% of the time, Pallas kernels for 54%

profile of v11, /device:TPU:1, one launch (start us, length us, event | category | flops | bytes accessed | tf_op | source)
XLA Modules:
  0.0 308.9 jit_solution(9765441200320556935)
XLA Ops:
  0.6 135.1 %backward.1 = (f32[768,768]{1,0:T(8,128)}, f32[768,768]{1,0:T(8,128)}, f32[256,768]{1,0:T(8,128)}, f32[128,768]{1,0:T(8,128)}, f32[8,128]{1,0:T(8,128)}) custom-call(f32[768,1536]{1,0:T(8,128)} %bitcast.19, f32[1536,768]{1,0:T(8,128)} %bitcast.23, bf16[512,768]{1,0:T(8,128)(2,1)} %bitcast.46, bf16[512,768]{1,0:T(8,128)(2,1)} %dy_hbm.1, ...), custom_call_target="tpu_custom_call" | custom-call | tf_op jit(solution)/shard_map/backward/pallas_call | solution.py:621
  135.7 1.3 collective-permute-start.1
  138.3 14.7 %update_own.1 = (f32[768,1536]{1,0:T(8,128)}, f32[1536,768]{1,0:T(8,128)}, f32[768,1536]{1,0:T(8,128)}, f32[1536,768]{1,0:T(8,128)}, f32[768,1536]{1,0:T(8,128)}...) custom-call(s32[1]{0:T(128)} %bitcast.d_ref, f32[1]{0:T(128)S(6)} %copy.38.lr_ref, ...), custom_call_target="tpu_custom_call" | custom-call | tf_op jit(solution)/shard_map/update_own/pallas_call | solution.py:657
  153.0 135.6 %forward.1 = (f32[640,768]{1,0:T(8,128)}, f32[512,768]{1,0:T(8,128)}, bf16[16,96,768]{2,1,0:T(8,128)(2,1)}) custom-call(bf16[768,768]{1,0:T(8,128)(2,1)} %get-tuple-element.38.bu_hbm, bf16[768,768]{1,0:T(8,128)(2,1)} %get-tuple-element.39.bd_hbm, f32[768,768]{1,0:T(8,128)} %get-tuple-element.36.gu.gbu_hbm, f32[768,768]{1,0:T(8,128)} %get-tuple-element.37.gd.gbd_hbm, ...), custom_call_target="tpu_custom_call" | custom-call | tf_op jit(solution)/shard_map/forward/pallas_call | solution.py:671
  288.6 0.9 collective-permute-start
  289.6 0.0 collective-permute-done.1.gd_early
  289.6 0.0 copy-start
  289.6 0.9 copy-done
  290.4 15.7 %update_other.1 = (f32[768,1536]{1,0:T(8,128)}, f32[1536,768]{1,0:T(8,128)}, f32[768,1536]{1,0:T(8,128)}, f32[1536,768]{1,0:T(8,128)}, f32[768,1536]{1,0:T(8,128...) custom-call(s32[1]{0:T(128)} %bitcast.d_ref, ...), custom_call_target="tpu_custom_call", output_to_operand_aliasing={{0}: (14, {}), {1}: (15, {}), {2}: (16, {}), {3}: (17, {}),... | custom-call | flops 10000000000 | bytes 40000000 | tf_op jit(solution)/shard_map/update_other/pallas_call | solution.py:701
  306.1 0.0 collective-permute-done.gu
  306.2 2.8 update_late.1
Async XLA Ops:
  135.7 153.9 %collective-permute-start.1 = (f32[256,768]{1,0:T(8,128)}, f32[256,768]{1,0:T(8,128)S(1)}, u32[]{:S(2)}, u32[]{:S(2)}) collective-permute-start(f32[256,768]{1,0:T(8,128)} %get-tuple-element.44), channel_id=1, source_target_pairs={{0,4},{4,0},{1,5},{5,1},{2,6},{6,2},{3,7},{7,3},{8,12},{12,8},{9,1... | collective-permute-start | bytes 2359304 | tf_op jit(solution)/shard_map/ppermute | solution.py:643
  288.6 17.5 %collective-permute-start = (f32[128,768]{1,0:T(8,128)}, f32[128,768]{1,0:T(8,128)}, u32[]{:S(2)}, u32[]{:S(2)}) collective-permute-start(f32[128,768]{1,0:T(8,128)} %get-tuple-element.42), channel_id=1, source_target_pairs={{0,4},{4,0},{1,5},{5,1},{2,6},{6,2},{3,7},{7,3},{8,12},{12,8},{9,1... | collective-permute-start | bytes 1179656 | tf_op jit(solution)/shard_map/ppermute | solution.py:689
  289.6 0.9 copy-start

commit v12 on v10

--- a/solution.py
+++ b/solution.py
@@ -116,14 +116,6 @@
     @pl.when(p == last)
     def _():
         dy_load.start()
-    for copy in loads[3:]:
-        copy.start()
-
-    @pl.when(by_sums)
-    def _():
-        gd_load.start()
-        gu_load.start()
-
     whole_barrier(n_model, n_data, n_stage)
     send_acts = remote(acts_hbm, hid_o, ysend.at[0], rrecv.at[0], (z, d, hub))
     relay_over = remote(hid_o, dz_o, rsend.at[0], rrecv.at[1], ypeer)
@@ -155,8 +147,15 @@
         h_own[at, :] = val.astype(BF16)
         slope[at, :] = slp
         return carry
+    loads[2].wait()
+
+    @pl.when(by_sums)
+    def _():
+        gd_load.start()
+        gu_load.start()
+    for copy in loads[3:]:
+        copy.start()
     lax.fori_loop(0, nb, own_pre, 0)
-    loads[2].wait()
 
     def cast_down(i, carry):
         at = pl.ds(pl.multiple_of(i * 128, 128), 128)
@@ -229,17 +228,23 @@
             fin_copy(c, zi).start()
 
     def chain(i, carry):
-        @pl.when(i < nb)
-        def _():
-            compute(i)
+        compute(i)
 
         @pl.when((i >= 1) & (p > 0))
         def _():
             finalize(i - 1)
         return carry
-    lax.fori_loop(0, nb + 1, chain, 0)
-
-    @pl.when(by_sums & (p < last))
+    lax.fori_loop(0, nb, chain, 0)
+
+    @pl.when(by_sums & (p < hub))
+    def _():
+        send_down()
+
+    @pl.when(p > 0)
+    def _():
+        finalize(nb - 1)
+
+    @pl.when((p >= hub) & (p < last))
     def _():
         send_down()
 

time: 305 us -> 302 us (level)
  Pallas kernels: 300 us -> 296 us
  transfers between devices with their start and end apart: 2 -> 2, of which waited for: 0 -> 0; matrix products, arithmetic and copies ran while one was open for 0% -> 0% of each run, Pallas kernels for 54% -> 55%
where the time goes in v12:
time: 302 us
  Pallas kernels  296 us (98%)
    pallas_call x1, Pallas kernels, device_step(): pl.pallas_call(functools.partial(fwd_kernel, dims), out_shape=(sds((width...  135 us
    pallas_call x1, Pallas kernels, device_step(): pl.pallas_call(functools.partial(bwd_kernel, dims), out_shape=(sds((width...  129 us
    pallas_call x1, Pallas kernels, device_step(): pl.pallas_call(fill_kernel, out_shape=state_shapes + (sds(y_next.shape, B...  15.7 us
    pallas_call x1, Pallas kernels, device_step(): pl.pallas_call(update_kernel, out_shape=state_shapes + (sds((width, half)...  14.7 us
  transfers between devices with their start and end apart: 2, of which 0 were waited for; matrix products, arithmetic and copies ran while one was open for 0% of the time, Pallas kernels for 55%

profile of v12, /device:TPU:1, one launch (start us, length us, event | category | flops | bytes accessed | tf_op | source)
XLA Modules:
  0.0 301.8 jit_solution(5322555005664629223)
XLA Ops:
  0.6 128.5 %backward.1 = (f32[768,768]{1,0:T(8,128)}, f32[768,768]{1,0:T(8,128)}, f32[256,768]{1,0:T(8,128)}, f32[128,768]{1,0:T(8,128)}, f32[8,128]{1,0:T(8,128)}) custom-call(f32[768,1536]{1,0:T(8,128)} %bitcast.19, f32[1536,768]{1,0:T(8,128)} %bitcast.23, bf16[512,768]{1,0:T(8,128)(2,1)} %bitcast.46, bf16[512,768]{1,0:T(8,128)(2,1)} %dy_hbm.1, ...), custom_call_target="tpu_custom_call" | custom-call | tf_op jit(solution)/shard_map/backward/pallas_call | solution.py:624
  129.1 1.3 collective-permute-start.1
  131.8 14.7 %update_own.1 = (f32[768,1536]{1,0:T(8,128)}, f32[1536,768]{1,0:T(8,128)}, f32[768,1536]{1,0:T(8,128)}, f32[1536,768]{1,0:T(8,128)}, f32[768,1536]{1,0:T(8,128)}...) custom-call(s32[1]{0:T(128)} %bitcast.d_ref, f32[1]{0:T(128)S(6)} %copy.38.lr_ref, ...), custom_call_target="tpu_custom_call" | custom-call | tf_op jit(solution)/shard_map/update_own/pallas_call | solution.py:660
  146.5 134.8 %forward.1 = (f32[640,768]{1,0:T(8,128)}, f32[512,768]{1,0:T(8,128)}, bf16[16,96,768]{2,1,0:T(8,128)(2,1)}) custom-call(bf16[768,768]{1,0:T(8,128)(2,1)} %get-tuple-element.38.bu_hbm, bf16[768,768]{1,0:T(8,128)(2,1)} %get-tuple-element.39.bd_hbm, f32[768,768]{1,0:T(8,128)} %get-tuple-element.36.gu.gbu_hbm, f32[768,768]{1,0:T(8,128)} %get-tuple-element.37.gd.gbd_hbm, ...), custom_call_target="tpu_custom_call" | custom-call | tf_op jit(solution)/shard_map/forward/pallas_call | solution.py:674
  281.2 1.2 collective-permute-start
  282.5 0.0 collective-permute-done.1.gd_early
  282.5 0.0 copy-start
  282.5 0.9 copy-done
  283.3 15.7 %update_other.1 = (f32[768,1536]{1,0:T(8,128)}, f32[1536,768]{1,0:T(8,128)}, f32[768,1536]{1,0:T(8,128)}, f32[1536,768]{1,0:T(8,128)}, f32[768,1536]{1,0:T(8,128...) custom-call(s32[1]{0:T(128)} %bitcast.d_ref, ...), custom_call_target="tpu_custom_call", output_to_operand_aliasing={{0}: (14, {}), {1}: (15, {}), {2}: (16, {}), {3}: (17, {}),... | custom-call | flops 10000000000 | bytes 40000000 | tf_op jit(solution)/shard_map/update_other/pallas_call | solution.py:704
  299.0 0.0 collective-permute-done.gu
  299.0 2.8 update_late.1
Async XLA Ops:
  129.1 153.3 %collective-permute-start.1 = (f32[256,768]{1,0:T(8,128)}, f32[256,768]{1,0:T(8,128)S(1)}, u32[]{:S(2)}, u32[]{:S(2)}) collective-permute-start(f32[256,768]{1,0:T(8,128)} %get-tuple-element.44), channel_id=1, source_target_pairs={{0,4},{4,0},{1,5},{5,1},{2,6},{6,2},{3,7},{7,3},{8,12},{12,8},{9,1... | collective-permute-start | bytes 2359304 | tf_op jit(solution)/shard_map/ppermute | solution.py:646
  281.2 17.8 %collective-permute-start = (f32[128,768]{1,0:T(8,128)}, f32[128,768]{1,0:T(8,128)}, u32[]{:S(2)}, u32[]{:S(2)}) collective-permute-start(f32[128,768]{1,0:T(8,128)} %get-tuple-element.42), channel_id=1, source_target_pairs={{0,4},{4,0},{1,5},{5,1},{2,6},{6,2},{3,7},{7,3},{8,12},{12,8},{9,1... | collective-permute-start | bytes 1179656 | tf_op jit(solution)/shard_map/ppermute | solution.py:692
  282.5 0.9 copy-start

commit v13 on v12

--- a/solution.py
+++ b/solution.py
@@ -117,9 +117,12 @@
     def _():
         dy_load.start()
     whole_barrier(n_model, n_data, n_stage)
-    send_acts = remote(acts_hbm, hid_o, ysend.at[0], rrecv.at[0], (z, d, hub))
-    relay_over = remote(hid_o, dz_o, rsend.at[0], rrecv.at[1], ypeer)
-    relay_back = remote(dz_o, aa.at[theirs], rsend.at[1], yrecv.at[0], (z, d, 0))
+    low, high = pl.ds(0, rows // 2), pl.ds(rows // 2, rows // 2)
+    late_rows = pl.ds(rows + rows // 2, rows // 2)
+    send_low = remote(acts_hbm.at[low], aa.at[pl.ds(rows, rows // 2)], ysend.at[0], yrecv.at[0], ypeer)
+    send_acts = remote(acts_hbm.at[high], hid_o.at[low], rsend.at[2], rrecv.at[0], (z, d, hub))
+    relay_over = remote(hid_o.at[low], dz_o.at[low], rsend.at[0], rrecv.at[1], ypeer)
+    relay_back = remote(dz_o.at[low], aa.at[late_rows], rsend.at[1], rrecv.at[2], (z, d, 0))
     raw_gu = remote(gu_hbm.at[:, oth_ff], gu_rcv, ysend.at[1], yrecv.at[1], ypeer)
     raw_gd = remote(gd_hbm.at[oth_ff, :], gd_rcv, ysend.at[2], yrecv.at[2], ypeer)
     sum_gu = remote(gu_oth, gu_rcv, ysend.at[1], yrecv.at[1], ypeer)
@@ -129,6 +132,7 @@
     @pl.when(by_rows)
     def _():
         send_acts.start()
+        send_low.start()
         raw_gd.start()
         raw_gu.start()
 
@@ -157,23 +161,6 @@
         copy.start()
     lax.fori_loop(0, nb, own_pre, 0)
 
-    def cast_down(i, carry):
-        at = pl.ds(pl.multiple_of(i * 128, 128), 128)
-        wd_bf[at, :] = wd32[at, :].astype(BF16)
-        return carry
-    lax.fori_loop(0, 2 * half // 128, cast_down, 0)
-
-    @pl.when(p == last)
-    def _():
-        dy_load.wait()
-
-    @pl.when(p == hub)
-    def _():
-        pltpu.make_async_copy(hid_o, hid_o, rrecv.at[0]).wait()
-        relay_over.start()
-        pltpu.make_async_copy(dz_o, dz_o, rrecv.at[1]).wait()
-        relay_back.start()
-
     def down_block(j, base):
         at = pl.ds(pl.multiple_of(base * half + j * 128, 128), 128)
         return mm(h_own[:, at], gg[mine, :], TN)
@@ -194,7 +181,22 @@
 
     @pl.when(p == last)
     def _():
+        dy_load.wait()
         send_down()
+
+
+    def cast_down(i, carry):
+        at = pl.ds(pl.multiple_of(i * 128, 128), 128)
+        wd_bf[at, :] = wd32[at, :].astype(BF16)
+        return carry
+    lax.fori_loop(0, 2 * half // 128, cast_down, 0)
+
+    @pl.when(p == hub)
+    def _():
+        pltpu.make_async_copy(hid_o.at[low], hid_o.at[low], rrecv.at[0]).wait()
+        relay_over.start()
+        pltpu.make_async_copy(dz_o.at[low], dz_o.at[low], rrecv.at[1]).wait()
+        relay_back.start()
 
     def g_at(c, zi):
         return gg.at[pl.ds(pl.multiple_of(c * rb + zi * hb, hb), hb)]
@@ -277,7 +279,8 @@
 
     @pl.when(by_rows)
     def _():
-        pltpu.make_async_copy(aa.at[theirs], aa.at[theirs], yrecv.at[0]).wait()
+        send_low.wait_recv()
+        pltpu.make_async_copy(aa.at[late_rows], aa.at[late_rows], rrecv.at[2]).wait()
 
         def oth_pre(i, carry):
             at = pl.ds(pl.multiple_of(i * rb, rb), rb)
@@ -354,7 +357,7 @@
 
     @pl.when(by_rows)
     def _():
-        for copy in (send_acts, raw_gu, raw_gd, send_g):
+        for copy in (send_acts, send_low, raw_gu, raw_gd, send_g):
             copy.wait_send()
 
     @pl.when(p == hub)
@@ -395,7 +398,8 @@
     clip = clip_of(norm_ref[...], mn_ref[0])
     rate = lr_ref[0]
     step = pl.program_id(0)
-    gd = jnp.where(step < EARLY_ROWS // UPD_ROWS, gd_early[...], gd_rest[...])
+    early_at = pl.ds(pl.multiple_of(jnp.minimum(step, EARLY_ROWS // UPD_ROWS - 1) * UPD_ROWS, UPD_ROWS), UPD_ROWS)
+    gd = jnp.where(step < EARLY_ROWS // UPD_ROWS, gd_early[early_at, :], gd_rest[...])
     owu[...], omu[...], ovu[...] = adamw_update(wu[...], mu[...], vu[...], clip * gu[...], rate)
     owd[...], omd[...], ovd[...] = adamw_update(wd[...], md[...], vd[...], clip * gd, rate)
     y_out[...] = y_in[...]
@@ -636,7 +640,7 @@
             ] + [pltpu.VMEM((width, half), F32), pltpu.VMEM((half, width), F32)] * 3 + [
                 pltpu.VMEM((nb, BACK_ROWS, width), F32), pltpu.VMEM((nb, hb, width), F32),
                 pltpu.VMEM((nb, hb, width), BF16), pltpu.VMEM((n_all, 8, 128), F32),
-                dma((8,)), dma((4,)), dma((4,)), dma((2,)), dma((2,)), dma((nb,)), dma((nb,)), dma((nb, 2)), dma((nb, 2)),
+                dma((8,)), dma((4,)), dma((4,)), dma((3,)), dma((3,)), dma((nb,)), dma((nb,)), dma((nb, 2)), dma((nb, 2)),
                 dma((n_all,)), dma((n_all,)), dma((4,)),
             ],
             compiler_params=pltpu.CompilerParams(collective_id=0, has_side_effects=True, vmem_limit_bytes=VMEM_LIMIT),
@@ -706,7 +710,7 @@
             out_shape=state_shapes + (sds(y_next.shape, BF16),),
             grid_spec=pltpu.PrefetchScalarGridSpec(
                 num_scalar_prefetch=1, grid=(steps,),
-                in_specs=small + [rows_spec(0, lastup + 1), rows_spec(0, nearly), rows_spec(nearly, blocks - nearly), y_spec] + other * 3 + [any_spec] * 6,
+                in_specs=small + [rows_spec(0, lastup + 1), vmem_spec, rows_spec(nearly, blocks - nearly), y_spec] + other * 3 + [any_spec] * 6,
                 out_specs=other * 3 + [y_spec]),
             input_output_aliases={14 + k: k for k in range(6)},
             compiler_params=pltpu.CompilerParams(dimension_semantics=('arbitrary',), vmem_limit_bytes=VMEM_LIMIT),

time: 302 us -> 299 us (0.990)
    pallas_call x1, Pallas kernels: 129 us -> 125 us  [device_step(): pl.pallas_call(functools.partial(bwd_kernel, dims), out_shape=(sds((width...]
  transfers between devices with their start and end apart: 2 -> 2, of which waited for: 0 -> 0; matrix products, arithmetic and copies ran while one was open for 0% -> 0% of each run, Pallas kernels for 55% -> 56%
where the time goes in v13:
time: 299 us
  Pallas kernels  296 us (99%)
    pallas_call x1, Pallas kernels, device_step(): pl.pallas_call(functools.partial(fwd_kernel, dims), out_shape=(sds((width...  137 us
    pallas_call x1, Pallas kernels, device_step(): pl.pallas_call(functools.partial(bwd_kernel, dims), out_shape=(sds((width...  125 us
    pallas_call x1, Pallas kernels, device_step(): pl.pallas_call(fill_kernel, out_shape=state_shapes + (sds(y_next.shape, B...  15.7 us
    pallas_call x1, Pallas kernels, device_step(): pl.pallas_call(update_kernel, out_shape=state_shapes + (sds((width, half)...  14.7 us
  transfers between devices with their start and end apart: 2, of which 0 were waited for; matrix products, arithmetic and copies ran while one was open for 0% of the time, Pallas kernels for 56%

profile of v13, /device:TPU:1, one launch (start us, length us, event | category | flops | bytes accessed | tf_op | source)
XLA Modules:
  0.0 298.8 jit_solution(13387031462653844230)
XLA Ops:
  0.6 125.4 %backward.1 = (f32[768,768]{1,0:T(8,128)}, f32[768,768]{1,0:T(8,128)}, f32[256,768]{1,0:T(8,128)}, f32[128,768]{1,0:T(8,128)}, f32[8,128]{1,0:T(8,128)}) custom-call(f32[768,1536]{1,0:T(8,128)} %bitcast.19, f32[1536,768]{1,0:T(8,128)} %bitcast.23, bf16[512,768]{1,0:T(8,128)(2,1)} %bitcast.46, bf16[512,768]{1,0:T(8,128)(2,1)} %dy_hbm.1, ...), custom_call_target="tpu_custom_call" | custom-call | tf_op jit(solution)/shard_map/backward/pallas_call | solution.py:628
  126.0 0.0 collective-permute-start.1
  127.4 14.7 %update_own.1 = (f32[768,1536]{1,0:T(8,128)}, f32[1536,768]{1,0:T(8,128)}, f32[768,1536]{1,0:T(8,128)}, f32[1536,768]{1,0:T(8,128)}, f32[768,1536]{1,0:T(8,128)}...) custom-call(s32[1]{0:T(128)} %bitcast.d_ref, f32[1]{0:T(128)S(6)} %copy.38.lr_ref, ...), custom_call_target="tpu_custom_call" | custom-call | tf_op jit(solution)/shard_map/update_own/pallas_call | solution.py:664
  142.1 137.2 %forward.1 = (f32[640,768]{1,0:T(8,128)}, f32[512,768]{1,0:T(8,128)}, bf16[16,96,768]{2,1,0:T(8,128)(2,1)}) custom-call(bf16[768,768]{1,0:T(8,128)(2,1)} %get-tuple-element.38.bu_hbm, bf16[768,768]{1,0:T(8,128)(2,1)} %get-tuple-element.39.bd_hbm, f32[768,768]{1,0:T(8,128)} %get-tuple-element.36.gu.gbu_hbm, f32[768,768]{1,0:T(8,128)} %get-tuple-element.37.gd.gbd_hbm, ...), custom_call_target="tpu_custom_call" | custom-call | tf_op jit(solution)/shard_map/forward/pallas_call | solution.py:678
  279.3 0.0 collective-permute-start
  279.3 0.0 collective-permute-done.1.gd_early
  279.4 0.0 copy-start
  279.4 0.9 copy-done
  280.2 15.7 %update_other.1 = (f32[768,1536]{1,0:T(8,128)}, f32[1536,768]{1,0:T(8,128)}, f32[768,1536]{1,0:T(8,128)}, f32[1536,768]{1,0:T(8,128)}, f32[768,1536]{1,0:T(8,128...) custom-call(s32[1]{0:T(128)} %bitcast.d_ref, ...), custom_call_target="tpu_custom_call", output_to_operand_aliasing={{0}: (14, {}), {1}: (15, {}), {2}: (16, {}), {3}: (17, {}),... | custom-call | flops 10000000000 | bytes 40000000 | tf_op jit(solution)/shard_map/update_other/pallas_call | solution.py:708
  296.0 0.0 collective-permute-done.gu
  296.0 2.8 update_late.1
Async XLA Ops:
  126.0 153.3 %collective-permute-start.1 = (f32[256,768]{1,0:T(8,128)}, f32[256,768]{1,0:T(8,128)S(1)}, u32[]{:S(2)}, u32[]{:S(2)}) collective-permute-start(f32[256,768]{1,0:T(8,128)} %get-tuple-element.44), channel_id=1, source_target_pairs={{0,4},{4,0},{1,5},{5,1},{2,6},{6,2},{3,7},{7,3},{8,12},{12,8},{9,1... | collective-permute-start | bytes 2359304 | tf_op jit(solution)/shard_map/ppermute | solution.py:650
  279.3 16.7 %collective-permute-start = (f32[128,768]{1,0:T(8,128)}, f32[128,768]{1,0:T(8,128)}, u32[]{:S(2)}, u32[]{:S(2)}) collective-permute-start(f32[128,768]{1,0:T(8,128)} %get-tuple-element.42), channel_id=1, source_target_pairs={{0,4},{4,0},{1,5},{5,1},{2,6},{6,2},{3,7},{7,3},{8,12},{12,8},{9,1... | collective-permute-start | bytes 1179656 | tf_op jit(solution)/shard_map/ppermute | solution.py:696
  279.4 0.9 copy-start

commit v14 on v13

--- a/solution.py
+++ b/solution.py
@@ -28,7 +28,7 @@
 UPD_ROWS = 128
 EARLY_ROWS = 256
 LATE_ROWS = 128
-TURN_STEP = 5
+TURN_STEP = 8
 VMEM_LIMIT = 66_000_000
 
 
@@ -490,6 +490,9 @@
     @pl.when(p == last)
     def _():
         shard[3].start()
+        pl.semaphore_wait(turn, 1)
+        send_gu.start()
+        send_gd.start()
         for copy in shard:
             copy.wait_recv()
 
@@ -568,7 +571,7 @@
         def _():
             publish(i - 1)
 
-        @pl.when((i == TURN_STEP) & first)
+        @pl.when((i == TURN_STEP) & (p == 0))
         def _():
             pl.semaphore_wait(turn, 1)
             send_gu.start()

time: 299 us -> 300 us (level)
  no operation moved by 1% of the time
where the time goes in v14:
time: 300 us
  Pallas kernels  296 us (99%)
    pallas_call x1, Pallas kernels, device_step(): pl.pallas_call(functools.partial(fwd_kernel, dims), out_shape=(sds((width...  137 us
    pallas_call x1, Pallas kernels, device_step(): pl.pallas_call(functools.partial(bwd_kernel, dims), out_shape=(sds((width...  125 us
    pallas_call x1, Pallas kernels, device_step(): pl.pallas_call(fill_kernel, out_shape=state_shapes + (sds(y_next.shape, B...  15.7 us
    pallas_call x1, Pallas kernels, device_step(): pl.pallas_call(update_kernel, out_shape=state_shapes + (sds((width, half)...  14.7 us
  transfers between devices with their start and end apart: 2, of which 0 were waited for; matrix products, arithmetic and copies ran while one was open for 0% of the time, Pallas kernels for 56%

profile of v14, /device:TPU:1, one launch (start us, length us, event | category | flops | bytes accessed | tf_op | source)
XLA Modules:
  0.0 300.1 jit_solution(6546062039856849698)
XLA Ops:
  0.6 125.4 %backward.1 = (f32[768,768]{1,0:T(8,128)}, f32[768,768]{1,0:T(8,128)}, f32[256,768]{1,0:T(8,128)}, f32[128,768]{1,0:T(8,128)}, f32[8,128]{1,0:T(8,128)}) custom-call(f32[768,1536]{1,0:T(8,128)} %bitcast.19, f32[1536,768]{1,0:T(8,128)} %bitcast.23, bf16[512,768]{1,0:T(8,128)(2,1)} %bitcast.46, bf16[512,768]{1,0:T(8,128)(2,1)} %dy_hbm.1, ...), custom_call_target="tpu_custom_call" | custom-call | tf_op jit(solution)/shard_map/backward/pallas_call | solution.py:631
  126.0 0.0 collective-permute-start.1
  127.4 14.7 %update_own.1 = (f32[768,1536]{1,0:T(8,128)}, f32[1536,768]{1,0:T(8,128)}, f32[768,1536]{1,0:T(8,128)}, f32[1536,768]{1,0:T(8,128)}, f32[768,1536]{1,0:T(8,128)}...) custom-call(s32[1]{0:T(128)} %bitcast.d_ref, f32[1]{0:T(128)S(6)} %copy.38.lr_ref, ...), custom_call_target="tpu_custom_call" | custom-call | tf_op jit(solution)/shard_map/update_own/pallas_call | solution.py:667
  142.1 137.2 %forward.1 = (f32[640,768]{1,0:T(8,128)}, f32[512,768]{1,0:T(8,128)}, bf16[16,96,768]{2,1,0:T(8,128)(2,1)}) custom-call(bf16[768,768]{1,0:T(8,128)(2,1)} %get-tuple-element.38.bu_hbm, bf16[768,768]{1,0:T(8,128)(2,1)} %get-tuple-element.39.bd_hbm, f32[768,768]{1,0:T(8,128)} %get-tuple-element.36.gu.gbu_hbm, f32[768,768]{1,0:T(8,128)} %get-tuple-element.37.gd.gbd_hbm, ...), custom_call_target="tpu_custom_call" | custom-call | tf_op jit(solution)/shard_map/forward/pallas_call | solution.py:681
  279.2 1.4 collective-permute-start
  280.7 0.0 collective-permute-done.1.gd_early
  280.7 0.0 copy-start
  280.7 0.9 copy-done
  281.5 15.7 %update_other.1 = (f32[768,1536]{1,0:T(8,128)}, f32[1536,768]{1,0:T(8,128)}, f32[768,1536]{1,0:T(8,128)}, f32[1536,768]{1,0:T(8,128)}, f32[768,1536]{1,0:T(8,128...) custom-call(s32[1]{0:T(128)} %bitcast.d_ref, ...), custom_call_target="tpu_custom_call", output_to_operand_aliasing={{0}: (14, {}), {1}: (15, {}), {2}: (16, {}), {3}: (17, {}),... | custom-call | flops 10000000000 | bytes 40000000 | tf_op jit(solution)/shard_map/update_other/pallas_call | solution.py:711
  297.3 0.0 collective-permute-done.gu
  297.3 2.8 update_late.1
Async XLA Ops:
  126.0 154.6 %collective-permute-start.1 = (f32[256,768]{1,0:T(8,128)}, f32[256,768]{1,0:T(8,128)S(1)}, u32[]{:S(2)}, u32[]{:S(2)}) collective-permute-start(f32[256,768]{1,0:T(8,128)} %get-tuple-element.44), channel_id=1, source_target_pairs={{0,4},{4,0},{1,5},{5,1},{2,6},{6,2},{3,7},{7,3},{8,12},{12,8},{9,1... | collective-permute-start | bytes 2359304 | tf_op jit(solution)/shard_map/ppermute | solution.py:653
  279.2 18.0 %collective-permute-start = (f32[128,768]{1,0:T(8,128)}, f32[128,768]{1,0:T(8,128)}, u32[]{:S(2)}, u32[]{:S(2)}) collective-permute-start(f32[128,768]{1,0:T(8,128)} %get-tuple-element.42), channel_id=1, source_target_pairs={{0,4},{4,0},{1,5},{5,1},{2,6},{6,2},{3,7},{7,3},{8,12},{12,8},{9,1... | collective-permute-start | bytes 1179656 | tf_op jit(solution)/shard_map/ppermute | solution.py:699
  280.7 0.9 copy-start

commit v15 on v13

--- a/solution.py
+++ b/solution.py
@@ -73,6 +73,18 @@
     pl.semaphore_wait(barrier, n_model * n_data * n_stage - 1)
 
 
+def replica_barrier(n_model, n_data, n_stage):
+    barrier = pltpu.get_barrier_semaphore()
+    z, d, p = lax.axis_index('model'), lax.axis_index('data'), lax.axis_index('stage')
+    pl.semaphore_signal(barrier, inc=1, device_id=(z, lax.rem(d + 1, n_data), p), device_id_type=MESH)
+    for dm in range(n_model):
+        for ds in range(n_stage):
+            if dm or ds:
+                peer = (lax.rem(z + dm, n_model), d, lax.rem(p + ds, n_stage))
+                pl.semaphore_signal(barrier, inc=1, device_id=peer, device_id_type=MESH)
+    pl.semaphore_wait(barrier, n_model * n_stage)
+
+
 def remote(src, dst, send_sem, recv_sem, device):
     return pltpu.make_async_remote_copy(src_ref=src, dst_ref=dst, send_sem=send_sem, recv_sem=recv_sem, device_id=device, device_id_type=MESH)
 
@@ -437,7 +449,7 @@
     @pl.when(p == 0)
     def _():
         x_load.start()
-    whole_barrier(n_model, n_data, n_stage)
+    replica_barrier(n_model, n_data, n_stage)
 
     send_wu = remote(bu_hbm, wu_bf.at[:, own_ff], ysend.at[0], yrecv.at[0], ypeer)
     send_wd = remote(bd_hbm, wd_bf.at[own_ff, :], ysend.at[1], yrecv.at[1], ypeer)

time: 299 us -> 299 us (level)
  no operation moved by 1% of the time
where the time goes in v15:
time: 299 us
  Pallas kernels  294 us (98%)
    pallas_call x1, Pallas kernels, device_step(): pl.pallas_call(functools.partial(fwd_kernel, dims), out_shape=(sds((width...  136 us
    pallas_call x1, Pallas kernels, device_step(): pl.pallas_call(functools.partial(bwd_kernel, dims), out_shape=(sds((width...  125 us
    pallas_call x1, Pallas kernels, device_step(): pl.pallas_call(fill_kernel, out_shape=state_shapes + (sds(y_next.shape, B...  15.7 us
    pallas_call x1, Pallas kernels, device_step(): pl.pallas_call(update_kernel, out_shape=state_shapes + (sds((width, half)...  14.7 us
  transfers between devices with their start and end apart: 2, of which 0 were waited for; matrix products, arithmetic and copies ran while one was open for 0% of the time, Pallas kernels for 56%

profile of v15, /device:TPU:1, one launch (start us, length us, event | category | flops | bytes accessed | tf_op | source)
XLA Modules:
  0.0 298.5 jit_solution(12530121902405900075)
XLA Ops:
  0.6 125.4 %backward.1 = (f32[768,768]{1,0:T(8,128)}, f32[768,768]{1,0:T(8,128)}, f32[256,768]{1,0:T(8,128)}, f32[128,768]{1,0:T(8,128)}, f32[8,128]{1,0:T(8,128)}) custom-call(f32[768,1536]{1,0:T(8,128)} %bitcast.19, f32[1536,768]{1,0:T(8,128)} %bitcast.23, bf16[512,768]{1,0:T(8,128)(2,1)} %bitcast.46, bf16[512,768]{1,0:T(8,128)(2,1)} %dy_hbm.1, ...), custom_call_target="tpu_custom_call" | custom-call | tf_op jit(solution)/shard_map/backward/pallas_call | solution.py:640
  126.0 0.0 collective-permute-start.1
  127.4 14.7 %update_own.1 = (f32[768,1536]{1,0:T(8,128)}, f32[1536,768]{1,0:T(8,128)}, f32[768,1536]{1,0:T(8,128)}, f32[1536,768]{1,0:T(8,128)}, f32[768,1536]{1,0:T(8,128)}...) custom-call(s32[1]{0:T(128)} %bitcast.d_ref, f32[1]{0:T(128)S(6)} %copy.38.lr_ref, ...), custom_call_target="tpu_custom_call" | custom-call | tf_op jit(solution)/shard_map/update_own/pallas_call | solution.py:676
  142.1 135.7 %forward.1 = (f32[640,768]{1,0:T(8,128)}, f32[512,768]{1,0:T(8,128)}, bf16[16,96,768]{2,1,0:T(8,128)(2,1)}) custom-call(bf16[768,768]{1,0:T(8,128)(2,1)} %get-tuple-element.38.bu_hbm, bf16[768,768]{1,0:T(8,128)(2,1)} %get-tuple-element.39.bd_hbm, f32[768,768]{1,0:T(8,128)} %get-tuple-element.36.gu.gbu_hbm, f32[768,768]{1,0:T(8,128)} %get-tuple-element.37.gd.gbd_hbm, ...), custom_call_target="tpu_custom_call" | custom-call | tf_op jit(solution)/shard_map/forward/pallas_call | solution.py:690
  277.8 1.3 collective-permute-start
  279.1 0.0 collective-permute-done.1.gd_early
  279.1 0.0 copy-start
  279.1 0.9 copy-done
  280.0 15.7 %update_other.1 = (f32[768,1536]{1,0:T(8,128)}, f32[1536,768]{1,0:T(8,128)}, f32[768,1536]{1,0:T(8,128)}, f32[1536,768]{1,0:T(8,128)}, f32[768,1536]{1,0:T(8,128...) custom-call(s32[1]{0:T(128)} %bitcast.d_ref, ...), custom_call_target="tpu_custom_call", output_to_operand_aliasing={{0}: (14, {}), {1}: (15, {}), {2}: (16, {}), {3}: (17, {}),... | custom-call | flops 10000000000 | bytes 40000000 | tf_op jit(solution)/shard_map/update_other/pallas_call | solution.py:720
  295.7 0.0 collective-permute-done.gu
  295.7 2.8 update_late.1
Async XLA Ops:
  126.0 153.1 %collective-permute-start.1 = (f32[256,768]{1,0:T(8,128)}, f32[256,768]{1,0:T(8,128)S(1)}, u32[]{:S(2)}, u32[]{:S(2)}) collective-permute-start(f32[256,768]{1,0:T(8,128)} %get-tuple-element.44), channel_id=1, source_target_pairs={{0,4},{4,0},{1,5},{5,1},{2,6},{6,2},{3,7},{7,3},{8,12},{12,8},{9,1... | collective-permute-start | bytes 2359304 | tf_op jit(solution)/shard_map/ppermute | solution.py:662
  277.8 17.9 %collective-permute-start = (f32[128,768]{1,0:T(8,128)}, f32[128,768]{1,0:T(8,128)}, u32[]{:S(2)}, u32[]{:S(2)}) collective-permute-start(f32[128,768]{1,0:T(8,128)} %get-tuple-element.42), channel_id=1, source_target_pairs={{0,4},{4,0},{1,5},{5,1},{2,6},{6,2},{3,7},{7,3},{8,12},{12,8},{9,1... | collective-permute-start | bytes 1179656 | tf_op jit(solution)/shard_map/ppermute | solution.py:708
  279.1 0.9 copy-start
